TPU v7x, 32 devices: a whole 2x2x4 slice. The times are simulated.
32 devices in a mesh: sec: 4 (over z), fsdp: 8 (over y, x, core).
Axes of the slice: x: 2, y: 2, z: 4, core: 2. Of those that a mesh axis runs over, the one named last changes fastest.
Arguments:
- hidden: bfloat16 [4096, 4096], P('fsdp', 'sec'), may hold values from -6 to 6
- window_proj: bfloat16 [4, 4096, 512], P('sec', 'fsdp'), may hold values from -0.09375 to 0.09375
- head_weights: bfloat16 [4, 512], P('sec'), may hold values from -0.25 to 0.25
- ref_logprob: float32 [8, 512], P('fsdp'), may hold values from -4 to 0
- resp_spans: int32 [8, 2], P('fsdp'), may hold values from 64 to 512, as said below
Outputs:
- actor_grad: float32 [4, 4096, 256], P('sec', 'fsdp')
- advantage: float32 [8, 512], P('fsdp')
Inputs may be any that keep to these rules, and one draw needn't show every extreme that they name: `resp_spans`: column 0 is a sequence's first response position, between 64 and 255; column 1 is one past its last response position, larger than column 0.
All inputs are finite; a program needn't handle non-finite values.
Results may differ from a plain program's by a relative error of at most 0.0085.
Values may be sent and summed in bfloat16 or wider, within the bound.
No kernel may reach another device: no remote copies, remote signals or barrier semaphores. Data moves between devices by JAX's collectives and lax.ppermute only.
A program may use at most 64 MiB of HBM per device.

v0:
```python
import jax
import jax.numpy as jnp
from jax import lax
from jax.sharding import PartitionSpec as P

KL_COEF = 0.1
DISCOUNT = 1.0
TRACE_DECAY = 0.95
NORM_EPS = 1e-05


def from_behind(array, axis, by):
    length = lax.axis_size(axis)
    pairs = [(i, i + by) for i in range(length) if 0 <= i + by < length]
    return lax.ppermute(array, axis, pairs)


def silu_slope(values):
    sigmoid = jax.nn.sigmoid(values)
    return sigmoid * (1.0 + values * (1.0 - sigmoid))


def normalize(hidden):
    widened = hidden.astype(jnp.float32)
    meansq = jnp.mean(widened * widened, axis=1, keepdims=True)
    return (widened * lax.rsqrt(meansq + NORM_EPS)).astype(jnp.bfloat16)


def advantage_of(log_prob, value_est, scores, ref_logprob, resp_spans, length):
    position = lax.broadcasted_iota(jnp.int32, (1, length), 1)
    starts = resp_spans[:, 0:1]
    ending = resp_spans[:, 1:2]
    inside = ((position >= starts) & (position < ending)).astype(jnp.float32)
    last_tok = (position == ending - 1).astype(jnp.float32)
    follow = (position + 1 < ending).astype(jnp.float32)
    reward = -KL_COEF * (log_prob - ref_logprob) * inside + scores * last_tok
    next_value = jnp.concatenate(
        [value_est[:, 1:], jnp.zeros((value_est.shape[0], 1), jnp.float32)], axis=1
    )
    deltas = (reward + DISCOUNT * next_value * follow - value_est) * inside
    source_pos = lax.broadcasted_iota(jnp.int32, (length, length), 0)
    target_pos = lax.broadcasted_iota(jnp.int32, (length, length), 1)
    spacing = source_pos - target_pos
    decays = jnp.where(
        spacing >= 0,
        jnp.power(jnp.float32(DISCOUNT * TRACE_DECAY), jnp.maximum(spacing, 0).astype(jnp.float32)),
        jnp.float32(0.0),
    )
    advantage = jnp.dot(deltas, decays, precision=lax.Precision.HIGHEST) * inside
    counts = (ending - starts).astype(jnp.float32)
    signal = -advantage / counts
    return (advantage, signal)


def shards(hidden, window_proj, head_weights, ref_logprob, resp_spans):
    features = lax.all_gather(hidden, "sec", axis=1, tiled=True)
    normed = normalize(features)
    weights = window_proj[0]
    own_head = head_weights[0]
    tok_rows = normed.shape[0]
    half_cols = own_head.shape[0] // 2
    whole_slab = lax.all_gather(weights, "fsdp", axis=0, tiled=True)
    pre_act = jnp.dot(normed, whole_slab, preferred_element_type=jnp.float32).astype(jnp.bfloat16)
    own_sum = jnp.sum(
        own_head.astype(jnp.float32) * jax.nn.silu(pre_act.astype(jnp.float32)),
        axis=1,
        keepdims=True,
    )
    totals = lax.all_gather(own_sum, "sec", axis=1, tiled=True)
    shaped = ref_logprob.shape
    log_prob = (totals[:, 0] + totals[:, 1]).reshape(shaped)
    value_est = totals[:, 2].reshape(shaped)
    scores = totals[:, 3].reshape(shaped)
    advantage, signal = advantage_of(
        log_prob, value_est, scores, ref_logprob, resp_spans, shaped[1]
    )
    far_side = lax.axis_index("sec") >= 2
    moved_pre, moved_head = from_behind((pre_act[:, half_cols:], own_head[half_cols:]), "sec", 2)
    chosen_pre = jnp.where(far_side, moved_pre, pre_act[:, :half_cols])
    chosen_head = jnp.where(far_side, moved_head, own_head[:half_cols])
    flat_signal = signal.reshape(tok_rows)
    slopes = (
        flat_signal[:, None]
        * chosen_head.astype(jnp.float32)[None, :]
        * silu_slope(chosen_pre.astype(jnp.float32))
    ).astype(jnp.bfloat16)
    grad_part = lax.psum_scatter(
        lax.dot_general(
            normed, slopes, (((0,), (0,)), ((), ())), preferred_element_type=jnp.float32
        ),
        "fsdp",
        scatter_dimension=0,
        tiled=True,
    )
    return (grad_part[None], advantage)


def solution(mesh):
    return jax.shard_map(
        shards,
        mesh=mesh,
        in_specs=(
            P("fsdp", "sec"),
            P("sec", "fsdp", None),
            P("sec", None),
            P("fsdp", None),
            P("fsdp", None),
        ),
        out_specs=(P("sec", "fsdp", None), P("fsdp", None)),
        check_vma=False,
    )
```

profile of v0, /device:TPU:4, one launch (start us, length us, event | category | flops | bytes accessed | tf_op | source)
XLA Modules:
  0.0 221.3 jit_solution(7474681093379864792)
XLA Ops:
  7.2 0.0 all-gather.5.cloned.1.call-start
  7.2 0.7 all-gather.5.cloned.1.call-update
  7.9 0.0 all-gather.7.cloned.1.call-start
  7.9 0.7 all-gather.7.cloned.1.call-update
  8.6 0.0 reduce-scatter.2.cloned.1.call-start
  8.7 0.7 slice_reduce_fusion
  9.4 4.5 %collective-permute-start = (bf16[256]{0:T(256)(128)(2,1)S(1)}, bf16[256]{0:T(256)(128)(2,1)S(1)}, u32[]{:S(2)}, u32[]{:S(2)}) collective-permute-start(bf16[256]{0:T(256)(128)(2,1)S(1)} %get-tuple-element.3), channel_id=1, source_target_pairs={{0,16},{8,24},{1,17},{9,25},{2,18},{10,26},{3,19},{11,27},{4,20},{... | collective-permute-start | bytes 1544 | tf_op jit(solution)/shard_map/ppermute | solution.py:15
  13.9 0.7 mul.95
  14.6 1.3 fusion.69
  17.8 0.0 collective-permute-done
  17.8 73.7 %all-gather.5.cloned.1.call-done = bf16[512,4096]{1,0:T(8,128)(2,1)} async-done(((bf16[512,1024]{1,0:T(8,128)(2,1)}), bf16[512,4096]{1,0:T(8,128)(2,1)}) %all-gather.5.cloned.1.call-update) | async-done | bytes 4194320 | tf_op jit(solution)/shard_map/all_gather | solution.py:56
  91.5 3.1 %fusion = f32[512]{0:T(512)S(1)} fusion(bf16[512,4096]{1,0:T(8,128)(2,1)} %all-gather.5.cloned.1.call-done), kind=kLoop, calls=%fused_computation.2 | loop fusion | flops 6290944 | bytes 4196352 | tf_op jit(solution)/shard_map/reduce_sum | solution.py:25
  94.6 33.7 %all-gather.7.cloned.1.call-done = bf16[1,4096,512]{2,1,0:T(8,128)(2,1)} async-done(((bf16[1,512,512]{2,1,0:T(8,128)(2,1)}), bf16[1,4096,512]{2,1,0:T(8,128)(2,1)}) %all-gather.7.cloned.1.call-update) | async-done | bytes 4194320 | tf_op jit(solution)/shard_map/all_gather | solution.py:62
  128.4 6.2 %fusion.22 = (f32[512]{0:T(512)S(1)}, bf16[512,512]{0,1:T(8,128)(2,1)S(1)}) fusion(f32[512]{0:T(512)S(1)} %bitcast.47, bf16[1,4096,512]{2,1,0:T(8,128)(2,1)} %all-gather.7.cloned.1.call-done, bf16[512,4096]{1,0:T(8,128)(2,1)} %all-gather.5.cloned.1.call-done, f32[512]{0:T(512)S(1)} %add_rsqrt_fusion), kind=kOutput, calls=%fused_computation.21 | convolution fusion | flops 2155871744 | bytes 8919040 | tf_op jit(solution)/shard_map/dot_general | solution.py:63
  134.6 12.0 %all-gather.1 = f32[4,1,512]{2,1,0:T(1,128)S(1)} all-gather(f32[1,1,512]{2,1,0:T(1,128)S(1)} %bitcast.46), channel_id=1, replica_groups=mesh['sec'=4,'fsdp'=8] {'sec'}, dimensions={0}, use_global_device_ids=true | all-gather | bytes 10240 | tf_op jit(solution)/shard_map/all_gather | solution.py:69
  146.6 0.1 slice.56
  146.7 2.9 %collective-permute-start.1 = (bf16[512,256]{0,1:T(8,128)(2,1)S(1)}, bf16[512,256]{0,1:T(8,128)(2,1)S(1)}, u32[]{:S(2)}, u32[]{:S(2)}) collective-permute-start(bf16[512,256]{0,1:T(8,128)(2,1)S(1)} %slice.57), channel_id=1, source_target_pairs={{0,16},{8,24},{1,17},{9,25},{2,18},{10,26},{3,19},{11,27},{4,20},{... | collective-permute-start | bytes 786440 | tf_op jit(solution)/shard_map/ppermute | solution.py:15
  149.6 0.0 copy-done.1
  149.6 1.9 fusion.16
  151.5 1.9 negate_divide_fusion
  153.4 0.1 collective-permute-done.1
  153.5 4.1 %fusion.4 = f32[4096,256]{1,0:T(8,128)} fusion(bf16[512,4096]{1,0:T(8,128)(2,1)S(1)} %copy-done, f32[512]{0:T(512)S(1)} %add_rsqrt_fusion, bf16[512,256]{0,1:T(8,128)(2,1)S(1)} %collective-permute-done.1, bf16[512,512]{0,1:T(8,128)(2,1)S(1)} %get-tuple-element.9, f32[256]{0:T(256)S(1)} %fusion.60, f32[512]{0:T(512)S(1)} %get-tuple-element.4, pred[]{:T(512)S(6)} %ge.34), kind=kOutput, calls=%fused_computation.6 | convolution fusion | flops 1081606144 | bytes 8918017 | tf_op jit(solution)/shard_map/dot_general | solution.py:88
  157.6 0.0 reduce-scatter.2.cloned.1.call-update
  157.6 57.2 %reduce-scatter.2.cloned.1.call-done = f32[512,256]{1,0:T(8,128)} async-done(((f32[4096,256]{1,0:T(8,128)}), f32[512,256]{1,0:T(8,128)}) %reduce-scatter.2.cloned.1.call-update) | async-done | bytes 524304 | tf_op jit(solution)/shard_map/reduce_scatter | solution.py:87
  (8 shorter events, 0.0 us)
Async XLA Ops:
  7.2 84.4 %all-gather.5.cloned.1.call-start = ((), (), s32[]{:S(2)}) async-start(), calls=%async_computation.1 | async-start | bytes 5242880 | tf_op jit(solution)/shard_map/all_gather | solution.py:56
  7.9 120.5 %all-gather.7.cloned.1.call-start = ((), (), s32[]{:S(2)}) async-start(), calls=%async_computation.3 | async-start | bytes 4718592 | tf_op jit(solution)/shard_map/all_gather | solution.py:62
  8.6 206.1 %reduce-scatter.2.cloned.1.call-start = ((), (), s32[]{:S(2)}) async-start(), calls=%async_computation.2 | async-start | bytes 4718592 | tf_op jit(solution)/shard_map/reduce_scatter | solution.py:87
  9.4 8.4 %collective-permute-start = (bf16[256]{0:T(256)(128)(2,1)S(1)}, bf16[256]{0:T(256)(128)(2,1)S(1)}, u32[]{:S(2)}, u32[]{:S(2)}) collective-permute-start(bf16[256]{0:T(256)(128)(2,1)S(1)} %get-tuple-element.3), channel_id=1, source_target_pairs={{0,16},{8,24},{1,17},{9,25},{2,18},{10,26},{3,19},{11,27},{4,20},{... | collective-permute-start | bytes 1544 | tf_op jit(solution)/shard_map/ppermute | solution.py:15
  128.4 21.2 %copy-start.1 = (f32[1,512]{1,0:T(1,128)S(1)}, f32[1,512]{1,0:T(1,128)}, u32[]{:S(2)}) copy-start(f32[1,512]{1,0:T(1,128)} %param.8) | copy-start | bytes 6148
  128.4 25.1 %copy-start = (bf16[512,4096]{1,0:T(8,128)(2,1)S(1)}, bf16[512,4096]{1,0:T(8,128)(2,1)}, u32[]{:S(2)}) copy-start(bf16[512,4096]{1,0:T(8,128)(2,1)} %all-gather.5.cloned.1.call-done) | copy-start | bytes 12582916
  146.7 6.8 %collective-permute-start.1 = (bf16[512,256]{0,1:T(8,128)(2,1)S(1)}, bf16[512,256]{0,1:T(8,128)(2,1)S(1)}, u32[]{:S(2)}, u32[]{:S(2)}) collective-permute-start(bf16[512,256]{0,1:T(8,128)(2,1)S(1)} %slice.57), channel_id=1, source_target_pairs={{0,16},{8,24},{1,17},{9,25},{2,18},{10,26},{3,19},{11,27},{4,20},{... | collective-permute-start | bytes 786440 | tf_op jit(solution)/shard_map/ppermute | solution.py:15
Sparse Core Ops, SparseCore 0:
  9.5 81.9 all-gather.4
  93.4 34.9 all-gather.6
  157.7 57.0 reduce-scatter.1
where the time goes:
time: 223 us; the launch traced here: 221 us
  waiting for transfers between devices  166 us (74%)
  between operations  15.7 us (7%)
  matrix products  12.3 us (6%)
  blocking collectives  12 us (5%)
  starting transfers between devices  7.47 us (3%)
  other arithmetic  5.64 us (3%)
    all_gather x1, waiting for transfers between devices, shards(): features = lax.all_gather(hidden, 'sec', axis=1, tiled=True)  73.7 us
    reduce_scatter x1, waiting for transfers between devices, shards(): lax.psum_scatter(lax.dot_general(normed, slopes, (((0,), (0,)), ((), ()))...  57.2 us
    all_gather x1, waiting for transfers between devices, shards(): whole_slab = lax.all_gather(weights, 'fsdp', axis=0, tiled=True)  33.7 us
    all_gather x1, blocking collectives, shards(): totals = lax.all_gather(own_sum, 'sec', axis=1, tiled=True)  12 us
    ppermute x2, starting transfers between devices, from_behind(): return lax.ppermute(array, axis, pairs)  7.36 us
    dot_general x1, matrix products, shards(): jnp.dot(normed, whole_slab, preferred_element_type=jnp.float32)  6.23 us
  transfers between devices with their start and end apart: 5, of which 4 were waited for; matrix products, arithmetic and copies ran while one was open for 4% of the time, Pallas kernels for 0%

commit v1 on v0

v1 whole, which is shorter than its diff:
```python
import jax
import jax.numpy as jnp
from jax import lax
from jax.sharding import PartitionSpec as P

KL_COEF = 0.1
DISCOUNT = 1.0
TRACE_DECAY = 0.95
NORM_EPS = 1e-05
FIRST_START = 64


def silu_slope(values):
    sigmoid = jax.nn.sigmoid(values)
    return sigmoid * (1.0 + values * (1.0 - sigmoid))


def advantage_of(log_prob, value_est, scores, ref_logprob, starts, ending, first):
    length = log_prob.shape[1]
    position = lax.broadcasted_iota(jnp.int32, (1, length), 1) + first
    inside = ((position >= starts) & (position < ending)).astype(jnp.float32)
    last_tok = (position == ending - 1).astype(jnp.float32)
    follow = (position + 1 < ending).astype(jnp.float32)
    reward = -KL_COEF * (log_prob - ref_logprob) * inside + scores * last_tok
    next_value = jnp.concatenate(
        [value_est[:, 1:], jnp.zeros((value_est.shape[0], 1), jnp.float32)], axis=1
    )
    deltas = (reward + DISCOUNT * next_value * follow - value_est) * inside
    source_pos = lax.broadcasted_iota(jnp.int32, (length, length), 0)
    target_pos = lax.broadcasted_iota(jnp.int32, (length, length), 1)
    spacing = source_pos - target_pos
    decays = jnp.where(
        spacing >= 0,
        jnp.power(jnp.float32(DISCOUNT * TRACE_DECAY), jnp.maximum(spacing, 0).astype(jnp.float32)),
        jnp.float32(0.0),
    )
    advantage = jnp.dot(deltas, decays, precision=lax.Precision.HIGHEST) * inside
    counts = (ending - starts).astype(jnp.float32)
    return advantage, -advantage / counts


def solution(mesh):
    n_dev = mesh.shape["fsdp"]
    chips = n_dev // 2
    top = chips.bit_length() - 1

    def swap_fsdp(array, flip):
        return lax.ppermute(array, "fsdp", [(i, i ^ flip) for i in range(n_dev)])

    def swap_sec(array, flip):
        return lax.ppermute(array, "sec", [(i, i ^ flip) for i in range(4)])

    def split(f):
        return f >> top, (f & (chips - 1)) >> 1, f & 1

    def join(t, m, c):
        return (t << top) | (m << 1) | c

    def slab_route(slot):
        pairs = []
        for z in range(4):
            for f in range(n_dev):
                d, k = z >> 1, z & 1
                t, m, r = split(f)
                pairs.append((z * n_dev + f, (2 * t + k) * n_dev + join(r, m, d ^ slot)))
        return pairs

    def final_route():
        pairs = []
        for z in range(4):
            for f in range(n_dev):
                d, k = z >> 1, z & 1
                t, m, c = split(f)
                pairs.append((z * n_dev + f, (2 * c + k) * n_dev + d * chips + 2 * m + t))
        return pairs

    m_bits = top - 1
    flips = [(1, n_dev // 2)] + [(2 << j, 2 << j) for j in range(m_bits)]

    def gather_pieces(own, order):
        pieces = {0: own}
        for rel, flip in order:
            for j in sorted(pieces):
                pieces[j | rel] = swap_fsdp(pieces[j], flip)
        return [pieces[j] for j in range(chips)]

    def scatter_sum(blocks, order):
        blocks = dict(enumerate(blocks))
        for rel, flip in order:
            keep = sorted(j for j in blocks if not j & rel)
            sent = jnp.concatenate([blocks[j | rel].astype(jnp.bfloat16) for j in keep], axis=0)
            came = swap_fsdp(sent, flip).astype(jnp.float32)
            came = jnp.split(came, len(keep), axis=0)
            blocks = {j: blocks[j] + part for j, part in zip(keep, came)}
        return blocks[0]

    def shards(hidden, window_proj, head_weights, ref_logprob, resp_spans):
        z = lax.axis_index("sec")
        f = lax.axis_index("fsdp")
        d, k = z // 2, z % 2
        t, m, c = f // chips, (f % chips) // 2, f % 2
        i0 = 2 * m + t
        weights = window_proj[0]
        rows, cols = weights.shape
        half = cols // 2
        length = ref_logprob.shape[1]
        first = FIRST_START
        kept = length - first

        def col_half(which, array):
            return jnp.where(which == 0, array[:, :half], array[:, half:])

        slots = [
            lax.ppermute(col_half(d ^ j, weights), ("sec", "fsdp"), slab_route(j)) for j in range(2)
        ]
        x_own = hidden[first:]
        x_mate = swap_sec(x_own, 1)
        side = jnp.concatenate([ref_logprob, resp_spans.astype(jnp.float32)], axis=1)
        side_other = swap_fsdp(side, 1)
        side = jnp.where(c == d, side, side_other)
        ref_lp = side[:, first:length]
        starts = side[:, length : length + 1].astype(jnp.int32)
        ending = side[:, length + 1 :].astype(jnp.int32)
        head_mate = swap_sec(head_weights[0], 2)
        head_k = jnp.where(d == 0, head_weights[0], head_mate)
        head_k2 = jnp.where(d == 0, head_mate, head_weights[0])
        actor_head = jnp.where(c == 0, head_k[:half], head_k[half:]).astype(jnp.float32)
        other_head = jnp.where(c == 0, head_k2[:half], head_k2[half:]).astype(jnp.float32)

        w_rel = [
            jnp.concatenate(gather_pieces(slots[0], flips[::-1]), axis=0),
            jnp.concatenate(gather_pieces(slots[1], flips), axis=0),
        ]

        x_own_o = swap_fsdp(x_own, 1)
        x_mate_o = swap_fsdp(x_mate, 1)

        def both(own, mate):
            return jnp.where(
                k == 0,
                jnp.concatenate([own, mate], axis=1),
                jnp.concatenate([mate, own], axis=1),
            )

        x_c, x_o = both(x_own, x_mate), both(x_own_o, x_mate_o)
        x_keep = jnp.where(c == d, x_c, x_o)
        x_send = jnp.where(c == d, x_o, x_c)
        x_all = jnp.concatenate([x_keep, x_send], axis=0)
        toks, feats = x_all.shape
        x_rel = jnp.take(
            x_all.reshape(toks, chips, rows), i0 ^ jnp.arange(chips), axis=1
        ).reshape(toks, feats)
        wide = x_rel.astype(jnp.float32)
        sq = jnp.sum(wide * wide, axis=1)
        sq_keep = sq[:kept] + swap_sec(sq[kept:], 2)
        scale = lax.rsqrt(sq_keep / (2 * feats) + NORM_EPS)

        pre, sums = [], []
        for j in range(2):
            part = jnp.dot(x_rel, w_rel[j], preferred_element_type=jnp.float32)
            came = swap_sec(part[kept:].astype(jnp.bfloat16), 2)
            total = part[:kept] + came.astype(jnp.float32)
            pre.append((total * scale[:, None]).astype(jnp.bfloat16))
        pre_actor = jnp.where(c == 0, pre[0], pre[1])
        pre_other = jnp.where(c == 0, pre[1], pre[0])
        pre_far = swap_sec(pre_actor, 2)
        sums = jnp.stack(
            [
                jnp.sum(h * jax.nn.silu(v.astype(jnp.float32)), axis=1)
                for h, v in ((actor_head, pre_actor), (other_head, pre_other))
            ]
        )
        sums = sums + swap_fsdp(sums, 1)
        sums_mate = swap_sec(sums, 1)
        log_prob = (sums[0] + sums_mate[0])[None]
        value_est = jnp.where(k == 0, sums[1], sums_mate[1])[None]
        scores = jnp.where(k == 0, sums_mate[1], sums[1])[None]
        advantage, signal = advantage_of(
            log_prob, value_est, scores, ref_lp, starts, ending, first
        )
        packed = jnp.stack([advantage[0], signal[0] * scale])
        packed_far = swap_sec(packed, 2)
        mine = jnp.where(c == d, packed[0], packed_far[0])
        advantage_out = jnp.concatenate([jnp.zeros((first,), jnp.float32), mine])[None]

        def slopes_of(coef, values):
            return (
                coef[:, None] * actor_head[None] * silu_slope(values.astype(jnp.float32))
            ).astype(jnp.bfloat16)

        slopes = jnp.concatenate(
            [slopes_of(packed[1], pre_actor), slopes_of(packed_far[1], pre_far)], axis=0
        )
        grad = lax.dot_general(
            x_rel, slopes, (((0,), (0,)), ((), ())), preferred_element_type=jnp.float32
        ).reshape(chips, rows, half)
        lanes = half // 2
        pieces = [
            scatter_sum([grad[j, :, :lanes] for j in range(chips)], flips),
            scatter_sum([grad[j, :, lanes:] for j in range(chips)], flips[::-1]),
        ]
        piece = jnp.concatenate(pieces, axis=1).astype(jnp.bfloat16)
        out = lax.ppermute(piece, ("sec", "fsdp"), final_route()).astype(jnp.float32)
        return (out[None], advantage_out)

    return jax.shard_map(
        shards,
        mesh=mesh,
        in_specs=(
            P("fsdp", "sec"),
            P("sec", "fsdp", None),
            P("sec", None),
            P("fsdp", None),
            P("fsdp", None),
        ),
        out_specs=(P("sec", "fsdp", None), P("fsdp", None)),
        check_vma=False,
    )
```

time: 223 us -> 143 us (0.64)
  waiting for transfers between devices: 166 us -> 77.5 us
  starting transfers between devices: 7.47 us -> 31.9 us
  local copies, waits for them, and re-layouts: 2.15 us -> 15.6 us
  between operations: 15.7 us -> 2.32 us
  blocking collectives: 12 us -> 0 us
  matrix products: 12.3 us -> 5.18 us
  other arithmetic: 5.64 us -> 10.1 us
    all_gather x2 -> x0, waiting for transfers between devices: 107 us -> none  [the longest x1 73.7 us: shards(): features = lax.all_gather(hidden, 'sec', axis=1, tiled=True)]
    ppermute x2 -> x25, waiting for transfers between devices: 0.1 us -> 77.5 us  [the longest x8 40.2 us: swap_sec(): return lax.ppermute(array, 'sec', [(i, i ^ flip) for i in range(4)])]
    reduce_scatter x1 -> x0, waiting for transfers between devices: 57.2 us -> none  [shards(): lax.psum_scatter(lax.dot_general(normed, slopes, (((0,), (0,)), ((), ()))...]
    ppermute x2 -> x25, starting transfers between devices: 7.36 us -> 31.9 us  [the longest x14 12.9 us: swap_fsdp(): return lax.ppermute(array, 'fsdp', [(i, i ^ flip) for i in range(n_dev)])]
    all_gather x1 -> x0, blocking collectives: 12 us -> none  [shards(): totals = lax.all_gather(own_sum, 'sec', axis=1, tiled=True)]
    gather x0 -> x2, local copies, waits for them, and re-layouts: none -> 10.6 us  [shards(): jnp.take(x_all.reshape(toks, chips, rows), i0 ^ jnp.arange(chips), axis=1)]
    dot_general x2 -> x3, matrix products: 10.3 us -> 4.63 us  [the longest x2 3.35 us: shards(): part = jnp.dot(x_rel, w_rel[j], preferred_element_type=jnp.float32)]
    select_n x0 -> x8, other arithmetic: none -> 3.92 us  [the longest x2 2.52 us: shards(): jnp.take(x_all.reshape(toks, chips, rows), i0 ^ jnp.arange(chips), axis=1)]
  transfers between devices with their start and end apart: 5 -> 25, of which waited for: 4 -> 12; matrix products, arithmetic and copies ran while one was open for 4% -> 18% of each run, Pallas kernels for 0% -> 0%
where the time goes in v1:
time: 143 us; the launch traced here: 142 us
  waiting for transfers between devices  77.5 us (54%)
  starting transfers between devices  31.9 us (22%)
  local copies, waits for them, and re-layouts  15.6 us (11%)
  other arithmetic  10.1 us (7%)
  matrix products  5.18 us (4%)
  between operations  2.32 us (2%)
    ppermute x8, waiting for transfers between devices, swap_sec(): return lax.ppermute(array, 'sec', [(i, i ^ flip) for i in range(4)])  40.2 us
    ppermute x14, waiting for transfers between devices, swap_fsdp(): return lax.ppermute(array, 'fsdp', [(i, i ^ flip) for i in range(n_dev)])  21.1 us
    ppermute x14, starting transfers between devices, swap_fsdp(): return lax.ppermute(array, 'fsdp', [(i, i ^ flip) for i in range(n_dev)])  12.9 us
    ppermute x8, starting transfers between devices, swap_sec(): return lax.ppermute(array, 'sec', [(i, i ^ flip) for i in range(4)])  11.8 us
    gather x2, local copies, waits for them, and re-layouts, shards(): jnp.take(x_all.reshape(toks, chips, rows), i0 ^ jnp.arange(chips), axis=1)  10.6 us
    ppermute x1, waiting for transfers between devices, shards(): lax.ppermute(piece, ('sec', 'fsdp'), final_route()).astype(jnp.float32)  8.34 us
    ppermute x2, waiting for transfers between devices, shards(): lax.ppermute(col_half(d ^ j, weights), ('sec', 'fsdp'), slab_route(j))  7.8 us
    ppermute x2, starting transfers between devices, shards(): lax.ppermute(col_half(d ^ j, weights), ('sec', 'fsdp'), slab_route(j))  5.33 us
  transfers between devices with their start and end apart: 25, of which 12 were waited for; matrix products, arithmetic and copies ran while one was open for 18% of the time, Pallas kernels for 0%

profile of v1, /device:TPU:4, one launch (start us, length us, event | category | flops | bytes accessed | tf_op | source)
XLA Modules:
  0.0 142.5 jit_solution(5874953624428502952)
XLA Ops:
  4.3 2.6 %collective-permute-start.4 = (bf16[512]{0:T(512)(128)(2,1)S(1)}, bf16[512]{0:T(512)(128)(2,1)S(1)}, u32[]{:S(2)}, u32[]{:S(2)}) collective-permute-start(bf16[512]{0:T(512)(128)(2,1)S(1)} %reduce.1), channel_id=1, source_target_pairs={{0,16},{8,24},{16,0},{24,8},{1,17},{9,25},{17,1},{25,9},{2,18},{10... | collective-permute-start | bytes 3080 | tf_op jit(solution)/shard_map/ppermute | solution.py:51
  7.7 2.2 %collective-permute-start.5 = (bf16[512,256]{1,0:T(8,128)(2,1)}, bf16[512,256]{1,0:T(8,128)(2,1)}, u32[]{:S(2)}, u32[]{:S(2)}) collective-permute-start(bf16[512,256]{1,0:T(8,128)(2,1)} %get-tuple-element.16), channel_id=1, source_target_pairs={{0,0},{1,4},{2,2},{3,6},{4,16},{5,20},{6,18},{7,22},{8,8},{9,12},{... | collective-permute-start | bytes 786440 | tf_op jit(solution)/shard_map/ppermute | solution.py:114
  9.9 3.2 %collective-permute-start.11 = (bf16[512,256]{1,0:T(8,128)(2,1)S(1)}, bf16[512,256]{1,0:T(8,128)(2,1)S(1)}, u32[]{:S(2)}, u32[]{:S(2)}) collective-permute-start(bf16[512,256]{1,0:T(8,128)(2,1)S(1)} %get-tuple-element.17), channel_id=1, source_target_pairs={{0,1},{1,5},{2,3},{3,7},{4,17},{5,21},{6,19},{7,23},{8,9},{9,13},{... | collective-permute-start | bytes 786440 | tf_op jit(solution)/shard_map/ppermute | solution.py:114
  13.0 11.3 %collective-permute-done = bf16[448,1024]{1,0:T(8,128)(2,1)S(1)} collective-permute-done((bf16[448,1024]{1,0:T(8,128)(2,1)S(1)}, bf16[448,1024]{1,0:T(8,128)(2,1)S(1)}, u32[]{:S(2)}, u32[]{:S(2)}) %collective-permute-start) | collective-permute-done | bytes 917536 | tf_op jit(solution)/shard_map/ppermute | solution.py:51
  25.2 4.9 %collective-permute-done.5 = bf16[512,256]{1,0:T(8,128)(2,1)} collective-permute-done((bf16[512,256]{1,0:T(8,128)(2,1)}, bf16[512,256]{1,0:T(8,128)(2,1)}, u32[]{:S(2)}, u32[]{:S(2)}) %collective-permute-start.5) | collective-permute-done | bytes 262176 | tf_op jit(solution)/shard_map/ppermute | solution.py:114
  31.6 2.9 %collective-permute-done.11 = bf16[512,256]{1,0:T(8,128)(2,1)S(1)} collective-permute-done((bf16[512,256]{1,0:T(8,128)(2,1)S(1)}, bf16[512,256]{1,0:T(8,128)(2,1)S(1)}, u32[]{:S(2)}, u32[]{:S(2)}) %collective-permute-start.11) | collective-permute-done | bytes 262176 | tf_op jit(solution)/shard_map/ppermute | solution.py:114
  34.5 3.7 %collective-permute-start.12 = (bf16[512,256]{1,0:T(8,128)(2,1)S(1)}, bf16[512,256]{1,0:T(8,128)(2,1)S(1)}, u32[]{:S(2)}, u32[]{:S(2)}) collective-permute-start(bf16[512,256]{1,0:T(8,128)(2,1)S(1)} %collective-permute-done.11), channel_id=1, source_target_pairs={{0,4},{1,5},{2,6},{3,7},{4,0},{5,1},{6,2},{7,3},{8,12},{9,13},{10,... | collective-permute-start | bytes 786440 | tf_op jit(solution)/shard_map/ppermute | solution.py:48
  38.9 6.5 %collective-permute-done.12 = bf16[512,256]{1,0:T(8,128)(2,1)S(1)} collective-permute-done((bf16[512,256]{1,0:T(8,128)(2,1)S(1)}, bf16[512,256]{1,0:T(8,128)(2,1)S(1)}, u32[]{:S(2)}, u32[]{:S(2)}) %collective-permute-start.12) | collective-permute-done | bytes 262176 | tf_op jit(solution)/shard_map/ppermute | solution.py:48
  45.4 2.0 %collective-permute-start.8 = (bf16[512,256]{1,0:T(8,128)(2,1)}, bf16[512,256]{1,0:T(8,128)(2,1)S(1)}, u32[]{:S(2)}, u32[]{:S(2)}) collective-permute-start(bf16[512,256]{1,0:T(8,128)(2,1)} %collective-permute-done.7), channel_id=1, source_target_pairs={{0,4},{1,5},{2,6},{3,7},{4,0},{5,1},{6,2},{7,3},{8,12},{9,13},{10,... | collective-permute-start | bytes 786440 | tf_op jit(solution)/shard_map/ppermute | solution.py:48
  49.7 2.1 %pad_maximum_fusion = bf16[896,4,512]{2,0,1:T(8,128)(2,1)} fusion(bf16[448,4,512]{2,0,1:T(8,128)(2,1)S(1)} %get-tuple-element.9, bf16[448,4,512]{2,0,1:T(8,128)(2,1)S(1)} %get-tuple-element.8), kind=kLoop, calls=%fused_computation.2 | loop fusion | flops 7340032 | bytes 7340032 | tf_op jit(solution)/shard_map/concatenate | solution.py:148
  51.7 4.6 %gather_fusion = bf16[4,896,512]{2,1,0:T(8,128)(2,1)} fusion(bf16[896,4,512]{2,0,1:T(8,128)(2,1)} %pad_maximum_fusion, s32[1024]{0:T(1024)S(1)} %pad_clamp_fusion), kind=kCustom, calls=%fused_computation | custom fusion | bytes 7340048 | tf_op jit(solution)/shard_map/jit(_take)/gather | solution.py:150
  56.3 6.0 %copy.16 = bf16[896,4,512]{0,2,1:T(8,128)(2,1)} copy(bf16[896,4,512]{2,0,1:T(8,128)(2,1)} %bitcast.80) | data formatting | bytes 7340032 | tf_op jit(solution)/shard_map/jit(_take)/gather | solution.py:150
  62.3 2.5 %bitcast_select_fusion = bf16[896,2048]{0,1:T(8,128)(2,1)S(1)} fusion(bf16[896,4,512]{0,2,1:T(8,128)(2,1)} %copy.16, pred[2048]{0:T(1024)(128)(4,1)S(1)} %bitcast.98), kind=kLoop, calls=%fused_computation.3 | loop fusion | flops 1835008 | bytes 7342080 | tf_op jit(solution)/shard_map/jit(_take)/select_n | solution.py:150
  68.0 2.2 %fusion = f32[896,256]{1,0:T(8,128)S(1)} fusion(bf16[896,2048]{0,1:T(8,128)(2,1)S(1)} %bitcast_select_fusion, bf16[512,256]{1,0:T(8,128)(2,1)S(1)} %collective-permute-done.8, bf16[512,256]{1,0:T(8,128)(2,1)} %collective-permute-done.7, bf16[512,256]{1,0:T(8,128)(2,1)S(1)} %collective-permute-done.6, bf16[512,256]{1,0:T(8,128)(2,1)} %collective-permute-done.5), kind=kOutput, calls=%fused_computation.8 | convolution fusion | flops 943718400 | bytes 5636096 | tf_op jit(solution)/shard_map/dot_general | solution.py:160
  71.4 1.6 %collective-permute-start.15 = (bf16[448,256]{1,0:T(8,128)(2,1)S(1)}, bf16[448,256]{1,0:T(8,128)(2,1)S(1)}, u32[]{:S(2)}, u32[]{:S(2)}) collective-permute-start(bf16[448,256]{1,0:T(8,128)(2,1)S(1)} %slice.227), channel_id=1, source_target_pairs={{0,16},{8,24},{16,0},{24,8},{1,17},{9,25},{17,1},{25,9},{2,18},{10... | collective-permute-start | bytes 688136 | tf_op jit(solution)/shard_map/ppermute | solution.py:51
  74.4 15.2 %collective-permute-done.15 = bf16[448,256]{1,0:T(8,128)(2,1)S(1)} collective-permute-done((bf16[448,256]{1,0:T(8,128)(2,1)S(1)}, bf16[448,256]{1,0:T(8,128)(2,1)S(1)}, u32[]{:S(2)}, u32[]{:S(2)}) %collective-permute-start.15) | collective-permute-done | bytes 229408 | tf_op jit(solution)/shard_map/ppermute | solution.py:51
  89.6 3.7 %collective-permute-done.9 = bf16[448,256]{1,0:T(8,128)(2,1)S(1)} collective-permute-done((bf16[448,256]{1,0:T(8,128)(2,1)S(1)}, bf16[448,256]{1,0:T(8,128)(2,1)S(1)}, u32[]{:S(2)}, u32[]{:S(2)}) %collective-permute-start.9) | collective-permute-done | bytes 229408 | tf_op jit(solution)/shard_map/ppermute | solution.py:51
  97.2 1.9 %collective-permute-start.19 = (bf16[448,256]{1,0:T(8,128)(2,1)S(1)}, bf16[448,256]{1,0:T(8,128)(2,1)S(1)}, u32[]{:S(2)}, u32[]{:S(2)}) collective-permute-start(bf16[448,256]{1,0:T(8,128)(2,1)S(1)} %get-tuple-element.5), channel_id=1, source_target_pairs={{0,16},{8,24},{16,0},{24,8},{1,17},{9,25},{17,1},{25,9},{2,18},{10... | collective-permute-start | bytes 688136 | tf_op jit(solution)/shard_map/ppermute | solution.py:51
  101.0 10.0 %collective-permute-done.18 = f32[2,448]{1,0:T(2,128)S(1)} collective-permute-done((f32[2,448]{1,0:T(2,128)S(1)}, f32[2,448]{1,0:T(2,128)S(1)}, u32[]{:S(2)}, u32[]{:S(2)}) %collective-permute-start.18) | collective-permute-done | bytes 3616 | tf_op jit(solution)/shard_map/ppermute | solution.py:51
  115.3 5.1 %collective-permute-done.20 = bf16[1024,128]{1,0:T(8,128)(2,1)S(1)} collective-permute-done((bf16[1024,128]{1,0:T(8,128)(2,1)S(1)}, bf16[1024,128]{1,0:T(8,128)(2,1)S(1)}, u32[]{:S(2)}, u32[]{:S(2)}) %collective-permute-start.20) | collective-permute-done | bytes 262176 | tf_op jit(solution)/shard_map/ppermute | solution.py:48
  121.2 4.3 %collective-permute-done.21 = bf16[512,128]{1,0:T(8,128)(2,1)S(1)} collective-permute-done((bf16[512,128]{1,0:T(8,128)(2,1)S(1)}, bf16[512,128]{1,0:T(8,128)(2,1)S(1)}, u32[]{:S(2)}, u32[]{:S(2)}) %collective-permute-start.21) | collective-permute-done | bytes 131104 | tf_op jit(solution)/shard_map/ppermute | solution.py:48
  126.5 4.1 %collective-permute-done.23 = bf16[512,128]{1,0:T(8,128)(2,1)S(1)} collective-permute-done((bf16[512,128]{1,0:T(8,128)(2,1)S(1)}, bf16[512,128]{1,0:T(8,128)(2,1)S(1)}, u32[]{:S(2)}, u32[]{:S(2)}) %collective-permute-start.23) | collective-permute-done | bytes 131104 | tf_op jit(solution)/shard_map/ppermute | solution.py:48
  130.7 1.9 %collective-permute-start.24 = (bf16[512,256]{1,0:T(8,128)(2,1)S(1)}, bf16[512,256]{1,0:T(8,128)(2,1)S(1)}, u32[]{:S(2)}, u32[]{:S(2)}) collective-permute-start(bf16[512,256]{1,0:T(8,128)(2,1)S(1)} %pad_maximum_fusion.3), channel_id=1, source_target_pairs={{0,0},{1,16},{2,2},{3,18},{4,1},{5,17},{6,3},{7,19},{8,8},{9,24},{... | collective-permute-start | bytes 786440 | tf_op jit(solution)/shard_map/ppermute | solution.py:203
  133.3 8.3 %collective-permute-done.24 = bf16[512,256]{1,0:T(8,128)(2,1)S(1)} collective-permute-done((bf16[512,256]{1,0:T(8,128)(2,1)S(1)}, bf16[512,256]{1,0:T(8,128)(2,1)S(1)}, u32[]{:S(2)}, u32[]{:S(2)}) %collective-permute-start.24) | collective-permute-done | bytes 262176 | tf_op jit(solution)/shard_map/ppermute | solution.py:203
  (89 shorter events, 27.2 us)
Async XLA Ops:
  2.0 22.4 %collective-permute-start = (bf16[448,1024]{1,0:T(8,128)(2,1)S(1)}, bf16[448,1024]{1,0:T(8,128)(2,1)S(1)}, u32[]{:S(2)}, u32[]{:S(2)}) collective-permute-start(bf16[448,1024]{1,0:T(8,128)(2,1)S(1)} %slice.103), channel_id=1, source_target_pairs={{0,8},{8,0},{16,24},{24,16},{1,9},{9,1},{17,25},{25,17},{2,10},{10... | collective-permute-start | bytes 2752520 | tf_op jit(solution)/shard_map/ppermute | solution.py:51
  3.6 34.6 %collective-permute-start.1 = (bf16[448,1024]{1,0:T(8,128)(2,1)S(1)}, bf16[448,1024]{1,0:T(8,128)(2,1)S(1)}, u32[]{:S(2)}, u32[]{:S(2)}) collective-permute-start(bf16[448,1024]{1,0:T(8,128)(2,1)S(1)} %slice.103), channel_id=1, source_target_pairs={{0,1},{1,0},{2,3},{3,2},{4,5},{5,4},{6,7},{7,6},{8,9},{9,8},{10,11... | collective-permute-start | bytes 2752520 | tf_op jit(solution)/shard_map/ppermute | solution.py:48
  4.3 20.3 %collective-permute-start.4 = (bf16[512]{0:T(512)(128)(2,1)S(1)}, bf16[512]{0:T(512)(128)(2,1)S(1)}, u32[]{:S(2)}, u32[]{:S(2)}) collective-permute-start(bf16[512]{0:T(512)(128)(2,1)S(1)} %reduce.1), channel_id=1, source_target_pairs={{0,16},{8,24},{16,0},{24,8},{1,17},{9,25},{17,1},{25,9},{2,18},{10... | collective-permute-start | bytes 3080 | tf_op jit(solution)/shard_map/ppermute | solution.py:51
  7.7 22.4 %collective-permute-start.5 = (bf16[512,256]{1,0:T(8,128)(2,1)}, bf16[512,256]{1,0:T(8,128)(2,1)}, u32[]{:S(2)}, u32[]{:S(2)}) collective-permute-start(bf16[512,256]{1,0:T(8,128)(2,1)} %get-tuple-element.16), channel_id=1, source_target_pairs={{0,0},{1,4},{2,2},{3,6},{4,16},{5,20},{6,18},{7,22},{8,8},{9,12},{... | collective-permute-start | bytes 786440 | tf_op jit(solution)/shard_map/ppermute | solution.py:114
  9.9 24.6 %collective-permute-start.11 = (bf16[512,256]{1,0:T(8,128)(2,1)S(1)}, bf16[512,256]{1,0:T(8,128)(2,1)S(1)}, u32[]{:S(2)}, u32[]{:S(2)}) collective-permute-start(bf16[512,256]{1,0:T(8,128)(2,1)S(1)} %get-tuple-element.17), channel_id=1, source_target_pairs={{0,1},{1,5},{2,3},{3,7},{4,17},{5,21},{6,19},{7,23},{8,9},{9,13},{... | collective-permute-start | bytes 786440 | tf_op jit(solution)/shard_map/ppermute | solution.py:114
  24.3 23.1 %collective-permute-start.2 = (bf16[448,1024]{1,0:T(8,128)(2,1)S(1)}, bf16[448,1024]{1,0:T(8,128)(2,1)}, u32[]{:S(2)}, u32[]{:S(2)}) collective-permute-start(bf16[448,1024]{1,0:T(8,128)(2,1)S(1)} %collective-permute-done), channel_id=1, source_target_pairs={{0,1},{1,0},{2,3},{3,2},{4,5},{5,4},{6,7},{7,6},{8,9},{9,8},{10,11... | collective-permute-start | bytes 2752520 | tf_op jit(solution)/shard_map/ppermute | solution.py:48
  24.6 69.5 %collective-permute-start.3 = (f32[1,514]{1,0:T(1,128)S(1)}, f32[1,514]{1,0:T(1,128)S(1)}, u32[]{:S(2)}, u32[]{:S(2)}) collective-permute-start(f32[1,514]{1,0:T(1,128)S(1)} %pad_maximum_fusion.6), channel_id=1, source_target_pairs={{0,1},{1,0},{2,3},{3,2},{4,5},{5,4},{6,7},{7,6},{8,9},{9,8},{10,11... | collective-permute-start | bytes 6176 | tf_op jit(solution)/shard_map/ppermute | solution.py:48
  30.1 8.4 %collective-permute-start.7 = (bf16[512,256]{1,0:T(8,128)(2,1)}, bf16[512,256]{1,0:T(8,128)(2,1)}, u32[]{:S(2)}, u32[]{:S(2)}) collective-permute-start(bf16[512,256]{1,0:T(8,128)(2,1)} %collective-permute-done.5), channel_id=1, source_target_pairs={{0,2},{1,3},{2,0},{3,1},{4,6},{5,7},{6,4},{7,5},{8,10},{9,11},{10,... | collective-permute-start | bytes 786440 | tf_op jit(solution)/shard_map/ppermute | solution.py:48
  34.5 10.9 %collective-permute-start.12 = (bf16[512,256]{1,0:T(8,128)(2,1)S(1)}, bf16[512,256]{1,0:T(8,128)(2,1)S(1)}, u32[]{:S(2)}, u32[]{:S(2)}) collective-permute-start(bf16[512,256]{1,0:T(8,128)(2,1)S(1)} %collective-permute-done.11), channel_id=1, source_target_pairs={{0,4},{1,5},{2,6},{3,7},{4,0},{5,1},{6,2},{7,3},{8,12},{9,13},{10,... | collective-permute-start | bytes 786440 | tf_op jit(solution)/shard_map/ppermute | solution.py:48
  38.2 28.4 %collective-permute-start.6 = (bf16[512,256]{1,0:T(8,128)(2,1)}, bf16[512,256]{1,0:T(8,128)(2,1)S(1)}, u32[]{:S(2)}, u32[]{:S(2)}) collective-permute-start(bf16[512,256]{1,0:T(8,128)(2,1)} %collective-permute-done.5), channel_id=1, source_target_pairs={{0,4},{1,5},{2,6},{3,7},{4,0},{5,1},{6,2},{7,3},{8,12},{9,13},{10,... | collective-permute-start | bytes 786440 | tf_op jit(solution)/shard_map/ppermute | solution.py:48
  38.5 31.8 %collective-permute-start.13 = (bf16[512,256]{1,0:T(8,128)(2,1)S(1)}, bf16[512,256]{1,0:T(8,128)(2,1)S(1)}, u32[]{:S(2)}, u32[]{:S(2)}) collective-permute-start(bf16[512,256]{1,0:T(8,128)(2,1)S(1)} %collective-permute-done.11), channel_id=1, source_target_pairs={{0,2},{1,3},{2,0},{3,1},{4,6},{5,7},{6,4},{7,5},{8,10},{9,11},{10,... | collective-permute-start | bytes 786440 | tf_op jit(solution)/shard_map/ppermute | solution.py:48
  45.4 22.6 %collective-permute-start.8 = (bf16[512,256]{1,0:T(8,128)(2,1)}, bf16[512,256]{1,0:T(8,128)(2,1)S(1)}, u32[]{:S(2)}, u32[]{:S(2)}) collective-permute-start(bf16[512,256]{1,0:T(8,128)(2,1)} %collective-permute-done.7), channel_id=1, source_target_pairs={{0,4},{1,5},{2,6},{3,7},{4,0},{5,1},{6,2},{7,3},{8,12},{9,13},{10,... | collective-permute-start | bytes 786440 | tf_op jit(solution)/shard_map/ppermute | solution.py:48
  47.4 22.8 %collective-permute-start.14 = (bf16[512,256]{1,0:T(8,128)(2,1)S(1)}, bf16[512,256]{1,0:T(8,128)(2,1)S(1)}, u32[]{:S(2)}, u32[]{:S(2)}) collective-permute-start(bf16[512,256]{1,0:T(8,128)(2,1)S(1)} %collective-permute-done.12), channel_id=1, source_target_pairs={{0,2},{1,3},{2,0},{3,1},{4,6},{5,7},{6,4},{7,5},{8,10},{9,11},{10,... | collective-permute-start | bytes 786440 | tf_op jit(solution)/shard_map/ppermute | solution.py:48
  66.6 7.8 %collective-permute-start.10 = (f32[448]{0:T(512)S(1)}, f32[448]{0:T(512)S(1)}, u32[]{:S(2)}, u32[]{:S(2)}) collective-permute-start(f32[448]{0:T(512)S(1)} %slice.113), channel_id=1, source_target_pairs={{0,16},{8,24},{16,0},{24,8},{1,17},{9,25},{17,1},{25,9},{2,18},{10... | collective-permute-start | bytes 5384 | tf_op jit(solution)/shard_map/ppermute | solution.py:51
  71.4 18.2 %collective-permute-start.15 = (bf16[448,256]{1,0:T(8,128)(2,1)S(1)}, bf16[448,256]{1,0:T(8,128)(2,1)S(1)}, u32[]{:S(2)}, u32[]{:S(2)}) collective-permute-start(bf16[448,256]{1,0:T(8,128)(2,1)S(1)} %slice.227), channel_id=1, source_target_pairs={{0,16},{8,24},{16,0},{24,8},{1,17},{9,25},{17,1},{25,9},{2,18},{10... | collective-permute-start | bytes 688136 | tf_op jit(solution)/shard_map/ppermute | solution.py:51
  73.1 20.3 %collective-permute-start.9 = (bf16[448,256]{1,0:T(8,128)(2,1)S(1)}, bf16[448,256]{1,0:T(8,128)(2,1)S(1)}, u32[]{:S(2)}, u32[]{:S(2)}) collective-permute-start(bf16[448,256]{1,0:T(8,128)(2,1)S(1)} %slice.228), channel_id=1, source_target_pairs={{0,16},{8,24},{16,0},{24,8},{1,17},{9,25},{17,1},{25,9},{2,18},{10... | collective-permute-start | bytes 688136 | tf_op jit(solution)/shard_map/ppermute | solution.py:51
  95.3 3.9 %collective-permute-start.17 = (f32[2,448]{1,0:T(2,128)S(1)}, f32[2,448]{1,0:T(2,128)S(1)}, u32[]{:S(2)}, u32[]{:S(2)}) collective-permute-start(f32[2,448]{1,0:T(2,128)S(1)} %fusion.95), channel_id=1, source_target_pairs={{0,8},{8,0},{16,24},{24,16},{1,9},{9,1},{17,25},{25,17},{2,10},{10... | collective-permute-start | bytes 10760 | tf_op jit(solution)/shard_map/ppermute | solution.py:51
  97.2 13.7 %collective-permute-start.19 = (bf16[448,256]{1,0:T(8,128)(2,1)S(1)}, bf16[448,256]{1,0:T(8,128)(2,1)S(1)}, u32[]{:S(2)}, u32[]{:S(2)}) collective-permute-start(bf16[448,256]{1,0:T(8,128)(2,1)S(1)} %get-tuple-element.5), channel_id=1, source_target_pairs={{0,16},{8,24},{16,0},{24,8},{1,17},{9,25},{17,1},{25,9},{2,18},{10... | collective-permute-start | bytes 688136 | tf_op jit(solution)/shard_map/ppermute | solution.py:51
  99.8 11.1 %collective-permute-start.18 = (f32[2,448]{1,0:T(2,128)S(1)}, f32[2,448]{1,0:T(2,128)S(1)}, u32[]{:S(2)}, u32[]{:S(2)}) collective-permute-start(f32[2,448]{1,0:T(2,128)S(1)} %pad_maximum_fusion.5), channel_id=1, source_target_pairs={{0,16},{8,24},{16,0},{24,8},{1,17},{9,25},{17,1},{25,9},{2,18},{10... | collective-permute-start | bytes 10760 | tf_op jit(solution)/shard_map/ppermute | solution.py:51
  112.8 7.6 %collective-permute-start.20 = (bf16[1024,128]{1,0:T(8,128)(2,1)S(1)}, bf16[1024,128]{1,0:T(8,128)(2,1)S(1)}, u32[]{:S(2)}, u32[]{:S(2)}) collective-permute-start(bf16[1024,128]{1,0:T(8,128)(2,1)S(1)} %pad_maximum_fusion.1), channel_id=1, source_target_pairs={{0,4},{1,5},{2,6},{3,7},{4,0},{5,1},{6,2},{7,3},{8,12},{9,13},{10,... | collective-permute-start | bytes 786440 | tf_op jit(solution)/shard_map/ppermute | solution.py:48
  113.7 7.5 %collective-permute-start.22 = (bf16[1024,128]{1,0:T(8,128)(2,1)S(1)}, bf16[1024,128]{1,0:T(8,128)(2,1)S(1)}, u32[]{:S(2)}, u32[]{:S(2)}) collective-permute-start(bf16[1024,128]{1,0:T(8,128)(2,1)S(1)} %pad_maximum_fusion.2), channel_id=1, source_target_pairs={{0,2},{1,3},{2,0},{3,1},{4,6},{5,7},{6,4},{7,5},{8,10},{9,11},{10,... | collective-permute-start | bytes 786440 | tf_op jit(solution)/shard_map/ppermute | solution.py:48
  120.5 5.0 %collective-permute-start.21 = (bf16[512,128]{1,0:T(8,128)(2,1)S(1)}, bf16[512,128]{1,0:T(8,128)(2,1)S(1)}, u32[]{:S(2)}, u32[]{:S(2)}) collective-permute-start(bf16[512,128]{1,0:T(8,128)(2,1)S(1)} %fusion.57), channel_id=1, source_target_pairs={{0,2},{1,3},{2,0},{3,1},{4,6},{5,7},{6,4},{7,5},{8,10},{9,11},{10,... | collective-permute-start | bytes 393224 | tf_op jit(solution)/shard_map/ppermute | solution.py:48
  125.6 5.0 %collective-permute-start.23 = (bf16[512,128]{1,0:T(8,128)(2,1)S(1)}, bf16[512,128]{1,0:T(8,128)(2,1)S(1)}, u32[]{:S(2)}, u32[]{:S(2)}) collective-permute-start(bf16[512,128]{1,0:T(8,128)(2,1)S(1)} %get-tuple-element.11), channel_id=1, source_target_pairs={{0,4},{1,5},{2,6},{3,7},{4,0},{5,1},{6,2},{7,3},{8,12},{9,13},{10,... | collective-permute-start | bytes 393224 | tf_op jit(solution)/shard_map/ppermute | solution.py:48
  130.7 10.9 %collective-permute-start.24 = (bf16[512,256]{1,0:T(8,128)(2,1)S(1)}, bf16[512,256]{1,0:T(8,128)(2,1)S(1)}, u32[]{:S(2)}, u32[]{:S(2)}) collective-permute-start(bf16[512,256]{1,0:T(8,128)(2,1)S(1)} %pad_maximum_fusion.3), channel_id=1, source_target_pairs={{0,0},{1,16},{2,2},{3,18},{4,1},{5,17},{6,3},{7,19},{8,8},{9,24},{... | collective-permute-start | bytes 786440 | tf_op jit(solution)/shard_map/ppermute | solution.py:203
  (5 other events, 58.3 us)

commit v2 on v0

v2 whole, which is shorter than its diff:
```python
import jax
import jax.numpy as jnp
from jax import lax
from jax.experimental import pallas as pl
from jax.experimental.pallas import tpu as pltpu
from jax.sharding import PartitionSpec as P


KL_COEF = 0.1
DISCOUNT = 1.0
TRACE_DECAY = 0.95
NORM_EPS = 1e-05
FIRST_START = 64


def silu_slope(values):
    sigmoid = jax.nn.sigmoid(values)
    return sigmoid * (1.0 + values * (1.0 - sigmoid))


def advantage_of(log_prob, value_est, scores, ref_logprob, starts, ending, first):
    length = log_prob.shape[1]
    position = lax.broadcasted_iota(jnp.int32, (1, length), 1) + first
    inside = ((position >= starts) & (position < ending)).astype(jnp.float32)
    last_tok = (position == ending - 1).astype(jnp.float32)
    follow = (position + 1 < ending).astype(jnp.float32)
    reward = -KL_COEF * (log_prob - ref_logprob) * inside + scores * last_tok
    next_value = jnp.concatenate(
        [value_est[:, 1:], jnp.zeros((value_est.shape[0], 1), jnp.float32)], axis=1
    )
    deltas = (reward + DISCOUNT * next_value * follow - value_est) * inside
    source_pos = lax.broadcasted_iota(jnp.int32, (length, length), 0)
    target_pos = lax.broadcasted_iota(jnp.int32, (length, length), 1)
    spacing = source_pos - target_pos
    decays = jnp.where(
        spacing >= 0,
        jnp.power(jnp.float32(DISCOUNT * TRACE_DECAY), jnp.maximum(spacing, 0).astype(jnp.float32)),
        jnp.float32(0.0),
    )
    advantage = jnp.dot(deltas, decays, precision=lax.Precision.HIGHEST) * inside
    counts = (ending - starts).astype(jnp.float32)
    return advantage, -advantage / counts


WHOLE = pl.BlockSpec(memory_space=pltpu.VMEM)
FLAGS = pl.BlockSpec(memory_space=pltpu.SMEM)


def by_source(flag_ref, native, refs, run):
    own_ref, own_o_ref, mate_ref, mate_o_ref = refs
    own_near = flag_ref[1] == 1
    for is_native, own, mate in ((True, own_ref, mate_ref), (False, own_o_ref, mate_o_ref)):
        here = native if is_native else jnp.logical_not(native)
        pl.when(here & own_near)(lambda own=own, mate=mate: run(own, mate))
        pl.when(here & jnp.logical_not(own_near))(lambda own=own, mate=mate: run(mate, own))


def block_of(flag_ref, near, far, j):
    block = near.shape[1] // 2
    half = flag_ref[2] if j % 2 == 0 else 1 - flag_ref[2]
    source = far if j >= 2 else near
    return source[:, pl.ds(pl.multiple_of(half * block, block), block)]


def products(flags, keep, sources, pieces, squares):
    tokens, _ = sources[0].shape
    half = pieces[0][0].shape[1]
    slabs = len(pieces)

    def body(flag_ref, *refs):
        source_refs, refs = refs[:4], refs[4:]
        piece_refs, refs = refs[: 4 * slabs], refs[4 * slabs :]
        part_refs, sent_ref = refs[:slabs], refs[slabs]
        native = flag_ref[0] == (1 if keep else 0)

        def run(near, far):
            for s in range(slabs):
                total = None
                for j in range(4):
                    term = jnp.dot(
                        block_of(flag_ref, near, far, j),
                        piece_refs[4 * s + j][...],
                        preferred_element_type=jnp.float32,
                    )
                    total = term if total is None else total + term
                part_refs[s][...] = total
            if squares:
                sums = jnp.zeros((tokens, 128), jnp.float32)
                for j in range(4):
                    value = block_of(flag_ref, near, far, j).astype(jnp.float32)
                    value = value * value
                    for lane in range(0, value.shape[1], 128):
                        sums = sums + value[:, lane : lane + 128]
                refs[slabs + 1][...] = jnp.sum(sums.T, axis=0, keepdims=True)

        by_source(flag_ref, native, source_refs, run)
        if slabs == 1:
            sent_ref[...] = part_refs[0][...].astype(jnp.bfloat16)
        else:
            @pl.when(flag_ref[3] == 0)
            def _():
                sent_ref[...] = part_refs[0][...].astype(jnp.bfloat16)

            @pl.when(flag_ref[3] != 0)
            def _():
                sent_ref[...] = part_refs[1][...].astype(jnp.bfloat16)

    shapes = [jax.ShapeDtypeStruct((tokens, half), jnp.float32)] * slabs
    shapes += [jax.ShapeDtypeStruct((tokens, half), jnp.bfloat16)]
    shapes += [jax.ShapeDtypeStruct((1, tokens), jnp.float32)] * squares
    return pl.pallas_call(
        body,
        in_specs=[FLAGS] + [WHOLE] * (4 + 4 * slabs),
        out_specs=[WHOLE] * len(shapes),
        out_shape=shapes,
        name="products",
    )(flags, *sources, *[p for group in pieces for p in group])


def turned(flags, keep_sources, send_sources):
    tokens, feats = keep_sources[0].shape
    block = feats // 2

    def body(flag_ref, *refs):
        keep_refs, send_refs, out_ref = refs[:4], refs[4:8], refs[8]

        def outer(near, far):
            def inner(near_s, far_s):
                for j in range(4):
                    value = jnp.concatenate(
                        [block_of(flag_ref, near, far, j), block_of(flag_ref, near_s, far_s, j)]
                    )
                    out_ref[j * block : (j + 1) * block, :] = value.T

            return inner

        native = flag_ref[0] == 1
        own_near = flag_ref[1] == 1
        for is_native in (True, False):
            here = native if is_native else jnp.logical_not(native)
            k_own, k_mate = (keep_refs[0], keep_refs[2]) if is_native else (keep_refs[1], keep_refs[3])
            s_own, s_mate = (send_refs[1], send_refs[3]) if is_native else (send_refs[0], send_refs[2])

            @pl.when(here & own_near)
            def _():
                outer(k_own, k_mate)(s_own, s_mate)

            @pl.when(here & jnp.logical_not(own_near))
            def _():
                outer(k_mate, k_own)(s_mate, s_own)

    return pl.pallas_call(
        body,
        in_specs=[FLAGS] + [WHOLE] * 8,
        out_specs=WHOLE,
        out_shape=jax.ShapeDtypeStruct((2 * feats, 2 * tokens), keep_sources[0].dtype),
        name="turned",
    )(flags, *keep_sources, *send_sources)


def solution(mesh):
    n_dev = mesh.shape["fsdp"]
    chips = n_dev // 2
    top = chips.bit_length() - 1

    def swap_fsdp(array, flip):
        return lax.ppermute(array, "fsdp", [(i, i ^ flip) for i in range(n_dev)])

    def swap_sec(array, flip):
        return lax.ppermute(array, "sec", [(i, i ^ flip) for i in range(4)])

    def split(f):
        return f >> top, (f & (chips - 1)) >> 1, f & 1

    def join(t, m, c):
        return (t << top) | (m << 1) | c

    def plane_route(slot):
        pairs = []
        for f in range(n_dev):
            t, m, r = split(f)
            pairs.append((f, join(r, m, t ^ slot)))
        return pairs

    def final_route():
        pairs = []
        for z in range(4):
            for f in range(n_dev):
                d, k = z >> 1, z & 1
                t, m, c = split(f)
                pairs.append((z * n_dev + f, (2 * c + k) * n_dev + d * chips + 2 * m + t))
        return pairs

    m_bits = top - 1
    flips = [(1, n_dev // 2)] + [(2 << j, 2 << j) for j in range(m_bits)]

    def gather_pieces(own, order):
        pieces = {0: own}
        for rel, flip in order:
            for j in sorted(pieces):
                pieces[j | rel] = swap_fsdp(pieces[j], flip)
        return [pieces[j] for j in range(chips)]

    def scatter_sum(blocks, order):
        blocks = dict(enumerate(blocks))
        for rel, flip in order:
            keep = sorted(j for j in blocks if not j & rel)
            sent = jnp.concatenate([blocks[j | rel].astype(jnp.bfloat16) for j in keep], axis=0)
            came = swap_fsdp(lax.optimization_barrier(sent), flip).astype(jnp.float32)
            came = jnp.split(came, len(keep), axis=0)
            blocks = {j: blocks[j] + part for j, part in zip(keep, came)}
        return blocks[0]

    def shards(hidden, window_proj, head_weights, ref_logprob, resp_spans):
      z = lax.axis_index("sec")
      f = lax.axis_index("fsdp")
      d, k = z // 2, z % 2
      t, m, c = f // chips, (f % chips) // 2, f % 2
      i0 = 2 * m + t
      weights = window_proj[0]
      rows, cols = weights.shape
      half = cols // 2
      length = ref_logprob.shape[1]
      first = FIRST_START
      kept = length - first

      def col_half(which, array):
          return jnp.where(which == 0, array[..., :half], array[..., half:])

      routed = []
      for j in range(2):
          routed.append(lax.ppermute(col_half(t ^ j, weights), "fsdp", plane_route(j)))
      stay = jnp.where(c == d, routed[0], routed[1])
      leave = jnp.where(c == d, routed[1], routed[0])
      came = swap_sec(leave, 2)
      w_own = gather_pieces(stay, flips[::-1])
      w_far = gather_pieces(came, flips)

      x_own = hidden[first:]
      swaps = {}
      for name, other in (("xsend", 1), ("xkeep", 0)):
          pairs = [
              (zz * n_dev + ff, (zz ^ 1) * n_dev + ff)
              for zz in range(4)
              for ff in range(n_dev)
              if (ff & 1) == (zz >> 1) ^ other
          ]
          swaps[name] = lax.ppermute(x_own, ("sec", "fsdp"), pairs)
          pairs = [
              (zz * n_dev + ff, zz * n_dev + (ff ^ 1))
              for zz in range(4)
              for ff in range(n_dev)
              if (ff & 1) == (zz >> 1) ^ other
          ]
          swaps[name + "core"] = lax.ppermute(swaps[name], ("sec", "fsdp"), pairs)
      x_own_o = swap_fsdp(x_own, 1)
      side = jnp.concatenate([ref_logprob, resp_spans.astype(jnp.float32)], axis=1)
      side_o = swap_fsdp(side, 1)
      side = jnp.where(c == d, jnp.concatenate([side, side_o]), jnp.concatenate([side_o, side]))
      ref_lp = side[:, first:length]
      starts = side[:, length : length + 1].astype(jnp.int32)
      ending = side[:, length + 1 :].astype(jnp.int32)

      local = chips == 4 and rows % 128 == 0
      feats = 2 * x_own.shape[1]
      send_sources = (x_own, x_own_o, swaps["xsend"], swaps["xsendcore"])
      keep_sources = (x_own, x_own_o, swaps["xkeep"], swaps["xkeepcore"])
      if local:
          flags = jnp.stack([(c == d).astype(jnp.int32), (m == k).astype(jnp.int32), t, d])
          send_own, sent_own, sq_send = products(flags, False, send_sources, [w_own], True)
          send_far, sent_far = products(flags, False, send_sources, [w_far], False)
          keep_own, keep_far, sent_actor, sq_keep = products(
              flags, True, keep_sources, [w_own, w_far], True
          )
          x_turned = turned(flags, keep_sources, send_sources)
      else:
          def features_of(native, sources):
              near, far = jnp.where(native, sources[0], sources[1]), jnp.where(native, sources[2], sources[3])
              whole = jnp.where(
                  k == 0,
                  jnp.concatenate([near, far], axis=1),
                  jnp.concatenate([far, near], axis=1),
              )
              whole = jnp.take(
                  whole.reshape(kept, chips, rows), i0 ^ jnp.arange(chips), axis=1
              ).reshape(kept, -1)
              wide = whole.astype(jnp.float32)
              return whole, jnp.sum(wide * wide, axis=1)[None]

          def product(x, pieces):
              return jnp.dot(x, jnp.concatenate(pieces, axis=0), preferred_element_type=jnp.float32)

          x_send, sq_send = features_of(c != d, send_sources)
          x_keep, sq_keep = features_of(c == d, keep_sources)
          send_own, send_far = product(x_send, w_own), product(x_send, w_far)
          keep_own, keep_far = product(x_keep, w_own), product(x_keep, w_far)
          sent_own, sent_far = send_own.astype(jnp.bfloat16), send_far.astype(jnp.bfloat16)
          sent_actor = jnp.where(d == 0, keep_own, keep_far).astype(jnp.bfloat16)
          x_turned = jnp.concatenate([x_keep, x_send]).T

      small = jnp.concatenate([sq_send[0], head_weights[0].astype(jnp.float32)])
      small_far = swap_sec(small, 2)
      head_own = col_half(c, head_weights[0].astype(jnp.float32))
      head_far = col_half(c, small_far[kept:])

      def scale_of(sq):
          return lax.rsqrt(sq / (2 * feats) + NORM_EPS)

      scale_keep = scale_of(sq_keep[0] + small_far[:kept])

      got_far = swap_sec(sent_own, 2)
      got_own = swap_sec(sent_far, 2)
      got_actor = swap_sec(sent_actor, 2)

      def pre_of(part, got, row_scale):
          return ((part + got.astype(jnp.float32)) * row_scale[:, None]).astype(jnp.bfloat16)

      pre_own = pre_of(keep_own, got_own, scale_keep)
      pre_far = pre_of(keep_far, got_far, scale_keep)
      pre_keep = jnp.where(d == 0, pre_own, pre_far)
      actor_head = jnp.where(d == 0, head_own, head_far)
      sum_own, sum_far = [
          jnp.sum(h * jax.nn.silu(v.astype(jnp.float32)), axis=1)
          for h, v in ((head_own, pre_own), (head_far, pre_far))
      ]
      sums = jnp.where(d == 0, jnp.stack([sum_own, sum_far]), jnp.stack([sum_far, sum_own]))
      sums = sums + swap_fsdp(sums, 1)
      others = [swap_sec(sums, 1), swap_sec(jnp.concatenate([sums, sq_keep]), 2), swap_sec(sums, 3)]
      scale_send = scale_of(sq_send[0] + others[1][2])
      pre_send = pre_of(jnp.where(d == 0, send_own, send_far), got_actor, scale_send)
      log_prob = jnp.stack([sums[0] + others[0][0], others[1][0] + others[2][0]])
      same_k = jnp.stack([sums[1], others[1][1]])
      other_k = jnp.stack([others[0][1], others[2][1]])
      value_est = jnp.where(k == 0, same_k, other_k)
      scores = jnp.where(k == 0, other_k, same_k)
      advantage, signal = advantage_of(
          log_prob, value_est, scores, ref_lp, starts, ending, first
      )
      mine = jnp.where(c == d, advantage[0], advantage[1])
      advantage_out = jnp.concatenate([jnp.zeros((first,), jnp.float32), mine])[None]
      coef_keep, coef_send = signal[0] * scale_keep, signal[1] * scale_send

      def slopes_of(row_coef, values):
          return (
              row_coef[:, None] * actor_head[None] * silu_slope(values.astype(jnp.float32))
          ).astype(jnp.bfloat16)

      slopes = jnp.concatenate(
          [slopes_of(coef_keep, pre_keep), slopes_of(coef_send, pre_send)], axis=0
      )
      grad = jnp.dot(
          x_turned, slopes, preferred_element_type=jnp.float32
      ).reshape(chips, rows, half)
      lanes = half // 2
      pieces = [
          scatter_sum([grad[j, :, :lanes] for j in range(chips)], flips),
          scatter_sum([grad[j, :, lanes:] for j in range(chips)], flips[::-1]),
      ]
      piece = jnp.concatenate(pieces, axis=1).astype(jnp.bfloat16)
      out = lax.ppermute(piece, ("sec", "fsdp"), final_route())
      return (out.astype(jnp.float32)[None], advantage_out)

    return jax.shard_map(
        shards,
        mesh=mesh,
        in_specs=(
            P("fsdp", "sec"),
            P("sec", "fsdp", None),
            P("sec", None),
            P("fsdp", None),
            P("fsdp", None),
        ),
        out_specs=(P("sec", "fsdp", None), P("fsdp", None)),
        check_vma=False,
    )
```

time: 223 us -> 143 us (0.64)
  waiting for transfers between devices: 166 us -> 60.3 us
  starting transfers between devices: 7.47 us -> 48.9 us
  Pallas kernels: 0 us -> 19.1 us
  between operations: 15.7 us -> 1.19 us
  blocking collectives: 12 us -> 0 us
  matrix products: 12.3 us -> 1.81 us
  other arithmetic: 5.64 us -> 8.51 us
    all_gather x2 -> x0, waiting for transfers between devices: 107 us -> none  [the longest x1 73.7 us: shards(): features = lax.all_gather(hidden, 'sec', axis=1, tiled=True)]
    ppermute x2 -> x28, waiting for transfers between devices: 0.1 us -> 60.3 us  [the longest x13 27.2 us: swap_fsdp(): return lax.ppermute(array, 'fsdp', [(i, i ^ flip) for i in range(n_dev)])]
    reduce_scatter x1 -> x0, waiting for transfers between devices: 57.2 us -> none  [shards(): lax.psum_scatter(lax.dot_general(normed, slopes, (((0,), (0,)), ((), ()))...]
    ppermute x2 -> x28, starting transfers between devices: 7.36 us -> 48.9 us  [the longest x13 21.4 us: swap_fsdp(): return lax.ppermute(array, 'fsdp', [(i, i ^ flip) for i in range(n_dev)])]
    pallas_call x0 -> x4, Pallas kernels: none -> 19.1 us  [the longest x3 13.1 us: products(): pl.pallas_call(body, in_specs=[FLAGS] + [WHOLE] * (4 + 4 * slabs), out_sp...]
    all_gather x1 -> x0, blocking collectives: 12 us -> none  [shards(): totals = lax.all_gather(own_sum, 'sec', axis=1, tiled=True)]
    dot_general x2 -> x1, matrix products: 10.3 us -> 1.25 us  [shards(): jnp.dot(x_turned, slopes, preferred_element_type=jnp.float32)]
  transfers between devices with their start and end apart: 5 -> 28, of which waited for: 4 -> 15; matrix products, arithmetic and copies ran while one was open for 4% -> 5% of each run, Pallas kernels for 0% -> 13%
where the time goes in v2:
time: 143 us
  waiting for transfers between devices  60.3 us (42%)
  starting transfers between devices  48.9 us (34%)
  Pallas kernels  19.1 us (13%)
  other arithmetic  8.51 us (6%)
  local copies, waits for them, and re-layouts  3.1 us (2%)
  matrix products  1.81 us (1%)
    ppermute x13, waiting for transfers between devices, swap_fsdp(): return lax.ppermute(array, 'fsdp', [(i, i ^ flip) for i in range(n_dev)])  27.2 us
    ppermute x13, starting transfers between devices, swap_fsdp(): return lax.ppermute(array, 'fsdp', [(i, i ^ flip) for i in range(n_dev)])  21.4 us
    ppermute x8, waiting for transfers between devices, swap_sec(): return lax.ppermute(array, 'sec', [(i, i ^ flip) for i in range(4)])  17.3 us
    ppermute x8, starting transfers between devices, swap_sec(): return lax.ppermute(array, 'sec', [(i, i ^ flip) for i in range(4)])  15.2 us
    pallas_call x3, Pallas kernels, products(): pl.pallas_call(body, in_specs=[FLAGS] + [WHOLE] * (4 + 4 * slabs), out_sp...  13.1 us
    ppermute x1, waiting for transfers between devices, shards(): out = lax.ppermute(piece, ('sec', 'fsdp'), final_route())  9.21 us
    ppermute x2, waiting for transfers between devices, shards(): lax.ppermute(col_half(t ^ j, weights), 'fsdp', plane_route(j))  6.62 us
    pallas_call x1, Pallas kernels, turned(): pl.pallas_call(body, in_specs=[FLAGS] + [WHOLE] * 8, out_specs=WHOLE, out...  6.07 us
  transfers between devices with their start and end apart: 28, of which 15 were waited for; matrix products, arithmetic and copies ran while one was open for 5% of the time, Pallas kernels for 13%

profile of v2, /device:TPU:4, one launch (start us, length us, event | category | flops | bytes accessed | tf_op | source)
XLA Modules:
  0.0 143.0 jit_solution(15815085919626952562)
XLA Ops:
  2.7 3.5 %collective-permute-start.1 = (bf16[448,1024]{1,0:T(8,128)(2,1)S(1)}, bf16[448,1024]{1,0:T(8,128)(2,1)}, u32[]{:S(2)}, u32[]{:S(2)}) collective-permute-start(bf16[448,1024]{1,0:T(8,128)(2,1)S(1)} %slice.110.refs_0_.refs_4_), channel_id=1, source_target_pairs={{0,8},{2,10},{4,12},{6,14},{8,0},{10,2},{12,4},{14,6},{17,25},{19,... | collective-permute-start | bytes 2752520 | tf_op jit(solution)/shard_map/ppermute | solution.py:248
  6.3 2.4 %collective-permute-start.6 = (bf16[512,256]{1,0:T(8,128)(2,1)S(1)}, bf16[512,256]{1,0:T(8,128)(2,1)S(1)}, u32[]{:S(2)}, u32[]{:S(2)}) collective-permute-start(bf16[512,256]{1,0:T(8,128)(2,1)S(1)} %get-tuple-element.40), channel_id=1, source_target_pairs={{0,0},{1,4},{2,2},{3,6},{4,1},{5,5},{6,3},{7,7},{8,8},{9,12},{10,1... | collective-permute-start | bytes 786440 | tf_op jit(solution)/shard_map/ppermute | solution.py:232
  8.8 5.2 %collective-permute-done.6 = bf16[512,256]{1,0:T(8,128)(2,1)S(1)} collective-permute-done((bf16[512,256]{1,0:T(8,128)(2,1)S(1)}, bf16[512,256]{1,0:T(8,128)(2,1)S(1)}, u32[]{:S(2)}, u32[]{:S(2)}) %collective-permute-start.6) | collective-permute-done | bytes 262176 | tf_op jit(solution)/shard_map/ppermute | solution.py:232
  15.5 3.0 %collective-permute-start.11 = (bf16[512,256]{1,0:T(8,128)(2,1)S(1)}, bf16[512,256]{1,0:T(8,128)(2,1)S(1)}, u32[]{:S(2)}, u32[]{:S(2)}) collective-permute-start(bf16[512,256]{1,0:T(8,128)(2,1)S(1)} %get-tuple-element.37), channel_id=1, source_target_pairs={{0,16},{8,24},{16,0},{24,8},{1,17},{9,25},{17,1},{25,9},{2,18},{10... | collective-permute-start | bytes 786440 | tf_op jit(solution)/shard_map/ppermute | solution.py:170
  21.5 10.7 %collective-permute-start.5 = (f32[1,514]{1,0:T(1,128)S(1)}, f32[1,514]{1,0:T(1,128)S(1)}, u32[]{:S(2)}, u32[]{:S(2)}) collective-permute-start(f32[1,514]{1,0:T(1,128)S(1)} %pad_maximum_fusion.7), channel_id=1, source_target_pairs={{0,1},{1,0},{2,3},{3,2},{4,5},{5,4},{6,7},{7,6},{8,9},{9,8},{10,11... | collective-permute-start | bytes 6176 | tf_op jit(solution)/shard_map/ppermute | solution.py:167
  35.3 2.5 %collective-permute-start.2 = (bf16[448,1024]{1,0:T(8,128)(2,1)}, bf16[448,1024]{1,0:T(8,128)(2,1)}, u32[]{:S(2)}, u32[]{:S(2)}) collective-permute-start(bf16[448,1024]{1,0:T(8,128)(2,1)} %collective-permute-done.1.refs_2_), channel_id=1, source_target_pairs={{0,1},{2,3},{4,5},{6,7},{8,9},{10,11},{12,13},{14,15},{17,16},{19,... | collective-permute-start | bytes 2752520 | tf_op jit(solution)/shard_map/ppermute | solution.py:255
  38.9 2.8 %collective-permute-done.9.refs_6_ = bf16[512,256]{1,0:T(8,128)(2,1)S(1)} collective-permute-done((bf16[512,256]{1,0:T(8,128)(2,1)S(1)}, bf16[512,256]{1,0:T(8,128)(2,1)S(1)}, u32[]{:S(2)}, u32[]{:S(2)}) %collective-permute-start.9) | collective-permute-done | bytes 262176 | tf_op jit(solution)/shard_map/ppermute | solution.py:167
  45.0 5.9 %collective-permute-done.12.refs_9_.refs_5_ = bf16[512,256]{1,0:T(8,128)(2,1)} collective-permute-done((bf16[512,256]{1,0:T(8,128)(2,1)S(1)}, bf16[512,256]{1,0:T(8,128)(2,1)}, u32[]{:S(2)}, u32[]{:S(2)}) %collective-permute-start.12) | collective-permute-done | bytes 262176 | tf_op jit(solution)/shard_map/ppermute | solution.py:167
  52.4 2.5 %collective-permute-done.10.refs_7_ = bf16[512,256]{1,0:T(8,128)(2,1)} collective-permute-done((bf16[512,256]{1,0:T(8,128)(2,1)S(1)}, bf16[512,256]{1,0:T(8,128)(2,1)}, u32[]{:S(2)}, u32[]{:S(2)}) %collective-permute-start.10) | collective-permute-done | bytes 262176 | tf_op jit(solution)/shard_map/ppermute | solution.py:167
  58.2 4.0 %products.5 = (f32[448,256]{1,0:T(8,128)}, bf16[448,256]{1,0:T(8,128)(2,1)}, f32[1,448]{1,0:T(1,128)}) custom-call(s32[4]{0:T(128)} %pad_add_fusion.flag_ref, bf16[448,1024]{1,0:T(8,128)(2,1)} %copy-done, bf16[448,1024]{1,0:T(8,128)(2,1)} %copy-done.1, bf16[448,1024]{1,0:T(8,128)(2,1)} %copy-done.3, ...), custom_call_target="tpu_custom_call" | custom-call | tf_op jit(solution)/shard_map/products/pallas_call | solution.py:111
  63.0 4.7 %collective-permute-start.16 = (f32[960]{0:T(1024)S(1)}, f32[960]{0:T(1024)S(1)}, u32[]{:S(2)}, u32[]{:S(2)}) collective-permute-start(f32[960]{0:T(1024)S(1)} %pad_maximum_fusion.4), channel_id=1, source_target_pairs={{0,16},{8,24},{16,0},{24,8},{1,17},{9,25},{17,1},{25,9},{2,18},{10... | collective-permute-start | bytes 11528 | tf_op jit(solution)/shard_map/ppermute | solution.py:170
  67.9 3.9 %products.4 = (f32[448,256]{1,0:T(8,128)}, bf16[448,256]{1,0:T(8,128)(2,1)}) custom-call(s32[4]{0:T(128)} %pad_add_fusion.flag_ref, bf16[448,1024]{1,0:T(8,128)(2,1)} %copy-done, bf16[448,1024]{1,0:T(8,128)(2,1)} %copy-done.1, bf16[448,1024]{1,0:T(8,128)(2,1)} %copy-done.3, bf16[448,1024]{1,0:T(8,128)(2,1)} %collective-permute-done.4.refs_7_.refs_3_, ...), custom_call_target="tpu_custom_call" | custom-call | tf_op jit(solution)/shard_map/products/pallas_call | solution.py:111
  71.8 2.9 %collective-permute-start.17 = (bf16[448,256]{1,0:T(8,128)(2,1)S(1)}, bf16[448,256]{1,0:T(8,128)(2,1)S(1)}, u32[]{:S(2)}, u32[]{:S(2)}) collective-permute-start(bf16[448,256]{1,0:T(8,128)(2,1)S(1)} %copy-done.17), channel_id=1, source_target_pairs={{0,16},{8,24},{16,0},{24,8},{1,17},{9,25},{17,1},{25,9},{2,18},{10... | collective-permute-start | bytes 688136 | tf_op jit(solution)/shard_map/ppermute | solution.py:170
  74.7 5.2 %products.3 = (f32[448,256]{1,0:T(8,128)}, f32[448,256]{1,0:T(8,128)}, bf16[448,256]{1,0:T(8,128)(2,1)}, f32[1,448]{1,0:T(1,128)}) custom-call(s32[4]{0:T(128)} %pad_add_fusion.flag_ref, bf16[448,1024]{1,0:T(8,128)(2,1)} %copy-done, bf16[448,1024]{1,0:T(8,128)(2,1)} %copy-done.1, bf16[448,1024]{1,0:T(8,128)(2,1)} %collective-permute-done.1.refs_2_, ...), custom_call_target="tpu_custom_call" | custom-call | tf_op jit(solution)/shard_map/products/pallas_call | solution.py:111
  80.6 9.8 %collective-permute-done.15 = bf16[448,256]{1,0:T(8,128)(2,1)S(1)} collective-permute-done((bf16[448,256]{1,0:T(8,128)(2,1)}, bf16[448,256]{1,0:T(8,128)(2,1)S(1)}, u32[]{:S(2)}, u32[]{:S(2)}) %collective-permute-start.15) | collective-permute-done | bytes 229408 | tf_op jit(solution)/shard_map/ppermute | solution.py:170
  90.4 2.9 %collective-permute-done.17 = bf16[448,256]{1,0:T(8,128)(2,1)S(1)} collective-permute-done((bf16[448,256]{1,0:T(8,128)(2,1)S(1)}, bf16[448,256]{1,0:T(8,128)(2,1)S(1)}, u32[]{:S(2)}, u32[]{:S(2)}) %collective-permute-start.17) | collective-permute-done | bytes 229408 | tf_op jit(solution)/shard_map/ppermute | solution.py:170
  95.4 6.1 %turned.1 = bf16[2048,896]{1,0:T(8,128)(2,1)} custom-call(s32[4]{0:T(128)} %pad_add_fusion.flag_ref, bf16[448,1024]{1,0:T(8,128)(2,1)} %copy-done, bf16[448,1024]{1,0:T(8,128)(2,1)} %copy-done.1, bf16[448,1024]{1,0:T(8,128)(2,1)} %collective-permute-done.1.refs_2_, bf16[448,1024]{1,0:T(8,128)(2,1)} %collective-permute-done.2.refs_3_, ...), custom_call_target="tpu_custom_call" | custom-call | tf_op jit(solution)/shard_map/turned/pallas_call | solution.py:152
  103.3 2.7 %collective-permute-start.21 = (f32[2,448]{1,0:T(2,128)S(1)}, f32[2,448]{1,0:T(2,128)S(1)}, u32[]{:S(2)}, u32[]{:S(2)}) collective-permute-start(f32[2,448]{1,0:T(2,128)S(1)} %fusion.77), channel_id=1, source_target_pairs={{0,24},{8,16},{16,8},{24,0},{1,25},{9,17},{17,9},{25,1},{2,26},{10... | collective-permute-start | bytes 10760 | tf_op jit(solution)/shard_map/ppermute | solution.py:170
  106.0 2.7 %collective-permute-done.21 = f32[2,448]{1,0:T(2,128)S(1)} collective-permute-done((f32[2,448]{1,0:T(2,128)S(1)}, f32[2,448]{1,0:T(2,128)S(1)}, u32[]{:S(2)}, u32[]{:S(2)}) %collective-permute-start.21) | collective-permute-done | bytes 3616 | tf_op jit(solution)/shard_map/ppermute | solution.py:170
  114.5 5.6 %collective-permute-done.23 = bf16[1024,128]{1,0:T(8,128)(2,1)S(1)} collective-permute-done((bf16[1024,128]{1,0:T(8,128)(2,1)S(1)}, bf16[1024,128]{1,0:T(8,128)(2,1)S(1)}, u32[]{:S(2)}, u32[]{:S(2)}) %collective-permute-start.23) | collective-permute-done | bytes 262176 | tf_op jit(solution)/shard_map/ppermute | solution.py:167
  121.1 4.2 %collective-permute-done.24 = bf16[512,128]{1,0:T(8,128)(2,1)S(1)} collective-permute-done((bf16[512,128]{1,0:T(8,128)(2,1)S(1)}, bf16[512,128]{1,0:T(8,128)(2,1)S(1)}, u32[]{:S(2)}, u32[]{:S(2)}) %collective-permute-start.24) | collective-permute-done | bytes 131104 | tf_op jit(solution)/shard_map/ppermute | solution.py:167
  125.8 4.5 %collective-permute-done.26 = bf16[512,128]{1,0:T(8,128)(2,1)S(1)} collective-permute-done((bf16[512,128]{1,0:T(8,128)(2,1)S(1)}, bf16[512,128]{1,0:T(8,128)(2,1)S(1)}, u32[]{:S(2)}, u32[]{:S(2)}) %collective-permute-start.26) | collective-permute-done | bytes 131104 | tf_op jit(solution)/shard_map/ppermute | solution.py:167
  130.4 1.9 %collective-permute-start.27 = (bf16[512,256]{1,0:T(8,128)(2,1)S(1)}, bf16[512,256]{1,0:T(8,128)(2,1)S(1)}, u32[]{:S(2)}, u32[]{:S(2)}) collective-permute-start(bf16[512,256]{1,0:T(8,128)(2,1)S(1)} %pad_maximum_fusion.2), channel_id=1, source_target_pairs={{0,0},{1,16},{2,2},{3,18},{4,1},{5,17},{6,3},{7,19},{8,8},{9,24},{... | collective-permute-start | bytes 786440 | tf_op jit(solution)/shard_map/ppermute | solution.py:360
  133.0 9.2 %collective-permute-done.27 = bf16[512,256]{1,0:T(8,128)(2,1)S(1)} collective-permute-done((bf16[512,256]{1,0:T(8,128)(2,1)S(1)}, bf16[512,256]{1,0:T(8,128)(2,1)S(1)}, u32[]{:S(2)}, u32[]{:S(2)}) %collective-permute-start.27) | collective-permute-done | bytes 262176 | tf_op jit(solution)/shard_map/ppermute | solution.py:360
  (116 shorter events, 33.0 us)
Async XLA Ops:
  2.0 18.2 %collective-permute-start.3 = (bf16[448,1024]{1,0:T(8,128)(2,1)S(1)}, bf16[448,1024]{1,0:T(8,128)(2,1)S(1)}, u32[]{:S(2)}, u32[]{:S(2)}) collective-permute-start(bf16[448,1024]{1,0:T(8,128)(2,1)S(1)} %slice.110.refs_0_.refs_4_), channel_id=1, source_target_pairs={{1,9},{3,11},{5,13},{7,15},{9,1},{11,3},{13,5},{15,7},{16,24},{18,... | collective-permute-start | bytes 2752520 | tf_op jit(solution)/shard_map/ppermute | solution.py:248
  2.7 32.6 %collective-permute-start.1 = (bf16[448,1024]{1,0:T(8,128)(2,1)S(1)}, bf16[448,1024]{1,0:T(8,128)(2,1)}, u32[]{:S(2)}, u32[]{:S(2)}) collective-permute-start(bf16[448,1024]{1,0:T(8,128)(2,1)S(1)} %slice.110.refs_0_.refs_4_), channel_id=1, source_target_pairs={{0,8},{2,10},{4,12},{6,14},{8,0},{10,2},{12,4},{14,6},{17,25},{19,... | collective-permute-start | bytes 2752520 | tf_op jit(solution)/shard_map/ppermute | solution.py:248
  6.3 7.7 %collective-permute-start.6 = (bf16[512,256]{1,0:T(8,128)(2,1)S(1)}, bf16[512,256]{1,0:T(8,128)(2,1)S(1)}, u32[]{:S(2)}, u32[]{:S(2)}) collective-permute-start(bf16[512,256]{1,0:T(8,128)(2,1)S(1)} %get-tuple-element.40), channel_id=1, source_target_pairs={{0,0},{1,4},{2,2},{3,6},{4,1},{5,5},{6,3},{7,7},{8,8},{9,12},{10,1... | collective-permute-start | bytes 786440 | tf_op jit(solution)/shard_map/ppermute | solution.py:232
  8.7 6.7 %collective-permute-start.7 = (bf16[512,256]{1,0:T(8,128)(2,1)S(1)}, bf16[512,256]{1,0:T(8,128)(2,1)S(1)}, u32[]{:S(2)}, u32[]{:S(2)}) collective-permute-start(bf16[512,256]{1,0:T(8,128)(2,1)S(1)} %get-tuple-element.39), channel_id=1, source_target_pairs={{0,1},{1,5},{2,3},{3,7},{4,0},{5,4},{6,2},{7,6},{8,9},{9,13},{10,1... | collective-permute-start | bytes 786440 | tf_op jit(solution)/shard_map/ppermute | solution.py:232
  15.5 19.3 %collective-permute-start.11 = (bf16[512,256]{1,0:T(8,128)(2,1)S(1)}, bf16[512,256]{1,0:T(8,128)(2,1)S(1)}, u32[]{:S(2)}, u32[]{:S(2)}) collective-permute-start(bf16[512,256]{1,0:T(8,128)(2,1)S(1)} %get-tuple-element.37), channel_id=1, source_target_pairs={{0,16},{8,24},{16,0},{24,8},{1,17},{9,25},{17,1},{25,9},{2,18},{10... | collective-permute-start | bytes 786440 | tf_op jit(solution)/shard_map/ppermute | solution.py:170
  18.5 38.8 %collective-permute-start = (bf16[448,1024]{1,0:T(8,128)(2,1)S(1)}, bf16[448,1024]{1,0:T(8,128)(2,1)S(1)}, u32[]{:S(2)}, u32[]{:S(2)}) collective-permute-start(bf16[448,1024]{1,0:T(8,128)(2,1)S(1)} %slice.110.refs_0_.refs_4_), channel_id=1, source_target_pairs={{0,1},{1,0},{2,3},{3,2},{4,5},{5,4},{6,7},{7,6},{8,9},{9,8},{10,11... | collective-permute-start | bytes 2752520 | tf_op jit(solution)/shard_map/ppermute | solution.py:167
  20.2 37.1 %collective-permute-start.4 = (bf16[448,1024]{1,0:T(8,128)(2,1)S(1)}, bf16[448,1024]{1,0:T(8,128)(2,1)}, u32[]{:S(2)}, u32[]{:S(2)}) collective-permute-start(bf16[448,1024]{1,0:T(8,128)(2,1)S(1)} %collective-permute-done.3.refs_6_.refs_2_), channel_id=1, source_target_pairs={{1,0},{3,2},{5,4},{7,6},{9,8},{11,10},{13,12},{15,14},{16,17},{18,... | collective-permute-start | bytes 2752520 | tf_op jit(solution)/shard_map/ppermute | solution.py:255
  21.5 11.8 %collective-permute-start.5 = (f32[1,514]{1,0:T(1,128)S(1)}, f32[1,514]{1,0:T(1,128)S(1)}, u32[]{:S(2)}, u32[]{:S(2)}) collective-permute-start(f32[1,514]{1,0:T(1,128)S(1)} %pad_maximum_fusion.7), channel_id=1, source_target_pairs={{0,1},{1,0},{2,3},{3,2},{4,5},{5,4},{6,7},{7,6},{8,9},{9,8},{10,11... | collective-permute-start | bytes 6176 | tf_op jit(solution)/shard_map/ppermute | solution.py:167
  33.3 8.3 %collective-permute-start.9 = (bf16[512,256]{1,0:T(8,128)(2,1)S(1)}, bf16[512,256]{1,0:T(8,128)(2,1)S(1)}, u32[]{:S(2)}, u32[]{:S(2)}) collective-permute-start(bf16[512,256]{1,0:T(8,128)(2,1)S(1)} %get-tuple-element.38.refs_4_), channel_id=1, source_target_pairs={{0,2},{1,3},{2,0},{3,1},{4,6},{5,7},{6,4},{7,5},{8,10},{9,11},{10,... | collective-permute-start | bytes 786440 | tf_op jit(solution)/shard_map/ppermute | solution.py:167
  34.8 8.2 %collective-permute-start.8 = (bf16[512,256]{1,0:T(8,128)(2,1)S(1)}, bf16[512,256]{1,0:T(8,128)(2,1)}, u32[]{:S(2)}, u32[]{:S(2)}) collective-permute-start(bf16[512,256]{1,0:T(8,128)(2,1)S(1)} %get-tuple-element.38.refs_4_), channel_id=1, source_target_pairs={{0,4},{1,5},{2,6},{3,7},{4,0},{5,1},{6,2},{7,3},{8,12},{9,13},{10,... | collective-permute-start | bytes 786440 | tf_op jit(solution)/shard_map/ppermute | solution.py:167
  35.3 39.4 %collective-permute-start.2 = (bf16[448,1024]{1,0:T(8,128)(2,1)}, bf16[448,1024]{1,0:T(8,128)(2,1)}, u32[]{:S(2)}, u32[]{:S(2)}) collective-permute-start(bf16[448,1024]{1,0:T(8,128)(2,1)} %collective-permute-done.1.refs_2_), channel_id=1, source_target_pairs={{0,1},{2,3},{4,5},{6,7},{8,9},{10,11},{12,13},{14,15},{17,16},{19,... | collective-permute-start | bytes 2752520 | tf_op jit(solution)/shard_map/ppermute | solution.py:255
  41.6 9.3 %collective-permute-start.12 = (bf16[512,256]{1,0:T(8,128)(2,1)S(1)}, bf16[512,256]{1,0:T(8,128)(2,1)}, u32[]{:S(2)}, u32[]{:S(2)}) collective-permute-start(bf16[512,256]{1,0:T(8,128)(2,1)S(1)} %collective-permute-done.11.refs_8_.refs_4_), channel_id=1, source_target_pairs={{0,4},{1,5},{2,6},{3,7},{4,0},{5,1},{6,2},{7,3},{8,12},{9,13},{10,... | collective-permute-start | bytes 786440 | tf_op jit(solution)/shard_map/ppermute | solution.py:167
  43.0 12.0 %collective-permute-start.10 = (bf16[512,256]{1,0:T(8,128)(2,1)S(1)}, bf16[512,256]{1,0:T(8,128)(2,1)}, u32[]{:S(2)}, u32[]{:S(2)}) collective-permute-start(bf16[512,256]{1,0:T(8,128)(2,1)S(1)} %collective-permute-done.9.refs_6_), channel_id=1, source_target_pairs={{0,4},{1,5},{2,6},{3,7},{4,0},{5,1},{6,2},{7,3},{8,12},{9,13},{10,... | collective-permute-start | bytes 786440 | tf_op jit(solution)/shard_map/ppermute | solution.py:167
  50.9 16.9 %collective-permute-start.13 = (bf16[512,256]{1,0:T(8,128)(2,1)S(1)}, bf16[512,256]{1,0:T(8,128)(2,1)}, u32[]{:S(2)}, u32[]{:S(2)}) collective-permute-start(bf16[512,256]{1,0:T(8,128)(2,1)S(1)} %collective-permute-done.11.refs_8_.refs_4_), channel_id=1, source_target_pairs={{0,2},{1,3},{2,0},{3,1},{4,6},{5,7},{6,4},{7,5},{8,10},{9,11},{10,... | collective-permute-start | bytes 786440 | tf_op jit(solution)/shard_map/ppermute | solution.py:167
  55.0 12.9 %collective-permute-start.14 = (bf16[512,256]{1,0:T(8,128)(2,1)}, bf16[512,256]{1,0:T(8,128)(2,1)}, u32[]{:S(2)}, u32[]{:S(2)}) collective-permute-start(bf16[512,256]{1,0:T(8,128)(2,1)} %collective-permute-done.12.refs_9_.refs_5_), channel_id=1, source_target_pairs={{0,2},{1,3},{2,0},{3,1},{4,6},{5,7},{6,4},{7,5},{8,10},{9,11},{10,... | collective-permute-start | bytes 786440 | tf_op jit(solution)/shard_map/ppermute | solution.py:167
  63.0 16.9 %collective-permute-start.16 = (f32[960]{0:T(1024)S(1)}, f32[960]{0:T(1024)S(1)}, u32[]{:S(2)}, u32[]{:S(2)}) collective-permute-start(f32[960]{0:T(1024)S(1)} %pad_maximum_fusion.4), channel_id=1, source_target_pairs={{0,16},{8,24},{16,0},{24,8},{1,17},{9,25},{17,1},{25,9},{2,18},{10... | collective-permute-start | bytes 11528 | tf_op jit(solution)/shard_map/ppermute | solution.py:170
  71.8 18.7 %collective-permute-start.15 = (bf16[448,256]{1,0:T(8,128)(2,1)}, bf16[448,256]{1,0:T(8,128)(2,1)S(1)}, u32[]{:S(2)}, u32[]{:S(2)}) collective-permute-start(bf16[448,256]{1,0:T(8,128)(2,1)} %get-tuple-element.12), channel_id=1, source_target_pairs={{0,16},{8,24},{16,0},{24,8},{1,17},{9,25},{17,1},{25,9},{2,18},{10... | collective-permute-start | bytes 688136 | tf_op jit(solution)/shard_map/ppermute | solution.py:170
  71.8 21.6 %collective-permute-start.17 = (bf16[448,256]{1,0:T(8,128)(2,1)S(1)}, bf16[448,256]{1,0:T(8,128)(2,1)S(1)}, u32[]{:S(2)}, u32[]{:S(2)}) collective-permute-start(bf16[448,256]{1,0:T(8,128)(2,1)S(1)} %copy-done.17), channel_id=1, source_target_pairs={{0,16},{8,24},{16,0},{24,8},{1,17},{9,25},{17,1},{25,9},{2,18},{10... | collective-permute-start | bytes 688136 | tf_op jit(solution)/shard_map/ppermute | solution.py:170
  95.0 6.5 %collective-permute-start.18 = (f32[2,448]{1,0:T(2,128)S(1)}, f32[2,448]{1,0:T(2,128)S(1)}, u32[]{:S(2)}, u32[]{:S(2)}) collective-permute-start(f32[2,448]{1,0:T(2,128)S(1)} %maximum_select_fusion.1), channel_id=1, source_target_pairs={{0,1},{1,0},{2,3},{3,2},{4,5},{5,4},{6,7},{7,6},{8,9},{9,8},{10,11... | collective-permute-start | bytes 10760 | tf_op jit(solution)/shard_map/ppermute | solution.py:167
  95.3 16.0 %collective-permute-start.22 = (bf16[448,256]{1,0:T(8,128)(2,1)}, bf16[448,256]{1,0:T(8,128)(2,1)S(1)}, u32[]{:S(2)}, u32[]{:S(2)}) collective-permute-start(bf16[448,256]{1,0:T(8,128)(2,1)} %get-tuple-element.19), channel_id=1, source_target_pairs={{0,16},{8,24},{16,0},{24,8},{1,17},{9,25},{17,1},{25,9},{2,18},{10... | collective-permute-start | bytes 688136 | tf_op jit(solution)/shard_map/ppermute | solution.py:170
  103.3 5.5 %collective-permute-start.21 = (f32[2,448]{1,0:T(2,128)S(1)}, f32[2,448]{1,0:T(2,128)S(1)}, u32[]{:S(2)}, u32[]{:S(2)}) collective-permute-start(f32[2,448]{1,0:T(2,128)S(1)} %fusion.77), channel_id=1, source_target_pairs={{0,24},{8,16},{16,8},{24,0},{1,25},{9,17},{17,9},{25,1},{2,26},{10... | collective-permute-start | bytes 10760 | tf_op jit(solution)/shard_map/ppermute | solution.py:170
  113.3 6.8 %collective-permute-start.23 = (bf16[1024,128]{1,0:T(8,128)(2,1)S(1)}, bf16[1024,128]{1,0:T(8,128)(2,1)S(1)}, u32[]{:S(2)}, u32[]{:S(2)}) collective-permute-start(bf16[1024,128]{1,0:T(8,128)(2,1)S(1)} %pad_maximum_fusion), channel_id=1, source_target_pairs={{0,4},{1,5},{2,6},{3,7},{4,0},{5,1},{6,2},{7,3},{8,12},{9,13},{10,... | collective-permute-start | bytes 786440 | tf_op jit(solution)/shard_map/ppermute | solution.py:167
  113.9 7.1 %collective-permute-start.25 = (bf16[1024,128]{1,0:T(8,128)(2,1)S(1)}, bf16[1024,128]{1,0:T(8,128)(2,1)S(1)}, u32[]{:S(2)}, u32[]{:S(2)}) collective-permute-start(bf16[1024,128]{1,0:T(8,128)(2,1)S(1)} %pad_maximum_fusion.1), channel_id=1, source_target_pairs={{0,2},{1,3},{2,0},{3,1},{4,6},{5,7},{6,4},{7,5},{8,10},{9,11},{10,... | collective-permute-start | bytes 786440 | tf_op jit(solution)/shard_map/ppermute | solution.py:167
  130.4 11.8 %collective-permute-start.27 = (bf16[512,256]{1,0:T(8,128)(2,1)S(1)}, bf16[512,256]{1,0:T(8,128)(2,1)S(1)}, u32[]{:S(2)}, u32[]{:S(2)}) collective-permute-start(bf16[512,256]{1,0:T(8,128)(2,1)S(1)} %pad_maximum_fusion.2), channel_id=1, source_target_pairs={{0,0},{1,16},{2,2},{3,18},{4,1},{5,17},{6,3},{7,19},{8,8},{9,24},{... | collective-permute-start | bytes 786440 | tf_op jit(solution)/shard_map/ppermute | solution.py:360
  (23 other events, 396.0 us)

commit v3 on v2

v3 whole, which is shorter than its diff:
```python
import jax
import jax.numpy as jnp
from jax import lax
from jax.experimental import pallas as pl
from jax.experimental.pallas import tpu as pltpu
from jax.sharding import PartitionSpec as P


KL_COEF = 0.1
DISCOUNT = 1.0
TRACE_DECAY = 0.95
NORM_EPS = 1e-05
FIRST_START = 64
GRANT = 16 * 1024 * 1024


def silu_slope(values):
    sigmoid = jax.nn.sigmoid(values)
    return sigmoid * (1.0 + values * (1.0 - sigmoid))


def advantage_of(log_prob, value_est, scores, ref_logprob, starts, ending, first):
    length = log_prob.shape[1]
    position = lax.broadcasted_iota(jnp.int32, (1, length), 1) + first
    inside = ((position >= starts) & (position < ending)).astype(jnp.float32)
    last_tok = (position == ending - 1).astype(jnp.float32)
    follow = (position + 1 < ending).astype(jnp.float32)
    reward = -KL_COEF * (log_prob - ref_logprob) * inside + scores * last_tok
    next_value = jnp.concatenate(
        [value_est[:, 1:], jnp.zeros((value_est.shape[0], 1), jnp.float32)], axis=1
    )
    deltas = (reward + DISCOUNT * next_value * follow - value_est) * inside
    source_pos = lax.broadcasted_iota(jnp.int32, (length, length), 0)
    target_pos = lax.broadcasted_iota(jnp.int32, (length, length), 1)
    spacing = source_pos - target_pos
    decays = jnp.where(
        spacing >= 0,
        jnp.power(jnp.float32(DISCOUNT * TRACE_DECAY), jnp.maximum(spacing, 0).astype(jnp.float32)),
        jnp.float32(0.0),
    )
    advantage = jnp.dot(deltas, decays, precision=lax.Precision.HIGHEST) * inside
    counts = (ending - starts).astype(jnp.float32)
    return advantage, -advantage / counts


WHOLE = pl.BlockSpec(memory_space=pltpu.VMEM)
FLAGS = pl.BlockSpec(memory_space=pltpu.SMEM)


def by_source(flag_ref, native, refs, run):
    own_ref, own_o_ref, mate_ref, mate_o_ref = refs
    own_near = flag_ref[1] == 1
    for is_native, own, mate in ((True, own_ref, mate_ref), (False, own_o_ref, mate_o_ref)):
        here = native if is_native else jnp.logical_not(native)
        pl.when(here & own_near)(lambda own=own, mate=mate: run(own, mate))
        pl.when(here & jnp.logical_not(own_near))(lambda own=own, mate=mate: run(mate, own))


def block_of(flag_ref, near, far, j, tokens):
    block = near.shape[1] // 2
    half = flag_ref[2] if j % 2 == 0 else 1 - flag_ref[2]
    source = far if j >= 2 else near
    return source[source.shape[0] - tokens :, pl.ds(pl.multiple_of(half * block, block), block)]


def products(flags, keep, sources, pieces, squares, head=None):
    tokens, _ = sources[0].shape
    half = pieces[0][0].shape[1]
    slabs = len(pieces)
    heads = [] if head is None else [head]
    at = -(-tokens // 128) * 128
    width = tokens if head is None else at + head.shape[1]

    def body(flag_ref, *refs):
        source_refs, refs = refs[:4], refs[4:]
        piece_refs, refs = refs[: 4 * slabs], refs[4 * slabs :]
        head_refs, refs = refs[: len(heads)], refs[len(heads) :]
        sent_ref, refs = refs[0], refs[1:]
        part_refs, sq_refs = refs[: slabs if keep else 0], refs[slabs if keep else 0 :]
        native = flag_ref[0] == (1 if keep else 0)

        def run(near, far):
            for s in range(slabs):
                total = None
                for j in range(4):
                    term = jnp.dot(
                        block_of(flag_ref, near, far, j, tokens),
                        piece_refs[4 * s + j][...],
                        preferred_element_type=jnp.float32,
                    )
                    total = term if total is None else total + term
                if keep:
                    part_refs[s][...] = total
                else:
                    sent_ref[...] = total.astype(jnp.bfloat16)
            if squares:
                sums = jnp.zeros((tokens, 128), jnp.float32)
                for j in range(4):
                    value = block_of(flag_ref, near, far, j, tokens).astype(jnp.float32)
                    value = value * value
                    for lane in range(0, value.shape[1], 128):
                        sums = sums + value[:, lane : lane + 128]
                sq_refs[0][:, :tokens] = jnp.sum(sums.T, axis=0, keepdims=True)

        by_source(flag_ref, native, source_refs, run)
        for head_ref in head_refs:
            sq_refs[0][:, at:] = head_ref[...].astype(jnp.float32)
        if keep:
            for s in range(slabs):
                @pl.when(flag_ref[3] == s)
                def _():
                    sent_ref[...] = part_refs[s][...].astype(jnp.bfloat16)

    shapes = [jax.ShapeDtypeStruct((tokens, half), jnp.bfloat16)]
    shapes += [jax.ShapeDtypeStruct((tokens, half), jnp.float32)] * (slabs if keep else 0)
    shapes += [jax.ShapeDtypeStruct((1, width), jnp.float32)] * squares
    return pl.pallas_call(
        body,
        in_specs=[FLAGS] + [WHOLE] * (4 + 4 * slabs + len(heads)),
        out_specs=[WHOLE] * len(shapes),
        out_shape=shapes,
        compiler_params=pltpu.CompilerParams(vmem_limit_bytes=GRANT),
        name="products",
    )(flags, *sources, *[p for group in pieces for p in group], *heads)


def turned(flags, keep, sources):
    tokens, feats = sources[0].shape
    block = feats // 2

    def body(flag_ref, *refs):
        source_refs, out_ref = refs[:4], refs[4]

        def run(near, far):
            for j in range(4):
                value = block_of(flag_ref, near, far, j, tokens)
                out_ref[j * block : (j + 1) * block, :] = value.T

        by_source(flag_ref, flag_ref[0] == (1 if keep else 0), source_refs, run)

    return pl.pallas_call(
        body,
        in_specs=[FLAGS] + [WHOLE] * 4,
        out_specs=WHOLE,
        out_shape=jax.ShapeDtypeStruct((2 * feats, tokens), sources[0].dtype),
        compiler_params=pltpu.CompilerParams(vmem_limit_bytes=GRANT),
        name="turned",
    )(flags, *sources)


def head_sums(flags, parts, gots, squares, message, head, feats):
    tokens, half = parts[0].shape
    at = message.shape[1] - head.shape[1]

    def body(flag_ref, own_ref, far_ref, got_own_ref, got_far_ref, sq_ref, message_ref, head_ref, pre_ref, sums_ref, actor_head_ref, scale_ref):
        scale = lax.rsqrt((sq_ref[...] + message_ref[:, :tokens]) / feats + NORM_EPS)
        scale_ref[...] = scale
        column = jnp.broadcast_to(scale, (128, tokens)).T
        start = pl.multiple_of(flag_ref[4] * half, half)
        head_own = head_ref[:, pl.ds(start, half)].astype(jnp.float32)
        head_far = message_ref[:, pl.ds(at + start, half)]

        def one(part_ref, got_ref, weights, store):
            total = None
            for lane in range(0, half, 128):
                value = part_ref[:, lane : lane + 128] + got_ref[:, lane : lane + 128].astype(jnp.float32)
                rounded = (value * column).astype(jnp.bfloat16)
                if store:
                    pre_ref[:, lane : lane + 128] = rounded
                value = rounded.astype(jnp.float32)
                term = weights[:, lane : lane + 128] * (value / (1.0 + jnp.exp(-value)))
                total = term if total is None else total + term
            return jnp.sum(total.T, axis=0, keepdims=True)

        def both(actor, other):
            actor_head_ref[...] = actor[2]
            sums_ref[0:1, :] = one(*actor, True)
            sums_ref[1:2, :] = one(*other, False)

        own = (own_ref, got_own_ref, head_own)
        far = (far_ref, got_far_ref, head_far)
        pl.when(flag_ref[3] == 0)(lambda: both(own, far))
        pl.when(flag_ref[3] != 0)(lambda: both(far, own))

    return pl.pallas_call(
        body,
        in_specs=[FLAGS] + [WHOLE] * 7,
        out_specs=[WHOLE] * 4,
        out_shape=[
            jax.ShapeDtypeStruct((tokens, half), jnp.bfloat16),
            jax.ShapeDtypeStruct((2, tokens), jnp.float32),
            jax.ShapeDtypeStruct((1, half), jnp.float32),
            jax.ShapeDtypeStruct((1, tokens), jnp.float32),
        ],
        compiler_params=pltpu.CompilerParams(vmem_limit_bytes=GRANT),
        name="head_sums",
    )(flags, *parts, *gots, squares, message, head)


def gradient(flags, turned, pre, sents, got, head, advantage, side, scale, message, far_squares, feats):
    tokens, half = pre.shape
    rows = turned[0].shape[0] // 4
    lanes = half // 2
    length = side.shape[1] - 2

    def body(flag_ref, keep_ref, send_ref, pre_ref, own_ref, far_ref, got_ref, head_ref, adv_ref, side_ref, scale_ref, message_ref, squares_ref, *out_refs):
        out_refs, slope_refs = out_refs[:-2], out_refs[-2:]
        counts = side_ref[:, length + 1 : length + 2] - side_ref[:, length : length + 1]
        signal = -adv_ref[...] / counts
        scale_send = lax.rsqrt((message_ref[:, :tokens] + squares_ref[2:3, :]) / feats + NORM_EPS)

        def column(row):
            return jnp.broadcast_to(row, (128, tokens)).T

        def slopes(value, coef, lane):
            sigmoid = 1.0 / (1.0 + jnp.exp(-value))
            slope = sigmoid * (1.0 + value * (1.0 - sigmoid))
            return (coef * head_ref[:, lane : lane + 128] * slope).astype(jnp.bfloat16)

        coef_keep = column(signal[0:1] * scale_ref[...])
        coef_send = column(signal[1:2] * scale_send)
        row_scale = column(scale_send)
        for lane in range(0, half, 128):
            value = pre_ref[:, lane : lane + 128].astype(jnp.float32)
            slope_refs[0][:, lane : lane + 128] = slopes(value, coef_keep, lane)

        def send_side(sent_ref):
            for lane in range(0, half, 128):
                value = sent_ref[:, lane : lane + 128].astype(jnp.float32)
                value = value + got_ref[:, lane : lane + 128].astype(jnp.float32)
                value = (value * row_scale).astype(jnp.bfloat16).astype(jnp.float32)
                slope_refs[1][:, lane : lane + 128] = slopes(value, coef_send, lane)

        pl.when(flag_ref[3] == 0)(lambda: send_side(own_ref))
        pl.when(flag_ref[3] != 0)(lambda: send_side(far_ref))
        for j in (3, 2, 1, 0):
            total = jnp.dot(
                keep_ref[j * rows : (j + 1) * rows, :], slope_refs[0][...], preferred_element_type=jnp.float32
            ) + jnp.dot(
                send_ref[j * rows : (j + 1) * rows, :], slope_refs[1][...], preferred_element_type=jnp.float32
            )
            for part in range(2):
                out_ref = out_refs[part * 4 + j]
                out_ref[...] = total[:, part * lanes : (part + 1) * lanes].astype(out_ref.dtype)

    shapes = [
        jax.ShapeDtypeStruct((rows, lanes), jnp.bfloat16 if j else jnp.float32)
        for _ in range(2)
        for j in range(4)
    ]
    outs = pl.pallas_call(
        body,
        in_specs=[FLAGS] + [WHOLE] * 12,
        out_specs=[WHOLE] * 8,
        out_shape=shapes,
        scratch_shapes=[pltpu.VMEM((tokens, half), jnp.bfloat16)] * 2,
        compiler_params=pltpu.CompilerParams(vmem_limit_bytes=GRANT),
        name="gradient",
    )(flags, *turned, pre, *sents, got, head, advantage, side, scale, message, far_squares)
    return outs[:4], outs[4:]


def solution(mesh):
    n_dev = mesh.shape["fsdp"]
    chips = n_dev // 2
    top = chips.bit_length() - 1

    def swap_fsdp(array, flip):
        return lax.ppermute(array, "fsdp", [(i, i ^ flip) for i in range(n_dev)])

    def swap_sec(array, flip):
        return lax.ppermute(array, "sec", [(i, i ^ flip) for i in range(4)])

    def split(f):
        return f >> top, (f & (chips - 1)) >> 1, f & 1

    def join(t, m, c):
        return (t << top) | (m << 1) | c

    def plane_route(slot):
        pairs = []
        for f in range(n_dev):
            t, m, r = split(f)
            pairs.append((f, join(r, m, t ^ slot)))
        return pairs

    def final_route():
        pairs = []
        for z in range(4):
            for f in range(n_dev):
                d, k = z >> 1, z & 1
                t, m, c = split(f)
                pairs.append((z * n_dev + f, (2 * c + k) * n_dev + d * chips + 2 * m + t))
        return pairs

    flip_of = [(n_dev // 2) * (j & 1) | (j & ~1) for j in range(chips)]

    def gather_pieces(own):
        return [own] + [swap_fsdp(own, flip_of[j]) for j in range(1, chips)]

    def scatter_sum(blocks):
        total = blocks[0]
        for j in range(1, chips):
            total = total + swap_fsdp(blocks[j].astype(jnp.bfloat16), flip_of[j]).astype(jnp.float32)
        return total

    def shards(hidden, window_proj, head_weights, ref_logprob, resp_spans):
      z = lax.axis_index("sec")
      f = lax.axis_index("fsdp")
      d, k = z // 2, z % 2
      t, m, c = f // chips, (f % chips) // 2, f % 2
      i0 = 2 * m + t
      weights = window_proj[0]
      rows, cols = weights.shape
      half = cols // 2
      length = ref_logprob.shape[1]
      first = FIRST_START
      kept = length - first

      def col_half(which, array):
          return jnp.where(which == 0, array[..., :half], array[..., half:])

      routed = []
      for j in range(2):
          routed.append(lax.ppermute(col_half(t ^ j, weights), "fsdp", plane_route(j)))
      stay = jnp.where(c == d, routed[0], routed[1])
      leave = jnp.where(c == d, routed[1], routed[0])
      came = swap_sec(leave, 2)
      w_own = gather_pieces(stay)
      w_far = gather_pieces(came)

      x_own = hidden[first:]
      swaps = {}
      for name, other in (("xsend", 1), ("xkeep", 0)):
          pairs = [
              (zz * n_dev + ff, (zz ^ 1) * n_dev + ff)
              for zz in range(4)
              for ff in range(n_dev)
              if (ff & 1) == (zz >> 1) ^ other
          ]
          swaps[name] = lax.ppermute(
              hidden if name == "xsend" else x_own, ("sec", "fsdp"), pairs
          )
          pairs = [
              (zz * n_dev + ff, zz * n_dev + (ff ^ 1))
              for zz in range(4)
              for ff in range(n_dev)
              if (ff & 1) == (zz >> 1) ^ other
          ]
          swaps[name + "core"] = lax.ppermute(swaps[name], ("sec", "fsdp"), pairs)
      x_own_o = swap_fsdp(x_own, 1)
      side = jnp.concatenate([ref_logprob, resp_spans.astype(jnp.float32)], axis=1)
      side_o = swap_fsdp(side, 1)
      side = jnp.where(c == d, jnp.concatenate([side, side_o]), jnp.concatenate([side_o, side]))
      ref_lp = side[:, first:length]
      starts = side[:, length : length + 1].astype(jnp.int32)
      ending = side[:, length + 1 :].astype(jnp.int32)

      local = chips == 4 and rows % 128 == 0
      feats = 2 * x_own.shape[1]
      send_sources = (x_own, x_own_o, swaps["xsend"], swaps["xsendcore"])
      keep_sources = (x_own, x_own_o, swaps["xkeep"], swaps["xkeepcore"])
      if local:
          flags = jnp.stack([(c == d).astype(jnp.int32), (m == k).astype(jnp.int32), t, d, c])
          sent_own, message = products(
              flags, False, send_sources, [w_own], True, head_weights
          )
          (sent_far,) = products(flags, False, send_sources, [w_far], False)
          sent_actor, keep_own, keep_far, sq_keep = products(
              flags, True, keep_sources, [w_own, w_far], True
          )
          turned_send = turned(flags, False, send_sources)
          turned_keep = turned(flags, True, keep_sources)
      else:
          def features_of(native, sources):
              sources = [source[-kept:] for source in sources]
              near, far = jnp.where(native, sources[0], sources[1]), jnp.where(native, sources[2], sources[3])
              whole = jnp.where(
                  k == 0,
                  jnp.concatenate([near, far], axis=1),
                  jnp.concatenate([far, near], axis=1),
              )
              whole = jnp.take(
                  whole.reshape(kept, chips, rows), i0 ^ jnp.arange(chips), axis=1
              ).reshape(kept, -1)
              wide = whole.astype(jnp.float32)
              return whole, jnp.sum(wide * wide, axis=1)[None]

          def product(x, pieces):
              return jnp.dot(x, jnp.concatenate(pieces, axis=0), preferred_element_type=jnp.float32)

          x_send, sq_send = features_of(c != d, send_sources)
          x_keep, sq_keep = features_of(c == d, keep_sources)
          sent_own, sent_far = [product(x_send, w).astype(jnp.bfloat16) for w in (w_own, w_far)]
          keep_own, keep_far = product(x_keep, w_own), product(x_keep, w_far)
          sent_actor = jnp.where(d == 0, keep_own, keep_far).astype(jnp.bfloat16)
          turned_send, turned_keep = x_send.T, x_keep.T
          gap = jnp.zeros((1, -kept % 128), jnp.float32)
          message = jnp.concatenate([sq_send, gap, head_weights.astype(jnp.float32)], axis=1)

      message_far = swap_sec(message, 2)
      at = message.shape[1] - cols
      got_far = swap_sec(sent_own, 2)
      got_own = swap_sec(sent_far, 2)
      got_actor = swap_sec(sent_actor, 2)

      def scale_of(sq):
          return lax.rsqrt(sq / (2 * feats) + NORM_EPS)

      def pre_of(part, got, row_scale):
          return (
              (part.astype(jnp.float32) + got.astype(jnp.float32)) * row_scale[:, None]
          ).astype(jnp.bfloat16)

      if local:
          pre_keep, sums, actor_head, scale_keep = head_sums(
              flags, (keep_own, keep_far), (got_own, got_far), sq_keep, message_far, head_weights, 2 * feats
          )
      else:
          scale_keep = scale_of(sq_keep[0] + message_far[0, :kept])
          head_own = col_half(c, head_weights[0].astype(jnp.float32))
          head_far = col_half(c, message_far[0, at:])
          pre_own = pre_of(keep_own, got_own, scale_keep)
          pre_far = pre_of(keep_far, got_far, scale_keep)
          pre_keep = jnp.where(d == 0, pre_own, pre_far)
          actor_head = jnp.where(d == 0, head_own, head_far)
          sum_own, sum_far = [
              jnp.sum(h * jax.nn.silu(v.astype(jnp.float32)), axis=1)
              for h, v in ((head_own, pre_own), (head_far, pre_far))
          ]
          sums = jnp.where(d == 0, jnp.stack([sum_own, sum_far]), jnp.stack([sum_far, sum_own]))
      sums = sums + swap_fsdp(sums, 1)
      others = [swap_sec(sums, 1), swap_sec(jnp.concatenate([sums, sq_keep]), 2), swap_sec(sums, 3)]
      log_prob = jnp.stack([sums[0] + others[0][0], others[1][0] + others[2][0]])
      same_k = jnp.stack([sums[1], others[1][1]])
      other_k = jnp.stack([others[0][1], others[2][1]])
      value_est = jnp.where(k == 0, same_k, other_k)
      scores = jnp.where(k == 0, other_k, same_k)
      advantage, signal = advantage_of(
          log_prob, value_est, scores, ref_lp, starts, ending, first
      )
      mine = jnp.where(c == d, advantage[0], advantage[1])
      advantage_out = jnp.concatenate([jnp.zeros((first,), jnp.float32), mine])[None]
      if local:
          blocks = gradient(
              flags, (turned_keep, turned_send), pre_keep, (sent_own, sent_far), got_actor,
              actor_head, advantage, side, scale_keep, message, others[1], 2 * feats,
          )
      else:
          scale_send = scale_of(message[0, :kept] + others[1][2])
          pre_send = pre_of(jnp.where(d == 0, sent_own, sent_far), got_actor, scale_send)

          def slopes_of(row_coef, values):
              return (
                  row_coef[:, None] * actor_head[None] * silu_slope(values.astype(jnp.float32))
              ).astype(jnp.bfloat16)

          grad = jnp.dot(
              turned_keep, slopes_of(signal[0] * scale_keep, pre_keep), preferred_element_type=jnp.float32
          ) + jnp.dot(
              turned_send, slopes_of(signal[1] * scale_send, pre_send), preferred_element_type=jnp.float32
          )
          grad = grad.reshape(chips, rows, half)
          blocks = (grad[..., : half // 2], grad[..., half // 2 :])
      placed = []
      for part in range(2):
          piece = scatter_sum(blocks[part]).astype(jnp.bfloat16)
          placed.append(lax.ppermute(piece, ("sec", "fsdp"), final_route()))
      out = jnp.concatenate(placed, axis=1)
      return (out.astype(jnp.float32)[None], advantage_out)

    return jax.shard_map(
        shards,
        mesh=mesh,
        in_specs=(
            P("fsdp", "sec"),
            P("sec", "fsdp", None),
            P("sec", None),
            P("fsdp", None),
            P("fsdp", None),
        ),
        out_specs=(P("sec", "fsdp", None), P("fsdp", None)),
        check_vma=False,
    )
```

time: 143 us -> 125 us (0.87)
  waiting for transfers between devices: 60.3 us -> 41.1 us
  other arithmetic: 8.51 us -> 3.07 us
  starting transfers between devices: 48.9 us -> 53.5 us
  local copies, waits for them, and re-layouts: 3.1 us -> 7.27 us
    ppermute x13 -> x15, waiting for transfers between devices: 27.2 us -> 15.4 us  [swap_fsdp(): return lax.ppermute(array, 'fsdp', [(i, i ^ flip) for i in range(n_dev)])]
    ppermute x8, starting transfers between devices: 15.2 us -> 24 us  [swap_sec(): return lax.ppermute(array, 'sec', [(i, i ^ flip) for i in range(4)])]
    ppermute x13 -> x15, starting transfers between devices: 21.4 us -> 13.9 us  [swap_fsdp(): return lax.ppermute(array, 'fsdp', [(i, i ^ flip) for i in range(n_dev)])]
    unnamed x38 -> x20, local copies, waits for them, and re-layouts: 0.99 us -> 5.22 us
    ppermute x2, waiting for transfers between devices: 6.62 us -> 3.49 us  [shards(): lax.ppermute(col_half(t ^ j, weights), 'fsdp', plane_route(j))]
    ppermute x3 -> x4, waiting for transfers between devices: 9.21 us -> 6.8 us  [the longest x2 6.79 us: shards(): placed.append(lax.ppermute(piece, ('sec', 'fsdp'), final_route()))]
    ppermute x3 -> x4, starting transfers between devices: 6.13 us -> 8.53 us  [the longest x2 4.35 us: shards(): lax.ppermute(hidden if name == 'xsend' else x_own, ('sec', 'fsdp'), pairs)]
    ppermute x8, waiting for transfers between devices: 17.3 us -> 15.4 us  [swap_sec(): return lax.ppermute(array, 'sec', [(i, i ^ flip) for i in range(4)])]
  transfers between devices with their start and end apart: 28 -> 31, of which waited for: 15 -> 14; matrix products, arithmetic and copies ran while one was open for 5% -> 4% of each run, Pallas kernels for 13% -> 10%
where the time goes in v3:
time: 125 us; the launch traced here: 124 us
  starting transfers between devices  53.5 us (43%)
  waiting for transfers between devices  41.1 us (33%)
  Pallas kernels  17.7 us (14%)
  local copies, waits for them, and re-layouts  7.27 us (6%)
  other arithmetic  3.07 us (2%)
    ppermute x8, starting transfers between devices, swap_sec(): return lax.ppermute(array, 'sec', [(i, i ^ flip) for i in range(4)])  24 us
    ppermute x8, waiting for transfers between devices, swap_sec(): return lax.ppermute(array, 'sec', [(i, i ^ flip) for i in range(4)])  15.4 us
    ppermute x15, waiting for transfers between devices, swap_fsdp(): return lax.ppermute(array, 'fsdp', [(i, i ^ flip) for i in range(n_dev)])  15.4 us
    ppermute x15, starting transfers between devices, swap_fsdp(): return lax.ppermute(array, 'fsdp', [(i, i ^ flip) for i in range(n_dev)])  13.9 us
    pallas_call x3, Pallas kernels, products(): pl.pallas_call(body, in_specs=[FLAGS] + [WHOLE] * (4 + 4 * slabs + len(he...  8.84 us
    ppermute x2, waiting for transfers between devices, shards(): placed.append(lax.ppermute(piece, ('sec', 'fsdp'), final_route()))  6.79 us
    unnamed x20, local copies, waits for them, and re-layouts  5.22 us
    ppermute x2, starting transfers between devices, shards(): lax.ppermute(hidden if name == 'xsend' else x_own, ('sec', 'fsdp'), pairs)  4.35 us
  transfers between devices with their start and end apart: 31, of which 14 were waited for; matrix products, arithmetic and copies ran while one was open for 4% of the time, Pallas kernels for 10%

profile of v3, /device:TPU:4, one launch (start us, length us, event | category | flops | bytes accessed | tf_op | source)
XLA Modules:
  0.0 124.2 jit_solution(13888621358160042691)
XLA Ops:
  2.8 3.5 %collective-permute-start.1 = (bf16[448,1024]{1,0:T(8,128)(2,1)S(1)}, bf16[448,1024]{1,0:T(8,128)(2,1)}, u32[]{:S(2)}, u32[]{:S(2)}) collective-permute-start(bf16[448,1024]{1,0:T(8,128)(2,1)S(1)} %slice.53.refs_0_), channel_id=1, source_target_pairs={{0,8},{2,10},{4,12},{6,14},{8,0},{10,2},{12,4},{14,6},{17,25},{19,... | collective-permute-start | bytes 2752520 | tf_op jit(solution)/shard_map/ppermute | solution.py:341
  7.6 3.1 %collective-permute-start.5 = (bf16[512,256]{1,0:T(8,128)(2,1)}, bf16[512,256]{1,0:T(8,128)(2,1)}, u32[]{:S(2)}, u32[]{:S(2)}) collective-permute-start(bf16[512,256]{1,0:T(8,128)(2,1)} %get-tuple-element.44), channel_id=1, source_target_pairs={{0,0},{1,4},{2,2},{3,6},{4,1},{5,5},{6,3},{7,7},{8,8},{9,12},{10,1... | collective-permute-start | bytes 786440 | tf_op jit(solution)/shard_map/ppermute | solution.py:325
  12.6 3.5 %collective-permute-done.5 = bf16[512,256]{1,0:T(8,128)(2,1)} collective-permute-done((bf16[512,256]{1,0:T(8,128)(2,1)}, bf16[512,256]{1,0:T(8,128)(2,1)}, u32[]{:S(2)}, u32[]{:S(2)}) %collective-permute-start.5) | collective-permute-done | bytes 262176 | tf_op jit(solution)/shard_map/ppermute | solution.py:325
  17.0 16.4 %collective-permute-start.10 = (bf16[512,256]{1,0:T(8,128)(2,1)S(1)}, bf16[512,256]{1,0:T(8,128)(2,1)}, u32[]{:S(2)}, u32[]{:S(2)}) collective-permute-start(bf16[512,256]{1,0:T(8,128)(2,1)S(1)} %get-tuple-element.41), channel_id=1, source_target_pairs={{0,16},{8,24},{16,0},{24,8},{1,17},{9,25},{17,1},{25,9},{2,18},{10... | collective-permute-start | bytes 786440 | tf_op jit(solution)/shard_map/ppermute | solution.py:272
  34.9 2.2 %collective-permute-start.2 = (bf16[448,1024]{1,0:T(8,128)(2,1)}, bf16[448,1024]{1,0:T(8,128)(2,1)}, u32[]{:S(2)}, u32[]{:S(2)}) collective-permute-start(bf16[448,1024]{1,0:T(8,128)(2,1)} %collective-permute-done.1.refs_2_), channel_id=1, source_target_pairs={{0,1},{2,3},{4,5},{6,7},{8,9},{10,11},{12,13},{14,15},{17,16},{19,... | collective-permute-start | bytes 2752520 | tf_op jit(solution)/shard_map/ppermute | solution.py:350
  37.1 6.2 %collective-permute-done.10.refs_8_.refs_4_ = bf16[512,256]{1,0:T(8,128)(2,1)} collective-permute-done((bf16[512,256]{1,0:T(8,128)(2,1)S(1)}, bf16[512,256]{1,0:T(8,128)(2,1)}, u32[]{:S(2)}, u32[]{:S(2)}) %collective-permute-start.10) | collective-permute-done | bytes 262176 | tf_op jit(solution)/shard_map/ppermute | solution.py:272
  45.3 5.2 %collective-permute-done.8.refs_6_ = bf16[512,256]{1,0:T(8,128)(2,1)S(1)} collective-permute-done((bf16[512,256]{1,0:T(8,128)(2,1)S(1)}, bf16[512,256]{1,0:T(8,128)(2,1)S(1)}, u32[]{:S(2)}, u32[]{:S(2)}) %collective-permute-start.8) | collective-permute-done | bytes 262176 | tf_op jit(solution)/shard_map/ppermute | solution.py:269
  57.4 2.8 %products.5 = (bf16[448,256]{1,0:T(8,128)(2,1)}, f32[1,1024]{1,0:T(1,128)S(1)}) custom-call(s32[5]{0:T(128)S(1)} %stack.42.flag_ref, bf16[448,1024]{1,0:T(8,128)(2,1)S(1)} %slice.53.refs_0_, bf16[448,1024]{1,0:T(8,128)(2,1)S(1)} %collective-permute-done.refs_1_, bf16[512,1024]{1,0:T(8,128)(2,1)S(1)} %collective-permute-done.3.refs_2_, ...), custom_call_target="tpu_custom_call" | custom-call | tf_op jit(solution)/shard_map/products/pallas_call | solution.py:117
  61.6 2.2 %collective-permute-done.12.refs_10_.refs_6_ = bf16[512,256]{1,0:T(8,128)(2,1)} collective-permute-done((bf16[512,256]{1,0:T(8,128)(2,1)}, bf16[512,256]{1,0:T(8,128)(2,1)}, u32[]{:S(2)}, u32[]{:S(2)}) %collective-permute-start.12) | collective-permute-done | bytes 262176 | tf_op jit(solution)/shard_map/ppermute | solution.py:269
  64.4 2.9 %products.4.far_ref = bf16[448,256]{1,0:T(8,128)(2,1)} custom-call(s32[5]{0:T(128)S(1)} %stack.42.flag_ref, bf16[448,1024]{1,0:T(8,128)(2,1)S(1)} %slice.53.refs_0_, bf16[448,1024]{1,0:T(8,128)(2,1)S(1)} %collective-permute-done.refs_1_, bf16[512,1024]{1,0:T(8,128)(2,1)S(1)} %collective-permute-done.3.refs_2_, ...), custom_call_target="tpu_custom_call" | custom-call | tf_op jit(solution)/shard_map/products/pallas_call | solution.py:117
  67.4 3.0 %collective-permute-start.16 = (f32[1,1024]{1,0:T(1,128)S(1)}, f32[1,1024]{1,0:T(1,128)S(1)}, u32[]{:S(2)}, u32[]{:S(2)}) collective-permute-start(f32[1,1024]{1,0:T(1,128)S(1)} %get-tuple-element.24.message_ref), channel_id=1, source_target_pairs={{0,16},{8,24},{16,0},{24,8},{1,17},{9,25},{17,1},{25,9},{2,18},{10... | collective-permute-start | bytes 12296 | tf_op jit(solution)/shard_map/ppermute | solution.py:272
  72.3 3.1 %products.3 = (bf16[448,256]{1,0:T(8,128)(2,1)S(1)}, f32[448,256]{1,0:T(8,128)S(1)}, f32[448,256]{1,0:T(8,128)S(1)}, f32[1,448]{1,0:T(1,128)S(1)}) custom-call(s32[5]{0:T(128)S(1)} %stack.42.flag_ref, bf16[448,1024]{1,0:T(8,128)(2,1)S(1)} %slice.53.refs_0_, bf16[448,1024]{1,0:T(8,128)(2,1)S(1)} %collective-permute-done.refs_1_, ...), custom_call_target="tpu_custom_call" | custom-call | tf_op jit(solution)/shard_map/products/pallas_call | solution.py:117
  75.4 4.7 %collective-permute-done.16.message_ref = f32[1,1024]{1,0:T(1,128)S(1)} collective-permute-done((f32[1,1024]{1,0:T(1,128)S(1)}, f32[1,1024]{1,0:T(1,128)S(1)}, u32[]{:S(2)}, u32[]{:S(2)}) %collective-permute-start.16) | collective-permute-done | bytes 4128 | tf_op jit(solution)/shard_map/ppermute | solution.py:272
  80.1 1.9 %head_sums.1 = (bf16[448,256]{1,0:T(8,128)(2,1)S(1)}, f32[2,448]{1,0:T(2,128)S(1)}, f32[1,256]{1,0:T(1,128)S(1)}, f32[1,448]{1,0:T(1,128)S(1)}) custom-call(s32[5]{0:T(128)S(1)} %stack.42.flag_ref, f32[448,256]{1,0:T(8,128)S(1)} %get-tuple-element.20.own_ref, f32[448,256]{1,0:T(8,128)S(1)} %get-tuple-element.21.far_ref, ...), custom_call_target="tpu_custom_call" | custom-call | tf_op jit(solution)/shard_map/head_sums/pallas_call | solution.py:185
  82.4 2.1 %turned.2.keep_ref = bf16[2048,448]{1,0:T(8,128)(2,1)S(1)} custom-call(s32[5]{0:T(128)S(1)} %stack.42.flag_ref, bf16[448,1024]{1,0:T(8,128)(2,1)S(1)} %slice.53.refs_0_, bf16[448,1024]{1,0:T(8,128)(2,1)S(1)} %collective-permute-done.refs_1_, bf16[448,1024]{1,0:T(8,128)(2,1)} %collective-permute-done.1.refs_2_, bf16[448,1024]{1,0:T(8,128)(2,1)} %collective-permute-done.2.refs_3_), custom_call_target="tpu_custom_call" | custom-call | tf_op jit(solution)/shard_map/turned/pallas_call | solution.py:141
  87.5 3.4 %collective-permute-start.22 = (f32[2,448]{1,0:T(2,128)S(1)}, f32[2,448]{1,0:T(2,128)S(1)}, u32[]{:S(2)}, u32[]{:S(2)}) collective-permute-start(f32[2,448]{1,0:T(2,128)S(1)} %add.86), channel_id=1, source_target_pairs={{0,24},{8,16},{16,8},{24,0},{1,25},{9,17},{17,9},{25,1},{2,26},{10... | collective-permute-start | bytes 10760 | tf_op jit(solution)/shard_map/ppermute | solution.py:272
  90.9 2.2 %collective-permute-done.22 = f32[2,448]{1,0:T(2,128)S(1)} collective-permute-done((f32[2,448]{1,0:T(2,128)S(1)}, f32[2,448]{1,0:T(2,128)S(1)}, u32[]{:S(2)}, u32[]{:S(2)}) %collective-permute-start.22) | collective-permute-done | bytes 3616 | tf_op jit(solution)/shard_map/ppermute | solution.py:272
  93.1 2.4 %collective-permute-done.21.squares_ref = f32[3,448]{1,0:T(4,128)S(1)} collective-permute-done((f32[3,448]{1,0:T(4,128)S(1)}, f32[3,448]{1,0:T(4,128)S(1)}, u32[]{:S(2)}, u32[]{:S(2)}) %collective-permute-start.21) | collective-permute-done | bytes 5408 | tf_op jit(solution)/shard_map/ppermute | solution.py:272
  96.1 3.0 %gradient.1 = (f32[512,128]{1,0:T(8,128)S(1)}, bf16[512,128]{1,0:T(8,128)(2,1)S(1)}, bf16[512,128]{1,0:T(8,128)(2,1)S(1)}, bf16[512,128]{1,0:T(8,128)(2,1)S(1)},...) custom-call(s32[5]{0:T(128)S(1)} %stack.42.flag_ref, ...), custom_call_target="tpu_custom_call" | custom-call | tf_op jit(solution)/shard_map/gradient/pallas_call | solution.py:251
  107.1 2.9 %collective-permute-done.25 = bf16[512,128]{1,0:T(8,128)(2,1)S(1)} collective-permute-done((bf16[512,128]{1,0:T(8,128)(2,1)S(1)}, bf16[512,128]{1,0:T(8,128)(2,1)S(1)}, u32[]{:S(2)}, u32[]{:S(2)}) %collective-permute-start.25) | collective-permute-done | bytes 131104 | tf_op jit(solution)/shard_map/ppermute | solution.py:269
  110.1 1.9 %collective-permute-start.26 = (bf16[512,128]{1,0:T(8,128)(2,1)S(1)}, bf16[512,128]{1,0:T(8,128)(2,1)S(1)}, u32[]{:S(2)}, u32[]{:S(2)}) collective-permute-start(bf16[512,128]{1,0:T(8,128)(2,1)S(1)} %add_convert_fusion.1), channel_id=1, source_target_pairs={{0,0},{1,16},{2,2},{3,18},{4,1},{5,17},{6,3},{7,19},{8,8},{9,24},{... | collective-permute-start | bytes 393224 | tf_op jit(solution)/shard_map/ppermute | solution.py:468
  113.6 2.3 %collective-permute-start.30 = (bf16[512,128]{1,0:T(8,128)(2,1)S(1)}, bf16[512,128]{1,0:T(8,128)(2,1)S(1)}, u32[]{:S(2)}, u32[]{:S(2)}) collective-permute-start(bf16[512,128]{1,0:T(8,128)(2,1)S(1)} %add_convert_fusion), channel_id=1, source_target_pairs={{0,0},{1,16},{2,2},{3,18},{4,1},{5,17},{6,3},{7,19},{8,8},{9,24},{... | collective-permute-start | bytes 393224 | tf_op jit(solution)/shard_map/ppermute | solution.py:468
  116.6 2.7 %collective-permute-done.26 = bf16[512,128]{1,0:T(8,128)(2,1)S(1)} collective-permute-done((bf16[512,128]{1,0:T(8,128)(2,1)S(1)}, bf16[512,128]{1,0:T(8,128)(2,1)S(1)}, u32[]{:S(2)}, u32[]{:S(2)}) %collective-permute-start.26) | collective-permute-done | bytes 131104 | tf_op jit(solution)/shard_map/ppermute | solution.py:468
  119.3 4.1 %collective-permute-done.30 = bf16[512,128]{1,0:T(8,128)(2,1)S(1)} collective-permute-done((bf16[512,128]{1,0:T(8,128)(2,1)S(1)}, bf16[512,128]{1,0:T(8,128)(2,1)S(1)}, u32[]{:S(2)}, u32[]{:S(2)}) %collective-permute-start.30) | collective-permute-done | bytes 131104 | tf_op jit(solution)/shard_map/ppermute | solution.py:468
  (86 shorter events, 35.6 us)
Async XLA Ops:
  0.7 10.6 %collective-permute-start.3 = (bf16[512,1024]{1,0:T(8,128)(2,1)}, bf16[512,1024]{1,0:T(8,128)(2,1)S(1)}, u32[]{:S(2)}, u32[]{:S(2)}) collective-permute-start(bf16[512,1024]{1,0:T(8,128)(2,1)} %param.5), channel_id=1, source_target_pairs={{1,9},{3,11},{5,13},{7,15},{9,1},{11,3},{13,5},{15,7},{16,24},{18,... | collective-permute-start | bytes 3145736 | tf_op jit(solution)/shard_map/ppermute | solution.py:341
  2.8 32.1 %collective-permute-start.1 = (bf16[448,1024]{1,0:T(8,128)(2,1)S(1)}, bf16[448,1024]{1,0:T(8,128)(2,1)}, u32[]{:S(2)}, u32[]{:S(2)}) collective-permute-start(bf16[448,1024]{1,0:T(8,128)(2,1)S(1)} %slice.53.refs_0_), channel_id=1, source_target_pairs={{0,8},{2,10},{4,12},{6,14},{8,0},{10,2},{12,4},{14,6},{17,25},{19,... | collective-permute-start | bytes 2752520 | tf_op jit(solution)/shard_map/ppermute | solution.py:341
  7.6 8.4 %collective-permute-start.5 = (bf16[512,256]{1,0:T(8,128)(2,1)}, bf16[512,256]{1,0:T(8,128)(2,1)}, u32[]{:S(2)}, u32[]{:S(2)}) collective-permute-start(bf16[512,256]{1,0:T(8,128)(2,1)} %get-tuple-element.44), channel_id=1, source_target_pairs={{0,0},{1,4},{2,2},{3,6},{4,1},{5,5},{6,3},{7,7},{8,8},{9,12},{10,1... | collective-permute-start | bytes 786440 | tf_op jit(solution)/shard_map/ppermute | solution.py:325
  10.8 43.4 %collective-permute-start = (bf16[448,1024]{1,0:T(8,128)(2,1)S(1)}, bf16[448,1024]{1,0:T(8,128)(2,1)S(1)}, u32[]{:S(2)}, u32[]{:S(2)}) collective-permute-start(bf16[448,1024]{1,0:T(8,128)(2,1)S(1)} %slice.53.refs_0_), channel_id=1, source_target_pairs={{0,1},{1,0},{2,3},{3,2},{4,5},{5,4},{6,7},{7,6},{8,9},{9,8},{10,11... | collective-permute-start | bytes 2752520 | tf_op jit(solution)/shard_map/ppermute | solution.py:269
  11.2 44.3 %collective-permute-start.4 = (bf16[512,1024]{1,0:T(8,128)(2,1)S(1)}, bf16[512,1024]{1,0:T(8,128)(2,1)}, u32[]{:S(2)}, u32[]{:S(2)}) collective-permute-start(bf16[512,1024]{1,0:T(8,128)(2,1)S(1)} %collective-permute-done.3.refs_2_), channel_id=1, source_target_pairs={{1,0},{3,2},{5,4},{7,6},{9,8},{11,10},{13,12},{15,14},{16,17},{18,... | collective-permute-start | bytes 3145736 | tf_op jit(solution)/shard_map/ppermute | solution.py:350
  17.0 26.2 %collective-permute-start.10 = (bf16[512,256]{1,0:T(8,128)(2,1)S(1)}, bf16[512,256]{1,0:T(8,128)(2,1)}, u32[]{:S(2)}, u32[]{:S(2)}) collective-permute-start(bf16[512,256]{1,0:T(8,128)(2,1)S(1)} %get-tuple-element.41), channel_id=1, source_target_pairs={{0,16},{8,24},{16,0},{24,8},{1,17},{9,25},{17,1},{25,9},{2,18},{10... | collective-permute-start | bytes 786440 | tf_op jit(solution)/shard_map/ppermute | solution.py:272
  33.5 11.3 %collective-permute-start.9 = (bf16[512,256]{1,0:T(8,128)(2,1)S(1)}, bf16[512,256]{1,0:T(8,128)(2,1)S(1)}, u32[]{:S(2)}, u32[]{:S(2)}) collective-permute-start(bf16[512,256]{1,0:T(8,128)(2,1)S(1)} %get-tuple-element.42.refs_4_), channel_id=1, source_target_pairs={{0,6},{1,7},{2,4},{3,5},{4,2},{5,3},{6,0},{7,1},{8,14},{9,15},{10,... | collective-permute-start | bytes 786440 | tf_op jit(solution)/shard_map/ppermute | solution.py:269
  34.9 35.5 %collective-permute-start.2 = (bf16[448,1024]{1,0:T(8,128)(2,1)}, bf16[448,1024]{1,0:T(8,128)(2,1)}, u32[]{:S(2)}, u32[]{:S(2)}) collective-permute-start(bf16[448,1024]{1,0:T(8,128)(2,1)} %collective-permute-done.1.refs_2_), channel_id=1, source_target_pairs={{0,1},{2,3},{4,5},{6,7},{8,9},{10,11},{12,13},{14,15},{17,16},{19,... | collective-permute-start | bytes 2752520 | tf_op jit(solution)/shard_map/ppermute | solution.py:350
  43.3 7.2 %collective-permute-start.8 = (bf16[512,256]{1,0:T(8,128)(2,1)S(1)}, bf16[512,256]{1,0:T(8,128)(2,1)S(1)}, u32[]{:S(2)}, u32[]{:S(2)}) collective-permute-start(bf16[512,256]{1,0:T(8,128)(2,1)S(1)} %get-tuple-element.42.refs_4_), channel_id=1, source_target_pairs={{0,2},{1,3},{2,0},{3,1},{4,6},{5,7},{6,4},{7,5},{8,10},{9,11},{10,... | collective-permute-start | bytes 786440 | tf_op jit(solution)/shard_map/ppermute | solution.py:269
  44.8 7.9 %collective-permute-start.7 = (bf16[512,256]{1,0:T(8,128)(2,1)S(1)}, bf16[512,256]{1,0:T(8,128)(2,1)S(1)}, u32[]{:S(2)}, u32[]{:S(2)}) collective-permute-start(bf16[512,256]{1,0:T(8,128)(2,1)S(1)} %get-tuple-element.42.refs_4_), channel_id=1, source_target_pairs={{0,4},{1,5},{2,6},{3,7},{4,0},{5,1},{6,2},{7,3},{8,12},{9,13},{10,... | collective-permute-start | bytes 786440 | tf_op jit(solution)/shard_map/ppermute | solution.py:269
  51.2 10.4 %collective-permute-start.13 = (bf16[512,256]{1,0:T(8,128)(2,1)}, bf16[512,256]{1,0:T(8,128)(2,1)}, u32[]{:S(2)}, u32[]{:S(2)}) collective-permute-start(bf16[512,256]{1,0:T(8,128)(2,1)} %collective-permute-done.10.refs_8_.refs_4_), channel_id=1, source_target_pairs={{0,6},{1,7},{2,4},{3,5},{4,2},{5,3},{6,0},{7,1},{8,14},{9,15},{10,... | collective-permute-start | bytes 786440 | tf_op jit(solution)/shard_map/ppermute | solution.py:269
  53.4 10.5 %collective-permute-start.12 = (bf16[512,256]{1,0:T(8,128)(2,1)}, bf16[512,256]{1,0:T(8,128)(2,1)}, u32[]{:S(2)}, u32[]{:S(2)}) collective-permute-start(bf16[512,256]{1,0:T(8,128)(2,1)} %collective-permute-done.10.refs_8_.refs_4_), channel_id=1, source_target_pairs={{0,2},{1,3},{2,0},{3,1},{4,6},{5,7},{6,4},{7,5},{8,10},{9,11},{10,... | collective-permute-start | bytes 786440 | tf_op jit(solution)/shard_map/ppermute | solution.py:269
  54.1 10.3 %collective-permute-start.11 = (bf16[512,256]{1,0:T(8,128)(2,1)}, bf16[512,256]{1,0:T(8,128)(2,1)}, u32[]{:S(2)}, u32[]{:S(2)}) collective-permute-start(bf16[512,256]{1,0:T(8,128)(2,1)} %collective-permute-done.10.refs_8_.refs_4_), channel_id=1, source_target_pairs={{0,4},{1,5},{2,6},{3,7},{4,0},{5,1},{6,2},{7,3},{8,12},{9,13},{10,... | collective-permute-start | bytes 786440 | tf_op jit(solution)/shard_map/ppermute | solution.py:269
  60.2 19.9 %collective-permute-start.15 = (bf16[448,256]{1,0:T(8,128)(2,1)}, bf16[448,256]{1,0:T(8,128)(2,1)}, u32[]{:S(2)}, u32[]{:S(2)}) collective-permute-start(bf16[448,256]{1,0:T(8,128)(2,1)} %get-tuple-element.22.own_ref), channel_id=1, source_target_pairs={{0,16},{8,24},{16,0},{24,8},{1,17},{9,25},{17,1},{25,9},{2,18},{10... | collective-permute-start | bytes 688136 | tf_op jit(solution)/shard_map/ppermute | solution.py:272
  67.3 12.9 %collective-permute-start.14 = (bf16[448,256]{1,0:T(8,128)(2,1)}, bf16[448,256]{1,0:T(8,128)(2,1)}, u32[]{:S(2)}, u32[]{:S(2)}) collective-permute-start(bf16[448,256]{1,0:T(8,128)(2,1)} %products.4.far_ref), channel_id=1, source_target_pairs={{0,16},{8,24},{16,0},{24,8},{1,17},{9,25},{17,1},{25,9},{2,18},{10... | collective-permute-start | bytes 688136 | tf_op jit(solution)/shard_map/ppermute | solution.py:272
  67.4 12.7 %collective-permute-start.16 = (f32[1,1024]{1,0:T(1,128)S(1)}, f32[1,1024]{1,0:T(1,128)S(1)}, u32[]{:S(2)}, u32[]{:S(2)}) collective-permute-start(f32[1,1024]{1,0:T(1,128)S(1)} %get-tuple-element.24.message_ref), channel_id=1, source_target_pairs={{0,16},{8,24},{16,0},{24,8},{1,17},{9,25},{17,1},{25,9},{2,18},{10... | collective-permute-start | bytes 12296 | tf_op jit(solution)/shard_map/ppermute | solution.py:272
  82.3 13.8 %collective-permute-start.17 = (bf16[448,256]{1,0:T(8,128)(2,1)S(1)}, bf16[448,256]{1,0:T(8,128)(2,1)S(1)}, u32[]{:S(2)}, u32[]{:S(2)}) collective-permute-start(bf16[448,256]{1,0:T(8,128)(2,1)S(1)} %get-tuple-element.26), channel_id=1, source_target_pairs={{0,16},{8,24},{16,0},{24,8},{1,17},{9,25},{17,1},{25,9},{2,18},{10... | collective-permute-start | bytes 688136 | tf_op jit(solution)/shard_map/ppermute | solution.py:272
  100.0 7.2 %collective-permute-start.24 = (bf16[512,128]{1,0:T(8,128)(2,1)S(1)}, bf16[512,128]{1,0:T(8,128)(2,1)S(1)}, u32[]{:S(2)}, u32[]{:S(2)}) collective-permute-start(bf16[512,128]{1,0:T(8,128)(2,1)S(1)} %get-tuple-element.32), channel_id=1, source_target_pairs={{0,2},{1,3},{2,0},{3,1},{4,6},{5,7},{6,4},{7,5},{8,10},{9,11},{10,... | collective-permute-start | bytes 393224 | tf_op jit(solution)/shard_map/ppermute | solution.py:269
  101.0 9.0 %collective-permute-start.25 = (bf16[512,128]{1,0:T(8,128)(2,1)S(1)}, bf16[512,128]{1,0:T(8,128)(2,1)S(1)}, u32[]{:S(2)}, u32[]{:S(2)}) collective-permute-start(bf16[512,128]{1,0:T(8,128)(2,1)S(1)} %get-tuple-element.33), channel_id=1, source_target_pairs={{0,6},{1,7},{2,4},{3,5},{4,2},{5,3},{6,0},{7,1},{8,14},{9,15},{10,... | collective-permute-start | bytes 393224 | tf_op jit(solution)/shard_map/ppermute | solution.py:269
  102.7 9.3 %collective-permute-start.27 = (bf16[512,128]{1,0:T(8,128)(2,1)S(1)}, bf16[512,128]{1,0:T(8,128)(2,1)S(1)}, u32[]{:S(2)}, u32[]{:S(2)}) collective-permute-start(bf16[512,128]{1,0:T(8,128)(2,1)S(1)} %get-tuple-element.35), channel_id=1, source_target_pairs={{0,4},{1,5},{2,6},{3,7},{4,0},{5,1},{6,2},{7,3},{8,12},{9,13},{10,... | collective-permute-start | bytes 393224 | tf_op jit(solution)/shard_map/ppermute | solution.py:269
  103.5 8.5 %collective-permute-start.28 = (bf16[512,128]{1,0:T(8,128)(2,1)S(1)}, bf16[512,128]{1,0:T(8,128)(2,1)S(1)}, u32[]{:S(2)}, u32[]{:S(2)}) collective-permute-start(bf16[512,128]{1,0:T(8,128)(2,1)S(1)} %get-tuple-element.36), channel_id=1, source_target_pairs={{0,2},{1,3},{2,0},{3,1},{4,6},{5,7},{6,4},{7,5},{8,10},{9,11},{10,... | collective-permute-start | bytes 393224 | tf_op jit(solution)/shard_map/ppermute | solution.py:269
  106.1 7.5 %collective-permute-start.29 = (bf16[512,128]{1,0:T(8,128)(2,1)S(1)}, bf16[512,128]{1,0:T(8,128)(2,1)S(1)}, u32[]{:S(2)}, u32[]{:S(2)}) collective-permute-start(bf16[512,128]{1,0:T(8,128)(2,1)S(1)} %get-tuple-element.37), channel_id=1, source_target_pairs={{0,6},{1,7},{2,4},{3,5},{4,2},{5,3},{6,0},{7,1},{8,14},{9,15},{10,... | collective-permute-start | bytes 393224 | tf_op jit(solution)/shard_map/ppermute | solution.py:269
  110.1 9.2 %collective-permute-start.26 = (bf16[512,128]{1,0:T(8,128)(2,1)S(1)}, bf16[512,128]{1,0:T(8,128)(2,1)S(1)}, u32[]{:S(2)}, u32[]{:S(2)}) collective-permute-start(bf16[512,128]{1,0:T(8,128)(2,1)S(1)} %add_convert_fusion.1), channel_id=1, source_target_pairs={{0,0},{1,16},{2,2},{3,18},{4,1},{5,17},{6,3},{7,19},{8,8},{9,24},{... | collective-permute-start | bytes 393224 | tf_op jit(solution)/shard_map/ppermute | solution.py:468
  113.6 9.7 %collective-permute-start.30 = (bf16[512,128]{1,0:T(8,128)(2,1)S(1)}, bf16[512,128]{1,0:T(8,128)(2,1)S(1)}, u32[]{:S(2)}, u32[]{:S(2)}) collective-permute-start(bf16[512,128]{1,0:T(8,128)(2,1)S(1)} %add_convert_fusion), channel_id=1, source_target_pairs={{0,0},{1,16},{2,2},{3,18},{4,1},{5,17},{6,3},{7,19},{8,8},{9,24},{... | collective-permute-start | bytes 393224 | tf_op jit(solution)/shard_map/ppermute | solution.py:468
  (17 other events, 162.0 us)

commit v4 on v3

--- a/solution.py
+++ b/solution.py
@@ -307,9 +307,13 @@
     def shards(hidden, window_proj, head_weights, ref_logprob, resp_spans):
       z = lax.axis_index("sec")
       f = lax.axis_index("fsdp")
-      d, k = z // 2, z % 2
-      t, m, c = f // chips, (f % chips) // 2, f % 2
+      d, k = z >> 1, z & 1
+      t, m, c = f >> top, (f & (chips - 1)) >> 1, f & 1
       i0 = 2 * m + t
+      flags = jnp.stack([1 - (c ^ d), (m == k).astype(jnp.int32), t, d, c])
+      flags, same, t_low, d_low, k_low, c_low, i0, hidden, window_proj = lax.optimization_barrier(
+          (flags, c == d, t == 0, d == 0, k == 0, c == 0, i0, hidden, window_proj)
+      )
       weights = window_proj[0]
       rows, cols = weights.shape
       half = cols // 2
@@ -317,14 +321,14 @@
       first = FIRST_START
       kept = length - first
 
-      def col_half(which, array):
-          return jnp.where(which == 0, array[..., :half], array[..., half:])
+      def col_half(low, array):
+          return jnp.where(low, array[..., :half], array[..., half:])
 
       routed = []
       for j in range(2):
-          routed.append(lax.ppermute(col_half(t ^ j, weights), "fsdp", plane_route(j)))
-      stay = jnp.where(c == d, routed[0], routed[1])
-      leave = jnp.where(c == d, routed[1], routed[0])
+          routed.append(lax.ppermute(col_half(t_low if j == 0 else ~t_low, weights), "fsdp", plane_route(j)))
+      stay = jnp.where(same, routed[0], routed[1])
+      leave = jnp.where(same, routed[1], routed[0])
       came = swap_sec(leave, 2)
       w_own = gather_pieces(stay)
       w_far = gather_pieces(came)
@@ -339,7 +343,7 @@
               if (ff & 1) == (zz >> 1) ^ other
           ]
           swaps[name] = lax.ppermute(
-              hidden if name == "xsend" else x_own, ("sec", "fsdp"), pairs
+              hidden, ("sec", "fsdp"), pairs
           )
           pairs = [
               (zz * n_dev + ff, zz * n_dev + (ff ^ 1))
@@ -351,7 +355,7 @@
       x_own_o = swap_fsdp(x_own, 1)
       side = jnp.concatenate([ref_logprob, resp_spans.astype(jnp.float32)], axis=1)
       side_o = swap_fsdp(side, 1)
-      side = jnp.where(c == d, jnp.concatenate([side, side_o]), jnp.concatenate([side_o, side]))
+      side = jnp.where(same, jnp.concatenate([side, side_o]), jnp.concatenate([side_o, side]))
       ref_lp = side[:, first:length]
       starts = side[:, length : length + 1].astype(jnp.int32)
       ending = side[:, length + 1 :].astype(jnp.int32)
@@ -361,7 +365,6 @@
       send_sources = (x_own, x_own_o, swaps["xsend"], swaps["xsendcore"])
       keep_sources = (x_own, x_own_o, swaps["xkeep"], swaps["xkeepcore"])
       if local:
-          flags = jnp.stack([(c == d).astype(jnp.int32), (m == k).astype(jnp.int32), t, d, c])
           sent_own, message = products(
               flags, False, send_sources, [w_own], True, head_weights
           )
@@ -376,7 +379,7 @@
               sources = [source[-kept:] for source in sources]
               near, far = jnp.where(native, sources[0], sources[1]), jnp.where(native, sources[2], sources[3])
               whole = jnp.where(
-                  k == 0,
+                  k_low,
                   jnp.concatenate([near, far], axis=1),
                   jnp.concatenate([far, near], axis=1),
               )
@@ -389,11 +392,11 @@
           def product(x, pieces):
               return jnp.dot(x, jnp.concatenate(pieces, axis=0), preferred_element_type=jnp.float32)
 
-          x_send, sq_send = features_of(c != d, send_sources)
-          x_keep, sq_keep = features_of(c == d, keep_sources)
+          x_send, sq_send = features_of(~same, send_sources)
+          x_keep, sq_keep = features_of(same, keep_sources)
           sent_own, sent_far = [product(x_send, w).astype(jnp.bfloat16) for w in (w_own, w_far)]
           keep_own, keep_far = product(x_keep, w_own), product(x_keep, w_far)
-          sent_actor = jnp.where(d == 0, keep_own, keep_far).astype(jnp.bfloat16)
+          sent_actor = jnp.where(d_low, keep_own, keep_far).astype(jnp.bfloat16)
           turned_send, turned_keep = x_send.T, x_keep.T
           gap = jnp.zeros((1, -kept % 128), jnp.float32)
           message = jnp.concatenate([sq_send, gap, head_weights.astype(jnp.float32)], axis=1)
@@ -418,28 +421,28 @@
           )
       else:
           scale_keep = scale_of(sq_keep[0] + message_far[0, :kept])
-          head_own = col_half(c, head_weights[0].astype(jnp.float32))
-          head_far = col_half(c, message_far[0, at:])
+          head_own = col_half(c_low, head_weights[0].astype(jnp.float32))
+          head_far = col_half(c_low, message_far[0, at:])
           pre_own = pre_of(keep_own, got_own, scale_keep)
           pre_far = pre_of(keep_far, got_far, scale_keep)
-          pre_keep = jnp.where(d == 0, pre_own, pre_far)
-          actor_head = jnp.where(d == 0, head_own, head_far)
+          pre_keep = jnp.where(d_low, pre_own, pre_far)
+          actor_head = jnp.where(d_low, head_own, head_far)
           sum_own, sum_far = [
               jnp.sum(h * jax.nn.silu(v.astype(jnp.float32)), axis=1)
               for h, v in ((head_own, pre_own), (head_far, pre_far))
           ]
-          sums = jnp.where(d == 0, jnp.stack([sum_own, sum_far]), jnp.stack([sum_far, sum_own]))
+          sums = jnp.where(d_low, jnp.stack([sum_own, sum_far]), jnp.stack([sum_far, sum_own]))
       sums = sums + swap_fsdp(sums, 1)
       others = [swap_sec(sums, 1), swap_sec(jnp.concatenate([sums, sq_keep]), 2), swap_sec(sums, 3)]
       log_prob = jnp.stack([sums[0] + others[0][0], others[1][0] + others[2][0]])
       same_k = jnp.stack([sums[1], others[1][1]])
       other_k = jnp.stack([others[0][1], others[2][1]])
-      value_est = jnp.where(k == 0, same_k, other_k)
-      scores = jnp.where(k == 0, other_k, same_k)
+      value_est = jnp.where(k_low, same_k, other_k)
+      scores = jnp.where(k_low, other_k, same_k)
       advantage, signal = advantage_of(
           log_prob, value_est, scores, ref_lp, starts, ending, first
       )
-      mine = jnp.where(c == d, advantage[0], advantage[1])
+      mine = jnp.where(same, advantage[0], advantage[1])
       advantage_out = jnp.concatenate([jnp.zeros((first,), jnp.float32), mine])[None]
       if local:
           blocks = gradient(
@@ -448,7 +451,7 @@
           )
       else:
           scale_send = scale_of(message[0, :kept] + others[1][2])
-          pre_send = pre_of(jnp.where(d == 0, sent_own, sent_far), got_actor, scale_send)
+          pre_send = pre_of(jnp.where(d_low, sent_own, sent_far), got_actor, scale_send)
 
           def slopes_of(row_coef, values):
               return (

time: 125 us -> 120 us (0.960)
  waiting for transfers between devices: 41.1 us -> 55.9 us
  Pallas kernels: 17.7 us -> 10.8 us
  starting transfers between devices: 53.5 us -> 47.4 us
  local copies, waits for them, and re-layouts: 7.27 us -> 2.06 us
    ppermute x4, waiting for transfers between devices: 3.5 us -> 12.6 us  [the longest x2 9.01 us: shards(): swaps[name] = lax.ppermute(hidden, ('sec', 'fsdp'), pairs)]
    ppermute x8, starting transfers between devices: 24 us -> 15.7 us  [swap_sec(): return lax.ppermute(array, 'sec', [(i, i ^ flip) for i in range(4)])]
    ppermute x8, waiting for transfers between devices: 15.4 us -> 21.5 us  [swap_sec(): return lax.ppermute(array, 'sec', [(i, i ^ flip) for i in range(4)])]
    unnamed x20 -> x6, local copies, waits for them, and re-layouts: 5.22 us -> 0.01 us
    pallas_call x3, Pallas kernels: 8.84 us -> 4.57 us  [products(): pl.pallas_call(body, in_specs=[FLAGS] + [WHOLE] * (4 + 4 * slabs + len(he...]
    ppermute x15, starting transfers between devices: 13.9 us -> 16.8 us  [swap_fsdp(): return lax.ppermute(array, 'fsdp', [(i, i ^ flip) for i in range(n_dev)])]
    ppermute x4, starting transfers between devices: 7.98 us -> 6.15 us  [the longest x2 4.2 us: shards(): swaps[name] = lax.ppermute(hidden, ('sec', 'fsdp'), pairs)]
    pallas_call x2, Pallas kernels: 3.95 us -> 2.34 us  [turned(): pl.pallas_call(body, in_specs=[FLAGS] + [WHOLE] * 4, out_specs=WHOLE, out...]
  transfers between devices with their start and end apart: 31 -> 31, of which waited for: 14 -> 17; matrix products, arithmetic and copies ran while one was open for 4% -> 3% of each run, Pallas kernels for 10% -> 6%
where the time goes in v4:
time: 120 us
  waiting for transfers between devices  55.9 us (47%)
  starting transfers between devices  47.4 us (40%)
  Pallas kernels  10.8 us (9%)
  other arithmetic  2.37 us (2%)
  local copies, waits for them, and re-layouts  2.06 us (2%)
    ppermute x8, waiting for transfers between devices, swap_sec(): return lax.ppermute(array, 'sec', [(i, i ^ flip) for i in range(4)])  21.5 us
    ppermute x15, starting transfers between devices, swap_fsdp(): return lax.ppermute(array, 'fsdp', [(i, i ^ flip) for i in range(n_dev)])  16.8 us
    ppermute x8, starting transfers between devices, swap_sec(): return lax.ppermute(array, 'sec', [(i, i ^ flip) for i in range(4)])  15.7 us
    ppermute x15, waiting for transfers between devices, swap_fsdp(): return lax.ppermute(array, 'fsdp', [(i, i ^ flip) for i in range(n_dev)])  15 us
    ppermute x2, waiting for transfers between devices, shards(): swaps[name] = lax.ppermute(hidden, ('sec', 'fsdp'), pairs)  9.01 us
    ppermute x2, waiting for transfers between devices, shards(): placed.append(lax.ppermute(piece, ('sec', 'fsdp'), final_route()))  6.75 us
    pallas_call x3, Pallas kernels, products(): pl.pallas_call(body, in_specs=[FLAGS] + [WHOLE] * (4 + 4 * slabs + len(he...  4.57 us
    ppermute x2, starting transfers between devices, shards(): placed.append(lax.ppermute(piece, ('sec', 'fsdp'), final_route()))  4.43 us
  transfers between devices with their start and end apart: 31, of which 17 were waited for; matrix products, arithmetic and copies ran while one was open for 3% of the time, Pallas kernels for 6%

profile of v4, /device:TPU:4, one launch (start us, length us, event | category | flops | bytes accessed | tf_op | source)
XLA Modules:
  0.0 120.0 jit_solution(11529027402212460523)
XLA Ops:
  1.5 3.5 %collective-permute-start.1 = (bf16[512,1024]{1,0:T(8,128)(2,1)}, bf16[512,1024]{1,0:T(8,128)(2,1)S(1)}, u32[]{:S(2)}, u32[]{:S(2)}) collective-permute-start(bf16[512,1024]{1,0:T(8,128)(2,1)} %param.5), channel_id=1, source_target_pairs={{0,8},{2,10},{4,12},{6,14},{8,0},{10,2},{12,4},{14,6},{17,25},{19,... | collective-permute-start | bytes 3145736 | tf_op jit(solution)/shard_map/ppermute | solution.py:345
  6.0 1.9 %collective-permute-start.5 = (bf16[512,256]{1,0:T(8,128)(2,1)S(1)}, bf16[512,256]{1,0:T(8,128)(2,1)S(1)}, u32[]{:S(2)}, u32[]{:S(2)}) collective-permute-start(bf16[512,256]{1,0:T(8,128)(2,1)S(1)} %get-tuple-element.56), channel_id=1, source_target_pairs={{0,0},{1,4},{2,2},{3,6},{4,1},{5,5},{6,3},{7,7},{8,8},{9,12},{10,1... | collective-permute-start | bytes 786440 | tf_op jit(solution)/shard_map/ppermute | solution.py:329
  11.1 2.6 %collective-permute-done.5 = bf16[512,256]{1,0:T(8,128)(2,1)S(1)} collective-permute-done((bf16[512,256]{1,0:T(8,128)(2,1)S(1)}, bf16[512,256]{1,0:T(8,128)(2,1)S(1)}, u32[]{:S(2)}, u32[]{:S(2)}) %collective-permute-start.5) | collective-permute-done | bytes 262176 | tf_op jit(solution)/shard_map/ppermute | solution.py:329
  14.7 2.5 %collective-permute-start.7 = (bf16[512,256]{1,0:T(8,128)(2,1)S(1)}, bf16[512,256]{1,0:T(8,128)(2,1)S(1)}, u32[]{:S(2)}, u32[]{:S(2)}) collective-permute-start(bf16[512,256]{1,0:T(8,128)(2,1)S(1)} %get-tuple-element.54.refs_4_), channel_id=1, source_target_pairs={{0,4},{1,5},{2,6},{3,7},{4,0},{5,1},{6,2},{7,3},{8,12},{9,13},{10,... | collective-permute-start | bytes 786440 | tf_op jit(solution)/shard_map/ppermute | solution.py:269
  18.7 9.0 %collective-permute-done.1.refs_2_ = bf16[512,1024]{1,0:T(8,128)(2,1)S(1)} collective-permute-done((bf16[512,1024]{1,0:T(8,128)(2,1)}, bf16[512,1024]{1,0:T(8,128)(2,1)S(1)}, u32[]{:S(2)}, u32[]{:S(2)}) %collective-permute-start.1) | collective-permute-done | bytes 1048608 | tf_op jit(solution)/shard_map/ppermute | solution.py:345
  27.7 3.1 %collective-permute-start.2 = (bf16[512,1024]{1,0:T(8,128)(2,1)S(1)}, bf16[512,1024]{1,0:T(8,128)(2,1)S(1)}, u32[]{:S(2)}, u32[]{:S(2)}) collective-permute-start(bf16[512,1024]{1,0:T(8,128)(2,1)S(1)} %collective-permute-done.1.refs_2_), channel_id=1, source_target_pairs={{0,1},{2,3},{4,5},{6,7},{8,9},{10,11},{12,13},{14,15},{17,16},{19,... | collective-permute-start | bytes 3145736 | tf_op jit(solution)/shard_map/ppermute | solution.py:354
  30.9 8.0 %collective-permute-start.10 = (bf16[512,256]{1,0:T(8,128)(2,1)S(1)}, bf16[512,256]{1,0:T(8,128)(2,1)S(1)}, u32[]{:S(2)}, u32[]{:S(2)}) collective-permute-start(bf16[512,256]{1,0:T(8,128)(2,1)S(1)} %get-tuple-element.53), channel_id=1, source_target_pairs={{0,16},{8,24},{16,0},{24,8},{1,17},{9,25},{17,1},{25,9},{2,18},{10... | collective-permute-start | bytes 786440 | tf_op jit(solution)/shard_map/ppermute | solution.py:272
  40.4 8.8 %collective-permute-done.10.refs_8_.refs_4_ = bf16[512,256]{1,0:T(8,128)(2,1)S(1)} collective-permute-done((bf16[512,256]{1,0:T(8,128)(2,1)S(1)}, bf16[512,256]{1,0:T(8,128)(2,1)S(1)}, u32[]{:S(2)}, u32[]{:S(2)}) %collective-permute-start.10) | collective-permute-done | bytes 262176 | tf_op jit(solution)/shard_map/ppermute | solution.py:272
  54.2 3.2 %collective-permute-done.11.refs_9_.refs_5_ = bf16[512,256]{1,0:T(8,128)(2,1)S(1)} collective-permute-done((bf16[512,256]{1,0:T(8,128)(2,1)S(1)}, bf16[512,256]{1,0:T(8,128)(2,1)S(1)}, u32[]{:S(2)}, u32[]{:S(2)}) %collective-permute-start.11) | collective-permute-done | bytes 262176 | tf_op jit(solution)/shard_map/ppermute | solution.py:269
  57.5 2.4 %collective-permute-done.12.refs_10_.refs_6_ = bf16[512,256]{1,0:T(8,128)(2,1)S(1)} collective-permute-done((bf16[512,256]{1,0:T(8,128)(2,1)S(1)}, bf16[512,256]{1,0:T(8,128)(2,1)S(1)}, u32[]{:S(2)}, u32[]{:S(2)}) %collective-permute-start.12) | collective-permute-done | bytes 262176 | tf_op jit(solution)/shard_map/ppermute | solution.py:269
  59.9 3.3 %collective-permute-done.13.refs_11_.refs_7_ = bf16[512,256]{1,0:T(8,128)(2,1)S(1)} collective-permute-done((bf16[512,256]{1,0:T(8,128)(2,1)S(1)}, bf16[512,256]{1,0:T(8,128)(2,1)S(1)}, u32[]{:S(2)}, u32[]{:S(2)}) %collective-permute-start.13) | collective-permute-done | bytes 262176 | tf_op jit(solution)/shard_map/ppermute | solution.py:269
  64.6 3.0 %collective-permute-start.16 = (f32[1,1024]{1,0:T(1,128)S(1)}, f32[1,1024]{1,0:T(1,128)S(1)}, u32[]{:S(2)}, u32[]{:S(2)}) collective-permute-start(f32[1,1024]{1,0:T(1,128)S(1)} %get-tuple-element.35.message_ref), channel_id=1, source_target_pairs={{0,16},{8,24},{16,0},{24,8},{1,17},{9,25},{17,1},{25,9},{2,18},{10... | collective-permute-start | bytes 12296 | tf_op jit(solution)/shard_map/ppermute | solution.py:272
  67.6 1.9 %products.3 = (bf16[448,256]{1,0:T(8,128)(2,1)S(1)}, f32[448,256]{1,0:T(8,128)S(1)}, f32[448,256]{1,0:T(8,128)S(1)}, f32[1,448]{1,0:T(1,128)S(1)}) custom-call(s32[5]{0:T(128)S(1)} %stack.38.flag_ref, bf16[448,1024]{1,0:T(8,128)(2,1)S(1)} %slice.53.refs_0_, bf16[448,1024]{1,0:T(8,128)(2,1)S(1)} %collective-permute-done.refs_1_, ...), custom_call_target="tpu_custom_call" | custom-call | tf_op jit(solution)/shard_map/products/pallas_call | solution.py:117
  69.6 6.8 %collective-permute-done.16.message_ref = f32[1,1024]{1,0:T(1,128)S(1)} collective-permute-done((f32[1,1024]{1,0:T(1,128)S(1)}, f32[1,1024]{1,0:T(1,128)S(1)}, u32[]{:S(2)}, u32[]{:S(2)}) %collective-permute-start.16) | collective-permute-done | bytes 4128 | tf_op jit(solution)/shard_map/ppermute | solution.py:272
  80.4 1.7 %collective-permute-start.20 = (f32[2,448]{1,0:T(2,128)S(1)}, f32[2,448]{1,0:T(2,128)S(1)}, u32[]{:S(2)}, u32[]{:S(2)}) collective-permute-start(f32[2,448]{1,0:T(2,128)S(1)} %add.71), channel_id=1, source_target_pairs={{0,8},{8,0},{16,24},{24,16},{1,9},{9,1},{17,25},{25,17},{2,10},{10... | collective-permute-start | bytes 10760 | tf_op jit(solution)/shard_map/ppermute | solution.py:272
  82.1 2.8 %collective-permute-start.22 = (f32[2,448]{1,0:T(2,128)S(1)}, f32[2,448]{1,0:T(2,128)S(1)}, u32[]{:S(2)}, u32[]{:S(2)}) collective-permute-start(f32[2,448]{1,0:T(2,128)S(1)} %add.71), channel_id=1, source_target_pairs={{0,24},{8,16},{16,8},{24,0},{1,25},{9,17},{17,9},{25,1},{2,26},{10... | collective-permute-start | bytes 10760 | tf_op jit(solution)/shard_map/ppermute | solution.py:272
  85.0 2.7 %collective-permute-done.22 = f32[2,448]{1,0:T(2,128)S(1)} collective-permute-done((f32[2,448]{1,0:T(2,128)S(1)}, f32[2,448]{1,0:T(2,128)S(1)}, u32[]{:S(2)}, u32[]{:S(2)}) %collective-permute-start.22) | collective-permute-done | bytes 3616 | tf_op jit(solution)/shard_map/ppermute | solution.py:272
  87.7 3.1 %collective-permute-done.21.squares_ref = f32[3,448]{1,0:T(4,128)S(1)} collective-permute-done((f32[3,448]{1,0:T(4,128)S(1)}, f32[3,448]{1,0:T(4,128)S(1)}, u32[]{:S(2)}, u32[]{:S(2)}) %collective-permute-start.21) | collective-permute-done | bytes 5408 | tf_op jit(solution)/shard_map/ppermute | solution.py:272
  91.5 2.5 %gradient.1 = (f32[512,128]{1,0:T(8,128)S(1)}, bf16[512,128]{1,0:T(8,128)(2,1)S(1)}, bf16[512,128]{1,0:T(8,128)(2,1)S(1)}, bf16[512,128]{1,0:T(8,128)(2,1)S(1)},...) custom-call(s32[5]{0:T(128)S(1)} %stack.38.flag_ref, ...), custom_call_target="tpu_custom_call" | custom-call | tf_op jit(solution)/shard_map/gradient/pallas_call | solution.py:251
  102.0 2.7 %collective-permute-done.25 = bf16[512,128]{1,0:T(8,128)(2,1)S(1)} collective-permute-done((bf16[512,128]{1,0:T(8,128)(2,1)S(1)}, bf16[512,128]{1,0:T(8,128)(2,1)S(1)}, u32[]{:S(2)}, u32[]{:S(2)}) %collective-permute-start.25) | collective-permute-done | bytes 131104 | tf_op jit(solution)/shard_map/ppermute | solution.py:269
  104.8 1.9 %collective-permute-start.26 = (bf16[512,128]{1,0:T(8,128)(2,1)S(1)}, bf16[512,128]{1,0:T(8,128)(2,1)S(1)}, u32[]{:S(2)}, u32[]{:S(2)}) collective-permute-start(bf16[512,128]{1,0:T(8,128)(2,1)S(1)} %add_convert_fusion.1), channel_id=1, source_target_pairs={{0,0},{1,16},{2,2},{3,18},{4,1},{5,17},{6,3},{7,19},{8,8},{9,24},{... | collective-permute-start | bytes 393224 | tf_op jit(solution)/shard_map/ppermute | solution.py:471
  109.3 2.5 %collective-permute-start.30 = (bf16[512,128]{1,0:T(8,128)(2,1)S(1)}, bf16[512,128]{1,0:T(8,128)(2,1)S(1)}, u32[]{:S(2)}, u32[]{:S(2)}) collective-permute-start(bf16[512,128]{1,0:T(8,128)(2,1)S(1)} %add_convert_fusion), channel_id=1, source_target_pairs={{0,0},{1,16},{2,2},{3,18},{4,1},{5,17},{6,3},{7,19},{8,8},{9,24},{... | collective-permute-start | bytes 393224 | tf_op jit(solution)/shard_map/ppermute | solution.py:471
  112.5 2.3 %collective-permute-done.26 = bf16[512,128]{1,0:T(8,128)(2,1)S(1)} collective-permute-done((bf16[512,128]{1,0:T(8,128)(2,1)S(1)}, bf16[512,128]{1,0:T(8,128)(2,1)S(1)}, u32[]{:S(2)}, u32[]{:S(2)}) %collective-permute-start.26) | collective-permute-done | bytes 131104 | tf_op jit(solution)/shard_map/ppermute | solution.py:471
  114.8 4.4 %collective-permute-done.30 = bf16[512,128]{1,0:T(8,128)(2,1)S(1)} collective-permute-done((bf16[512,128]{1,0:T(8,128)(2,1)S(1)}, bf16[512,128]{1,0:T(8,128)(2,1)S(1)}, u32[]{:S(2)}, u32[]{:S(2)}) %collective-permute-start.30) | collective-permute-done | bytes 131104 | tf_op jit(solution)/shard_map/ppermute | solution.py:471
  (72 shorter events, 32.0 us)
Async XLA Ops:
  0.8 9.1 %collective-permute-start.3 = (bf16[512,1024]{1,0:T(8,128)(2,1)}, bf16[512,1024]{1,0:T(8,128)(2,1)S(1)}, u32[]{:S(2)}, u32[]{:S(2)}) collective-permute-start(bf16[512,1024]{1,0:T(8,128)(2,1)} %param.5), channel_id=1, source_target_pairs={{1,9},{3,11},{5,13},{7,15},{9,1},{11,3},{13,5},{15,7},{16,24},{18,... | collective-permute-start | bytes 3145736 | tf_op jit(solution)/shard_map/ppermute | solution.py:345
  1.5 26.3 %collective-permute-start.1 = (bf16[512,1024]{1,0:T(8,128)(2,1)}, bf16[512,1024]{1,0:T(8,128)(2,1)S(1)}, u32[]{:S(2)}, u32[]{:S(2)}) collective-permute-start(bf16[512,1024]{1,0:T(8,128)(2,1)} %param.5), channel_id=1, source_target_pairs={{0,8},{2,10},{4,12},{6,14},{8,0},{10,2},{12,4},{14,6},{17,25},{19,... | collective-permute-start | bytes 3145736 | tf_op jit(solution)/shard_map/ppermute | solution.py:345
  6.0 7.7 %collective-permute-start.5 = (bf16[512,256]{1,0:T(8,128)(2,1)S(1)}, bf16[512,256]{1,0:T(8,128)(2,1)S(1)}, u32[]{:S(2)}, u32[]{:S(2)}) collective-permute-start(bf16[512,256]{1,0:T(8,128)(2,1)S(1)} %get-tuple-element.56), channel_id=1, source_target_pairs={{0,0},{1,4},{2,2},{3,6},{4,1},{5,5},{6,3},{7,7},{8,8},{9,12},{10,1... | collective-permute-start | bytes 786440 | tf_op jit(solution)/shard_map/ppermute | solution.py:329
  8.0 6.7 %collective-permute-start.6 = (bf16[512,256]{1,0:T(8,128)(2,1)S(1)}, bf16[512,256]{1,0:T(8,128)(2,1)S(1)}, u32[]{:S(2)}, u32[]{:S(2)}) collective-permute-start(bf16[512,256]{1,0:T(8,128)(2,1)S(1)} %get-tuple-element.55), channel_id=1, source_target_pairs={{0,1},{1,5},{2,3},{3,7},{4,0},{5,4},{6,2},{7,6},{8,9},{9,13},{10,1... | collective-permute-start | bytes 786440 | tf_op jit(solution)/shard_map/ppermute | solution.py:329
  9.3 42.0 %collective-permute-start = (bf16[448,1024]{1,0:T(8,128)(2,1)S(1)}, bf16[448,1024]{1,0:T(8,128)(2,1)S(1)}, u32[]{:S(2)}, u32[]{:S(2)}) collective-permute-start(bf16[448,1024]{1,0:T(8,128)(2,1)S(1)} %slice.53.refs_0_), channel_id=1, source_target_pairs={{0,1},{1,0},{2,3},{3,2},{4,5},{5,4},{6,7},{7,6},{8,9},{9,8},{10,11... | collective-permute-start | bytes 2752520 | tf_op jit(solution)/shard_map/ppermute | solution.py:269
  9.8 42.9 %collective-permute-start.4 = (bf16[512,1024]{1,0:T(8,128)(2,1)S(1)}, bf16[512,1024]{1,0:T(8,128)(2,1)S(1)}, u32[]{:S(2)}, u32[]{:S(2)}) collective-permute-start(bf16[512,1024]{1,0:T(8,128)(2,1)S(1)} %collective-permute-done.3.refs_2_), channel_id=1, source_target_pairs={{1,0},{3,2},{5,4},{7,6},{9,8},{11,10},{13,12},{15,14},{16,17},{18,... | collective-permute-start | bytes 3145736 | tf_op jit(solution)/shard_map/ppermute | solution.py:354
  14.7 16.2 %collective-permute-start.7 = (bf16[512,256]{1,0:T(8,128)(2,1)S(1)}, bf16[512,256]{1,0:T(8,128)(2,1)S(1)}, u32[]{:S(2)}, u32[]{:S(2)}) collective-permute-start(bf16[512,256]{1,0:T(8,128)(2,1)S(1)} %get-tuple-element.54.refs_4_), channel_id=1, source_target_pairs={{0,4},{1,5},{2,6},{3,7},{4,0},{5,1},{6,2},{7,3},{8,12},{9,13},{10,... | collective-permute-start | bytes 786440 | tf_op jit(solution)/shard_map/ppermute | solution.py:269
  17.2 21.7 %collective-permute-start.8 = (bf16[512,256]{1,0:T(8,128)(2,1)S(1)}, bf16[512,256]{1,0:T(8,128)(2,1)S(1)}, u32[]{:S(2)}, u32[]{:S(2)}) collective-permute-start(bf16[512,256]{1,0:T(8,128)(2,1)S(1)} %get-tuple-element.54.refs_4_), channel_id=1, source_target_pairs={{0,2},{1,3},{2,0},{3,1},{4,6},{5,7},{6,4},{7,5},{8,10},{9,11},{10,... | collective-permute-start | bytes 786440 | tf_op jit(solution)/shard_map/ppermute | solution.py:269
  27.7 39.9 %collective-permute-start.2 = (bf16[512,1024]{1,0:T(8,128)(2,1)S(1)}, bf16[512,1024]{1,0:T(8,128)(2,1)S(1)}, u32[]{:S(2)}, u32[]{:S(2)}) collective-permute-start(bf16[512,1024]{1,0:T(8,128)(2,1)S(1)} %collective-permute-done.1.refs_2_), channel_id=1, source_target_pairs={{0,1},{2,3},{4,5},{6,7},{8,9},{10,11},{12,13},{14,15},{17,16},{19,... | collective-permute-start | bytes 3145736 | tf_op jit(solution)/shard_map/ppermute | solution.py:354
  30.9 18.3 %collective-permute-start.10 = (bf16[512,256]{1,0:T(8,128)(2,1)S(1)}, bf16[512,256]{1,0:T(8,128)(2,1)S(1)}, u32[]{:S(2)}, u32[]{:S(2)}) collective-permute-start(bf16[512,256]{1,0:T(8,128)(2,1)S(1)} %get-tuple-element.53), channel_id=1, source_target_pairs={{0,16},{8,24},{16,0},{24,8},{1,17},{9,25},{17,1},{25,9},{2,18},{10... | collective-permute-start | bytes 786440 | tf_op jit(solution)/shard_map/ppermute | solution.py:272
  38.9 11.8 %collective-permute-start.9 = (bf16[512,256]{1,0:T(8,128)(2,1)S(1)}, bf16[512,256]{1,0:T(8,128)(2,1)S(1)}, u32[]{:S(2)}, u32[]{:S(2)}) collective-permute-start(bf16[512,256]{1,0:T(8,128)(2,1)S(1)} %get-tuple-element.54.refs_4_), channel_id=1, source_target_pairs={{0,6},{1,7},{2,4},{3,5},{4,2},{5,3},{6,0},{7,1},{8,14},{9,15},{10,... | collective-permute-start | bytes 786440 | tf_op jit(solution)/shard_map/ppermute | solution.py:269
  49.2 8.3 %collective-permute-start.11 = (bf16[512,256]{1,0:T(8,128)(2,1)S(1)}, bf16[512,256]{1,0:T(8,128)(2,1)S(1)}, u32[]{:S(2)}, u32[]{:S(2)}) collective-permute-start(bf16[512,256]{1,0:T(8,128)(2,1)S(1)} %collective-permute-done.10.refs_8_.refs_4_), channel_id=1, source_target_pairs={{0,4},{1,5},{2,6},{3,7},{4,0},{5,1},{6,2},{7,3},{8,12},{9,13},{10,... | collective-permute-start | bytes 786440 | tf_op jit(solution)/shard_map/ppermute | solution.py:269
  50.7 9.2 %collective-permute-start.12 = (bf16[512,256]{1,0:T(8,128)(2,1)S(1)}, bf16[512,256]{1,0:T(8,128)(2,1)S(1)}, u32[]{:S(2)}, u32[]{:S(2)}) collective-permute-start(bf16[512,256]{1,0:T(8,128)(2,1)S(1)} %collective-permute-done.10.refs_8_.refs_4_), channel_id=1, source_target_pairs={{0,2},{1,3},{2,0},{3,1},{4,6},{5,7},{6,4},{7,5},{8,10},{9,11},{10,... | collective-permute-start | bytes 786440 | tf_op jit(solution)/shard_map/ppermute | solution.py:269
  51.3 12.0 %collective-permute-start.13 = (bf16[512,256]{1,0:T(8,128)(2,1)S(1)}, bf16[512,256]{1,0:T(8,128)(2,1)S(1)}, u32[]{:S(2)}, u32[]{:S(2)}) collective-permute-start(bf16[512,256]{1,0:T(8,128)(2,1)S(1)} %collective-permute-done.10.refs_8_.refs_4_), channel_id=1, source_target_pairs={{0,6},{1,7},{2,4},{3,5},{4,2},{5,3},{6,0},{7,1},{8,14},{9,15},{10,... | collective-permute-start | bytes 786440 | tf_op jit(solution)/shard_map/ppermute | solution.py:269
  54.2 22.2 %collective-permute-start.15 = (bf16[448,256]{1,0:T(8,128)(2,1)S(1)}, bf16[448,256]{1,0:T(8,128)(2,1)S(1)}, u32[]{:S(2)}, u32[]{:S(2)}) collective-permute-start(bf16[448,256]{1,0:T(8,128)(2,1)S(1)} %get-tuple-element.33.own_ref), channel_id=1, source_target_pairs={{0,16},{8,24},{16,0},{24,8},{1,17},{9,25},{17,1},{25,9},{2,18},{10... | collective-permute-start | bytes 688136 | tf_op jit(solution)/shard_map/ppermute | solution.py:272
  64.4 11.9 %collective-permute-start.14 = (bf16[448,256]{1,0:T(8,128)(2,1)S(1)}, bf16[448,256]{1,0:T(8,128)(2,1)S(1)}, u32[]{:S(2)}, u32[]{:S(2)}) collective-permute-start(bf16[448,256]{1,0:T(8,128)(2,1)S(1)} %products.4.far_ref), channel_id=1, source_target_pairs={{0,16},{8,24},{16,0},{24,8},{1,17},{9,25},{17,1},{25,9},{2,18},{10... | collective-permute-start | bytes 688136 | tf_op jit(solution)/shard_map/ppermute | solution.py:272
  64.6 11.7 %collective-permute-start.16 = (f32[1,1024]{1,0:T(1,128)S(1)}, f32[1,1024]{1,0:T(1,128)S(1)}, u32[]{:S(2)}, u32[]{:S(2)}) collective-permute-start(f32[1,1024]{1,0:T(1,128)S(1)} %get-tuple-element.35.message_ref), channel_id=1, source_target_pairs={{0,16},{8,24},{16,0},{24,8},{1,17},{9,25},{17,1},{25,9},{2,18},{10... | collective-permute-start | bytes 12296 | tf_op jit(solution)/shard_map/ppermute | solution.py:272
  78.0 13.5 %collective-permute-start.17 = (bf16[448,256]{1,0:T(8,128)(2,1)S(1)}, bf16[448,256]{1,0:T(8,128)(2,1)S(1)}, u32[]{:S(2)}, u32[]{:S(2)}) collective-permute-start(bf16[448,256]{1,0:T(8,128)(2,1)S(1)} %get-tuple-element.37), channel_id=1, source_target_pairs={{0,16},{8,24},{16,0},{24,8},{1,17},{9,25},{17,1},{25,9},{2,18},{10... | collective-permute-start | bytes 688136 | tf_op jit(solution)/shard_map/ppermute | solution.py:272
  96.2 8.6 %collective-permute-start.25 = (bf16[512,128]{1,0:T(8,128)(2,1)S(1)}, bf16[512,128]{1,0:T(8,128)(2,1)S(1)}, u32[]{:S(2)}, u32[]{:S(2)}) collective-permute-start(bf16[512,128]{1,0:T(8,128)(2,1)S(1)} %get-tuple-element.45), channel_id=1, source_target_pairs={{0,6},{1,7},{2,4},{3,5},{4,2},{5,3},{6,0},{7,1},{8,14},{9,15},{10,... | collective-permute-start | bytes 393224 | tf_op jit(solution)/shard_map/ppermute | solution.py:269
  97.6 9.2 %collective-permute-start.27 = (bf16[512,128]{1,0:T(8,128)(2,1)S(1)}, bf16[512,128]{1,0:T(8,128)(2,1)S(1)}, u32[]{:S(2)}, u32[]{:S(2)}) collective-permute-start(bf16[512,128]{1,0:T(8,128)(2,1)S(1)} %get-tuple-element.47), channel_id=1, source_target_pairs={{0,4},{1,5},{2,6},{3,7},{4,0},{5,1},{6,2},{7,3},{8,12},{9,13},{10,... | collective-permute-start | bytes 393224 | tf_op jit(solution)/shard_map/ppermute | solution.py:269
  99.1 8.5 %collective-permute-start.28 = (bf16[512,128]{1,0:T(8,128)(2,1)S(1)}, bf16[512,128]{1,0:T(8,128)(2,1)S(1)}, u32[]{:S(2)}, u32[]{:S(2)}) collective-permute-start(bf16[512,128]{1,0:T(8,128)(2,1)S(1)} %get-tuple-element.48), channel_id=1, source_target_pairs={{0,2},{1,3},{2,0},{3,1},{4,6},{5,7},{6,4},{7,5},{8,10},{9,11},{10,... | collective-permute-start | bytes 393224 | tf_op jit(solution)/shard_map/ppermute | solution.py:269
  99.9 9.3 %collective-permute-start.29 = (bf16[512,128]{1,0:T(8,128)(2,1)S(1)}, bf16[512,128]{1,0:T(8,128)(2,1)S(1)}, u32[]{:S(2)}, u32[]{:S(2)}) collective-permute-start(bf16[512,128]{1,0:T(8,128)(2,1)S(1)} %get-tuple-element.49), channel_id=1, source_target_pairs={{0,6},{1,7},{2,4},{3,5},{4,2},{5,3},{6,0},{7,1},{8,14},{9,15},{10,... | collective-permute-start | bytes 393224 | tf_op jit(solution)/shard_map/ppermute | solution.py:269
  104.8 9.9 %collective-permute-start.26 = (bf16[512,128]{1,0:T(8,128)(2,1)S(1)}, bf16[512,128]{1,0:T(8,128)(2,1)S(1)}, u32[]{:S(2)}, u32[]{:S(2)}) collective-permute-start(bf16[512,128]{1,0:T(8,128)(2,1)S(1)} %add_convert_fusion.1), channel_id=1, source_target_pairs={{0,0},{1,16},{2,2},{3,18},{4,1},{5,17},{6,3},{7,19},{8,8},{9,24},{... | collective-permute-start | bytes 393224 | tf_op jit(solution)/shard_map/ppermute | solution.py:471
  109.3 9.9 %collective-permute-start.30 = (bf16[512,128]{1,0:T(8,128)(2,1)S(1)}, bf16[512,128]{1,0:T(8,128)(2,1)S(1)}, u32[]{:S(2)}, u32[]{:S(2)}) collective-permute-start(bf16[512,128]{1,0:T(8,128)(2,1)S(1)} %add_convert_fusion), channel_id=1, source_target_pairs={{0,0},{1,16},{2,2},{3,18},{4,1},{5,17},{6,3},{7,19},{8,8},{9,24},{... | collective-permute-start | bytes 393224 | tf_op jit(solution)/shard_map/ppermute | solution.py:471
  (10 other events, 148.5 us)

commit v5 on v4

--- a/solution.py
+++ b/solution.py
@@ -197,13 +197,24 @@
     )(flags, *parts, *gots, squares, message, head)
 
 
-def gradient(flags, turned, pre, sents, got, head, advantage, side, scale, message, far_squares, feats):
-    tokens, half = pre.shape
+def gradient(flags, turned, raw, sents, got, head, advantage, side, scale, message, far_squares, feats):
+    tokens, half = raw.shape
     rows = turned[0].shape[0] // 4
     lanes = half // 2
     length = side.shape[1] - 2
 
-    def body(flag_ref, keep_ref, send_ref, pre_ref, own_ref, far_ref, got_ref, head_ref, adv_ref, side_ref, scale_ref, message_ref, squares_ref, *out_refs):
+    def block_products(keep_ref, send_ref, slope_keep_ref, slope_send_ref, out_refs, blocks):
+        for at, j in enumerate(blocks):
+            total = jnp.dot(
+                keep_ref[j * rows : (j + 1) * rows, :], slope_keep_ref[...], preferred_element_type=jnp.float32
+            ) + jnp.dot(
+                send_ref[j * rows : (j + 1) * rows, :], slope_send_ref[...], preferred_element_type=jnp.float32
+            )
+            for part in range(2):
+                out_ref = out_refs[2 * at + part]
+                out_ref[...] = total[:, part * lanes : (part + 1) * lanes].astype(out_ref.dtype)
+
+    def body(flag_ref, keep_ref, send_ref, raw_ref, own_ref, far_ref, got_ref, head_ref, adv_ref, side_ref, scale_ref, message_ref, squares_ref, *out_refs):
         out_refs, slope_refs = out_refs[:-2], out_refs[-2:]
         counts = side_ref[:, length + 1 : length + 2] - side_ref[:, length : length + 1]
         signal = -adv_ref[...] / counts
@@ -221,8 +232,8 @@
         coef_send = column(signal[1:2] * scale_send)
         row_scale = column(scale_send)
         for lane in range(0, half, 128):
-            value = pre_ref[:, lane : lane + 128].astype(jnp.float32)
-            slope_refs[0][:, lane : lane + 128] = slopes(value, coef_keep, lane)
+            value = raw_ref[:, lane : lane + 128]
+            slope_refs[0][:, lane : lane + 128] = (coef_keep * value).astype(jnp.bfloat16)
 
         def send_side(sent_ref):
             for lane in range(0, half, 128):
@@ -233,31 +244,30 @@
 
         pl.when(flag_ref[3] == 0)(lambda: send_side(own_ref))
         pl.when(flag_ref[3] != 0)(lambda: send_side(far_ref))
-        for j in (3, 2, 1, 0):
-            total = jnp.dot(
-                keep_ref[j * rows : (j + 1) * rows, :], slope_refs[0][...], preferred_element_type=jnp.float32
-            ) + jnp.dot(
-                send_ref[j * rows : (j + 1) * rows, :], slope_refs[1][...], preferred_element_type=jnp.float32
-            )
-            for part in range(2):
-                out_ref = out_refs[part * 4 + j]
-                out_ref[...] = total[:, part * lanes : (part + 1) * lanes].astype(out_ref.dtype)
-
-    shapes = [
-        jax.ShapeDtypeStruct((rows, lanes), jnp.bfloat16 if j else jnp.float32)
-        for _ in range(2)
-        for j in range(4)
-    ]
-    outs = pl.pallas_call(
+        block_products(keep_ref, send_ref, slope_refs[0], slope_refs[1], out_refs, (3, 2))
+
+    far = pl.pallas_call(
         body,
         in_specs=[FLAGS] + [WHOLE] * 12,
-        out_specs=[WHOLE] * 8,
-        out_shape=shapes,
-        scratch_shapes=[pltpu.VMEM((tokens, half), jnp.bfloat16)] * 2,
+        out_specs=[WHOLE] * 6,
+        out_shape=[jax.ShapeDtypeStruct((rows, lanes), jnp.bfloat16)] * 4
+        + [jax.ShapeDtypeStruct((tokens, half), jnp.bfloat16)] * 2,
         compiler_params=pltpu.CompilerParams(vmem_limit_bytes=GRANT),
         name="gradient",
-    )(flags, *turned, pre, *sents, got, head, advantage, side, scale, message, far_squares)
-    return outs[:4], outs[4:]
+    )(flags, *turned, raw, *sents, got, head, advantage, side, scale, message, far_squares)
+
+    def near_body(keep_ref, send_ref, slope_keep_ref, slope_send_ref, *out_refs):
+        block_products(keep_ref, send_ref, slope_keep_ref, slope_send_ref, out_refs, (1, 0))
+
+    near = pl.pallas_call(
+        near_body,
+        in_specs=[WHOLE] * 4,
+        out_specs=[WHOLE] * 4,
+        out_shape=[jax.ShapeDtypeStruct((rows, lanes), kind) for kind in (jnp.bfloat16, jnp.float32) for _ in range(2)],
+        compiler_params=pltpu.CompilerParams(vmem_limit_bytes=GRANT),
+        name="gradient",
+    )(*turned, *far[4:])
+    return [[near[2 + part], near[part], far[2 + part], far[part]] for part in range(2)]
 
 
 def solution(mesh):
@@ -324,9 +334,11 @@
       def col_half(low, array):
           return jnp.where(low, array[..., :half], array[..., half:])
 
+      halves = [col_half(t_low if j == 0 else ~t_low, weights) for j in range(2)]
+      halves, hidden = lax.optimization_barrier((halves, hidden))
       routed = []
       for j in range(2):
-          routed.append(lax.ppermute(col_half(t_low if j == 0 else ~t_low, weights), "fsdp", plane_route(j)))
+          routed.append(lax.ppermute(halves[j], "fsdp", plane_route(j)))
       stay = jnp.where(same, routed[0], routed[1])
       leave = jnp.where(same, routed[1], routed[0])
       came = swap_sec(leave, 2)
@@ -343,7 +355,7 @@
               if (ff & 1) == (zz >> 1) ^ other
           ]
           swaps[name] = lax.ppermute(
-              hidden, ("sec", "fsdp"), pairs
+              hidden if name == "xsend" else x_own, ("sec", "fsdp"), pairs
           )
           pairs = [
               (zz * n_dev + ff, zz * n_dev + (ff ^ 1))
@@ -445,8 +457,9 @@
       mine = jnp.where(same, advantage[0], advantage[1])
       advantage_out = jnp.concatenate([jnp.zeros((first,), jnp.float32), mine])[None]
       if local:
+          raw = actor_head * silu_slope(pre_keep.astype(jnp.float32))
           blocks = gradient(
-              flags, (turned_keep, turned_send), pre_keep, (sent_own, sent_far), got_actor,
+              flags, (turned_keep, turned_send), raw, (sent_own, sent_far), got_actor,
               actor_head, advantage, side, scale_keep, message, others[1], 2 * feats,
           )
       else:

time: 120 us -> 125 us (1.042)
  starting transfers between devices: 47.4 us -> 52.7 us
    ppermute x8, starting transfers between devices: 15.7 us -> 23.5 us  [swap_sec(): return lax.ppermute(array, 'sec', [(i, i ^ flip) for i in range(4)])]
    ppermute x4, waiting for transfers between devices: 12.6 us -> 4.86 us  [the longest x2 4.86 us: shards(): routed.append(lax.ppermute(halves[j], 'fsdp', plane_route(j)))]
    ppermute x15, waiting for transfers between devices: 15 us -> 18.8 us  [swap_fsdp(): return lax.ppermute(array, 'fsdp', [(i, i ^ flip) for i in range(n_dev)])]
    ppermute x8, waiting for transfers between devices: 21.5 us -> 25.2 us  [swap_sec(): return lax.ppermute(array, 'sec', [(i, i ^ flip) for i in range(4)])]
    ppermute x2, starting transfers between devices: 4.41 us -> 2.62 us  [shards(): swaps[name + 'core'] = lax.ppermute(swaps[name], ('sec', 'fsdp'), pairs)]
    ppermute x15, starting transfers between devices: 16.8 us -> 15.2 us  [swap_fsdp(): return lax.ppermute(array, 'fsdp', [(i, i ^ flip) for i in range(n_dev)])]
  transfers between devices with their start and end apart: 31 -> 31, of which waited for: 17 -> 16; matrix products, arithmetic and copies ran while one was open for 3% -> 3% of each run, Pallas kernels for 6% -> 7%
where the time goes in v5:
time: 125 us
  waiting for transfers between devices  55 us (44%)
  starting transfers between devices  52.7 us (42%)
  Pallas kernels  10.9 us (9%)
  other arithmetic  2.55 us (2%)
  local copies, waits for them, and re-layouts  2.06 us (2%)
    ppermute x8, waiting for transfers between devices, swap_sec(): return lax.ppermute(array, 'sec', [(i, i ^ flip) for i in range(4)])  25.2 us
    ppermute x8, starting transfers between devices, swap_sec(): return lax.ppermute(array, 'sec', [(i, i ^ flip) for i in range(4)])  23.5 us
    ppermute x15, waiting for transfers between devices, swap_fsdp(): return lax.ppermute(array, 'fsdp', [(i, i ^ flip) for i in range(n_dev)])  18.8 us
    ppermute x15, starting transfers between devices, swap_fsdp(): return lax.ppermute(array, 'fsdp', [(i, i ^ flip) for i in range(n_dev)])  15.2 us
    ppermute x2, waiting for transfers between devices, shards(): placed.append(lax.ppermute(piece, ('sec', 'fsdp'), final_route()))  6.15 us
    ppermute x2, starting transfers between devices, shards(): placed.append(lax.ppermute(piece, ('sec', 'fsdp'), final_route()))  5.16 us
    ppermute x2, waiting for transfers between devices, shards(): routed.append(lax.ppermute(halves[j], 'fsdp', plane_route(j)))  4.86 us
    pallas_call x3, Pallas kernels, products(): pl.pallas_call(body, in_specs=[FLAGS] + [WHOLE] * (4 + 4 * slabs + len(he...  4.59 us
  transfers between devices with their start and end apart: 31, of which 16 were waited for; matrix products, arithmetic and copies ran while one was open for 3% of the time, Pallas kernels for 7%

profile of v5, /device:TPU:4, one launch (start us, length us, event | category | flops | bytes accessed | tf_op | source)
XLA Modules:
  0.0 124.7 jit_solution(3296043886283637186)
XLA Ops:
  3.8 3.5 %collective-permute-start.1 = (bf16[448,1024]{1,0:T(8,128)(2,1)S(1)}, bf16[448,1024]{1,0:T(8,128)(2,1)S(1)}, u32[]{:S(2)}, u32[]{:S(2)}) collective-permute-start(bf16[448,1024]{1,0:T(8,128)(2,1)S(1)} %slice.55.refs_0_), channel_id=1, source_target_pairs={{0,8},{2,10},{4,12},{6,14},{8,0},{10,2},{12,4},{14,6},{17,25},{19,... | collective-permute-start | bytes 2752520 | tf_op jit(solution)/shard_map/ppermute | solution.py:357
  7.3 1.9 %collective-permute-start.5 = (bf16[512,256]{1,0:T(8,128)(2,1)S(1)}, bf16[512,256]{1,0:T(8,128)(2,1)S(1)}, u32[]{:S(2)}, u32[]{:S(2)}) collective-permute-start(bf16[512,256]{1,0:T(8,128)(2,1)S(1)} %get-tuple-element.37), channel_id=1, source_target_pairs={{0,0},{1,4},{2,2},{3,6},{4,1},{5,5},{6,3},{7,7},{8,8},{9,12},{10,1... | collective-permute-start | bytes 786440 | tf_op jit(solution)/shard_map/ppermute | solution.py:341
  11.1 3.9 %collective-permute-done.5 = bf16[512,256]{1,0:T(8,128)(2,1)S(1)} collective-permute-done((bf16[512,256]{1,0:T(8,128)(2,1)S(1)}, bf16[512,256]{1,0:T(8,128)(2,1)S(1)}, u32[]{:S(2)}, u32[]{:S(2)}) %collective-permute-start.5) | collective-permute-done | bytes 262176 | tf_op jit(solution)/shard_map/ppermute | solution.py:341
  16.0 16.7 %collective-permute-start.10 = (bf16[512,256]{1,0:T(8,128)(2,1)S(1)}, bf16[512,256]{1,0:T(8,128)(2,1)S(1)}, u32[]{:S(2)}, u32[]{:S(2)}) collective-permute-start(bf16[512,256]{1,0:T(8,128)(2,1)S(1)} %get-tuple-element.63), channel_id=1, source_target_pairs={{0,16},{8,24},{16,0},{24,8},{1,17},{9,25},{17,1},{25,9},{2,18},{10... | collective-permute-start | bytes 786440 | tf_op jit(solution)/shard_map/ppermute | solution.py:282
  35.4 6.8 %collective-permute-done.10.refs_8_.refs_4_ = bf16[512,256]{1,0:T(8,128)(2,1)S(1)} collective-permute-done((bf16[512,256]{1,0:T(8,128)(2,1)S(1)}, bf16[512,256]{1,0:T(8,128)(2,1)S(1)}, u32[]{:S(2)}, u32[]{:S(2)}) %collective-permute-start.10) | collective-permute-done | bytes 262176 | tf_op jit(solution)/shard_map/ppermute | solution.py:282
  42.3 1.5 %collective-permute-start.8 = (bf16[512,256]{1,0:T(8,128)(2,1)S(1)}, bf16[512,256]{1,0:T(8,128)(2,1)S(1)}, u32[]{:S(2)}, u32[]{:S(2)}) collective-permute-start(bf16[512,256]{1,0:T(8,128)(2,1)S(1)} %get-tuple-element.64.refs_4_), channel_id=1, source_target_pairs={{0,2},{1,3},{2,0},{3,1},{4,6},{5,7},{6,4},{7,5},{8,10},{9,11},{10,... | collective-permute-start | bytes 786440 | tf_op jit(solution)/shard_map/ppermute | solution.py:279
  44.3 5.2 %collective-permute-done.8.refs_6_ = bf16[512,256]{1,0:T(8,128)(2,1)S(1)} collective-permute-done((bf16[512,256]{1,0:T(8,128)(2,1)S(1)}, bf16[512,256]{1,0:T(8,128)(2,1)S(1)}, u32[]{:S(2)}, u32[]{:S(2)}) %collective-permute-start.8) | collective-permute-done | bytes 262176 | tf_op jit(solution)/shard_map/ppermute | solution.py:279
  54.5 5.0 %collective-permute-done.13.refs_11_.refs_7_ = bf16[512,256]{1,0:T(8,128)(2,1)S(1)} collective-permute-done((bf16[512,256]{1,0:T(8,128)(2,1)S(1)}, bf16[512,256]{1,0:T(8,128)(2,1)S(1)}, u32[]{:S(2)}, u32[]{:S(2)}) %collective-permute-start.13) | collective-permute-done | bytes 262176 | tf_op jit(solution)/shard_map/ppermute | solution.py:279
  59.6 2.2 %collective-permute-done.12.refs_10_.refs_6_ = bf16[512,256]{1,0:T(8,128)(2,1)S(1)} collective-permute-done((bf16[512,256]{1,0:T(8,128)(2,1)S(1)}, bf16[512,256]{1,0:T(8,128)(2,1)S(1)}, u32[]{:S(2)}, u32[]{:S(2)}) %collective-permute-start.12) | collective-permute-done | bytes 262176 | tf_op jit(solution)/shard_map/ppermute | solution.py:279
  63.8 2.9 %collective-permute-start.16 = (f32[1,1024]{1,0:T(1,128)S(1)}, f32[1,1024]{1,0:T(1,128)S(1)}, u32[]{:S(2)}, u32[]{:S(2)}) collective-permute-start(f32[1,1024]{1,0:T(1,128)S(1)} %get-tuple-element.43.message_ref), channel_id=1, source_target_pairs={{0,16},{8,24},{16,0},{24,8},{1,17},{9,25},{17,1},{25,9},{2,18},{10... | collective-permute-start | bytes 12296 | tf_op jit(solution)/shard_map/ppermute | solution.py:282
  66.9 1.9 %products.3 = (bf16[448,256]{1,0:T(8,128)(2,1)S(1)}, f32[448,256]{1,0:T(8,128)S(1)}, f32[448,256]{1,0:T(8,128)S(1)}, f32[1,448]{1,0:T(1,128)S(1)}) custom-call(s32[5]{0:T(128)S(1)} %stack.38.flag_ref, bf16[448,1024]{1,0:T(8,128)(2,1)S(1)} %slice.55.refs_0_, bf16[448,1024]{1,0:T(8,128)(2,1)S(1)} %collective-permute-done.refs_1_, ...), custom_call_target="tpu_custom_call" | custom-call | tf_op jit(solution)/shard_map/products/pallas_call | solution.py:117
  71.5 16.3 %collective-permute-done.16.message_ref = f32[1,1024]{1,0:T(1,128)S(1)} collective-permute-done((f32[1,1024]{1,0:T(1,128)S(1)}, f32[1,1024]{1,0:T(1,128)S(1)}, u32[]{:S(2)}, u32[]{:S(2)}) %collective-permute-start.16) | collective-permute-done | bytes 4128 | tf_op jit(solution)/shard_map/ppermute | solution.py:282
  91.3 2.5 %collective-permute-start.21 = (f32[3,448]{1,0:T(4,128)S(1)}, f32[3,448]{1,0:T(4,128)S(1)}, u32[]{:S(2)}, u32[]{:S(2)}) collective-permute-start(f32[3,448]{1,0:T(4,128)S(1)} %pad_maximum_fusion), channel_id=1, source_target_pairs={{0,16},{8,24},{16,0},{24,8},{1,17},{9,25},{17,1},{25,9},{2,18},{10... | collective-permute-start | bytes 16136 | tf_op jit(solution)/shard_map/ppermute | solution.py:282
  93.9 1.9 %collective-permute-done.22 = f32[2,448]{1,0:T(2,128)S(1)} collective-permute-done((f32[2,448]{1,0:T(2,128)S(1)}, f32[2,448]{1,0:T(2,128)S(1)}, u32[]{:S(2)}, u32[]{:S(2)}) %collective-permute-start.22) | collective-permute-done | bytes 3616 | tf_op jit(solution)/shard_map/ppermute | solution.py:282
  96.6 1.9 %gradient.2 = (bf16[512,128]{1,0:T(8,128)(2,1)S(1)}, bf16[512,128]{1,0:T(8,128)(2,1)S(1)}, bf16[512,128]{1,0:T(8,128)(2,1)S(1)}, bf16[512,128]{1,0:T(8,128)(2,1)...) custom-call(s32[5]{0:T(128)S(1)} %stack.38.flag_ref, bf16[2048,448]{1,0:T(8,128)(2,1)S(1)} %turned.2.keep_ref, ...), custom_call_target="tpu_custom_call" | custom-call | tf_op jit(solution)/shard_map/gradient/pallas_call | solution.py:249
  99.3 2.3 %collective-permute-start.24 = (bf16[512,128]{1,0:T(8,128)(2,1)S(1)}, bf16[512,128]{1,0:T(8,128)(2,1)S(1)}, u32[]{:S(2)}, u32[]{:S(2)}) collective-permute-start(bf16[512,128]{1,0:T(8,128)(2,1)S(1)} %get-tuple-element.54), channel_id=1, source_target_pairs={{0,2},{1,3},{2,0},{3,1},{4,6},{5,7},{6,4},{7,5},{8,10},{9,11},{10,... | collective-permute-start | bytes 393224 | tf_op jit(solution)/shard_map/ppermute | solution.py:279
  103.5 1.5 %collective-permute-start.28 = (bf16[512,128]{1,0:T(8,128)(2,1)S(1)}, bf16[512,128]{1,0:T(8,128)(2,1)S(1)}, u32[]{:S(2)}, u32[]{:S(2)}) collective-permute-start(bf16[512,128]{1,0:T(8,128)(2,1)S(1)} %get-tuple-element.58), channel_id=1, source_target_pairs={{0,2},{1,3},{2,0},{3,1},{4,6},{5,7},{6,4},{7,5},{8,10},{9,11},{10,... | collective-permute-start | bytes 393224 | tf_op jit(solution)/shard_map/ppermute | solution.py:279
  106.0 1.8 %collective-permute-start.29 = (bf16[512,128]{1,0:T(8,128)(2,1)S(1)}, bf16[512,128]{1,0:T(8,128)(2,1)S(1)}, u32[]{:S(2)}, u32[]{:S(2)}) collective-permute-start(bf16[512,128]{1,0:T(8,128)(2,1)S(1)} %get-tuple-element.59), channel_id=1, source_target_pairs={{0,6},{1,7},{2,4},{3,5},{4,2},{5,3},{6,0},{7,1},{8,14},{9,15},{10,... | collective-permute-start | bytes 393224 | tf_op jit(solution)/shard_map/ppermute | solution.py:279
  107.8 2.4 %collective-permute-done.25 = bf16[512,128]{1,0:T(8,128)(2,1)S(1)} collective-permute-done((bf16[512,128]{1,0:T(8,128)(2,1)S(1)}, bf16[512,128]{1,0:T(8,128)(2,1)S(1)}, u32[]{:S(2)}, u32[]{:S(2)}) %collective-permute-start.25) | collective-permute-done | bytes 131104 | tf_op jit(solution)/shard_map/ppermute | solution.py:279
  110.3 1.9 %collective-permute-start.26 = (bf16[512,128]{1,0:T(8,128)(2,1)S(1)}, bf16[512,128]{1,0:T(8,128)(2,1)S(1)}, u32[]{:S(2)}, u32[]{:S(2)}) collective-permute-start(bf16[512,128]{1,0:T(8,128)(2,1)S(1)} %add_convert_fusion.1), channel_id=1, source_target_pairs={{0,0},{1,16},{2,2},{3,18},{4,1},{5,17},{6,3},{7,19},{8,8},{9,24},{... | collective-permute-start | bytes 393224 | tf_op jit(solution)/shard_map/ppermute | solution.py:484
  112.3 1.5 %collective-permute-done.29 = bf16[512,128]{1,0:T(8,128)(2,1)S(1)} collective-permute-done((bf16[512,128]{1,0:T(8,128)(2,1)S(1)}, bf16[512,128]{1,0:T(8,128)(2,1)S(1)}, u32[]{:S(2)}, u32[]{:S(2)}) %collective-permute-start.29) | collective-permute-done | bytes 131104 | tf_op jit(solution)/shard_map/ppermute | solution.py:279
  113.8 3.2 %collective-permute-start.30 = (bf16[512,128]{1,0:T(8,128)(2,1)S(1)}, bf16[512,128]{1,0:T(8,128)(2,1)S(1)}, u32[]{:S(2)}, u32[]{:S(2)}) collective-permute-start(bf16[512,128]{1,0:T(8,128)(2,1)S(1)} %add_convert_fusion), channel_id=1, source_target_pairs={{0,0},{1,16},{2,2},{3,18},{4,1},{5,17},{6,3},{7,19},{8,8},{9,24},{... | collective-permute-start | bytes 393224 | tf_op jit(solution)/shard_map/ppermute | solution.py:484
  117.7 2.7 %collective-permute-done.26 = bf16[512,128]{1,0:T(8,128)(2,1)S(1)} collective-permute-done((bf16[512,128]{1,0:T(8,128)(2,1)S(1)}, bf16[512,128]{1,0:T(8,128)(2,1)S(1)}, u32[]{:S(2)}, u32[]{:S(2)}) %collective-permute-start.26) | collective-permute-done | bytes 131104 | tf_op jit(solution)/shard_map/ppermute | solution.py:484
  120.4 3.5 %collective-permute-done.30 = bf16[512,128]{1,0:T(8,128)(2,1)S(1)} collective-permute-done((bf16[512,128]{1,0:T(8,128)(2,1)S(1)}, bf16[512,128]{1,0:T(8,128)(2,1)S(1)}, u32[]{:S(2)}, u32[]{:S(2)}) %collective-permute-start.30) | collective-permute-done | bytes 131104 | tf_op jit(solution)/shard_map/ppermute | solution.py:484
  (74 shorter events, 28.7 us)
Async XLA Ops:
  1.8 7.9 %collective-permute-start.3 = (bf16[512,1024]{1,0:T(8,128)(2,1)}, bf16[512,1024]{1,0:T(8,128)(2,1)S(1)}, u32[]{:S(2)}, u32[]{:S(2)}) collective-permute-start(bf16[512,1024]{1,0:T(8,128)(2,1)} %param.5), channel_id=1, source_target_pairs={{1,9},{3,11},{5,13},{7,15},{9,1},{11,3},{13,5},{15,7},{16,24},{18,... | collective-permute-start | bytes 3145736 | tf_op jit(solution)/shard_map/ppermute | solution.py:357
  3.8 30.3 %collective-permute-start.1 = (bf16[448,1024]{1,0:T(8,128)(2,1)S(1)}, bf16[448,1024]{1,0:T(8,128)(2,1)S(1)}, u32[]{:S(2)}, u32[]{:S(2)}) collective-permute-start(bf16[448,1024]{1,0:T(8,128)(2,1)S(1)} %slice.55.refs_0_), channel_id=1, source_target_pairs={{0,8},{2,10},{4,12},{6,14},{8,0},{10,2},{12,4},{14,6},{17,25},{19,... | collective-permute-start | bytes 2752520 | tf_op jit(solution)/shard_map/ppermute | solution.py:357
  7.3 7.7 %collective-permute-start.5 = (bf16[512,256]{1,0:T(8,128)(2,1)S(1)}, bf16[512,256]{1,0:T(8,128)(2,1)S(1)}, u32[]{:S(2)}, u32[]{:S(2)}) collective-permute-start(bf16[512,256]{1,0:T(8,128)(2,1)S(1)} %get-tuple-element.37), channel_id=1, source_target_pairs={{0,0},{1,4},{2,2},{3,6},{4,1},{5,5},{6,3},{7,7},{8,8},{9,12},{10,1... | collective-permute-start | bytes 786440 | tf_op jit(solution)/shard_map/ppermute | solution.py:341
  9.3 42.4 %collective-permute-start = (bf16[448,1024]{1,0:T(8,128)(2,1)S(1)}, bf16[448,1024]{1,0:T(8,128)(2,1)S(1)}, u32[]{:S(2)}, u32[]{:S(2)}) collective-permute-start(bf16[448,1024]{1,0:T(8,128)(2,1)S(1)} %slice.55.refs_0_), channel_id=1, source_target_pairs={{0,1},{1,0},{2,3},{3,2},{4,5},{5,4},{6,7},{7,6},{8,9},{9,8},{10,11... | collective-permute-start | bytes 2752520 | tf_op jit(solution)/shard_map/ppermute | solution.py:279
  9.8 43.2 %collective-permute-start.4 = (bf16[512,1024]{1,0:T(8,128)(2,1)S(1)}, bf16[512,1024]{1,0:T(8,128)(2,1)S(1)}, u32[]{:S(2)}, u32[]{:S(2)}) collective-permute-start(bf16[512,1024]{1,0:T(8,128)(2,1)S(1)} %collective-permute-done.3.refs_2_), channel_id=1, source_target_pairs={{1,0},{3,2},{5,4},{7,6},{9,8},{11,10},{13,12},{15,14},{16,17},{18,... | collective-permute-start | bytes 3145736 | tf_op jit(solution)/shard_map/ppermute | solution.py:366
  16.0 26.3 %collective-permute-start.10 = (bf16[512,256]{1,0:T(8,128)(2,1)S(1)}, bf16[512,256]{1,0:T(8,128)(2,1)S(1)}, u32[]{:S(2)}, u32[]{:S(2)}) collective-permute-start(bf16[512,256]{1,0:T(8,128)(2,1)S(1)} %get-tuple-element.63), channel_id=1, source_target_pairs={{0,16},{8,24},{16,0},{24,8},{1,17},{9,25},{17,1},{25,9},{2,18},{10... | collective-permute-start | bytes 786440 | tf_op jit(solution)/shard_map/ppermute | solution.py:282
  32.6 11.1 %collective-permute-start.9 = (bf16[512,256]{1,0:T(8,128)(2,1)S(1)}, bf16[512,256]{1,0:T(8,128)(2,1)S(1)}, u32[]{:S(2)}, u32[]{:S(2)}) collective-permute-start(bf16[512,256]{1,0:T(8,128)(2,1)S(1)} %get-tuple-element.64.refs_4_), channel_id=1, source_target_pairs={{0,6},{1,7},{2,4},{3,5},{4,2},{5,3},{6,0},{7,1},{8,14},{9,15},{10,... | collective-permute-start | bytes 786440 | tf_op jit(solution)/shard_map/ppermute | solution.py:279
  34.1 32.8 %collective-permute-start.2 = (bf16[448,1024]{1,0:T(8,128)(2,1)S(1)}, bf16[448,1024]{1,0:T(8,128)(2,1)S(1)}, u32[]{:S(2)}, u32[]{:S(2)}) collective-permute-start(bf16[448,1024]{1,0:T(8,128)(2,1)S(1)} %collective-permute-done.1.refs_2_), channel_id=1, source_target_pairs={{0,1},{2,3},{4,5},{6,7},{8,9},{10,11},{12,13},{14,15},{17,16},{19,... | collective-permute-start | bytes 2752520 | tf_op jit(solution)/shard_map/ppermute | solution.py:366
  42.3 7.2 %collective-permute-start.8 = (bf16[512,256]{1,0:T(8,128)(2,1)S(1)}, bf16[512,256]{1,0:T(8,128)(2,1)S(1)}, u32[]{:S(2)}, u32[]{:S(2)}) collective-permute-start(bf16[512,256]{1,0:T(8,128)(2,1)S(1)} %get-tuple-element.64.refs_4_), channel_id=1, source_target_pairs={{0,2},{1,3},{2,0},{3,1},{4,6},{5,7},{6,4},{7,5},{8,10},{9,11},{10,... | collective-permute-start | bytes 786440 | tf_op jit(solution)/shard_map/ppermute | solution.py:279
  49.5 10.1 %collective-permute-start.13 = (bf16[512,256]{1,0:T(8,128)(2,1)S(1)}, bf16[512,256]{1,0:T(8,128)(2,1)S(1)}, u32[]{:S(2)}, u32[]{:S(2)}) collective-permute-start(bf16[512,256]{1,0:T(8,128)(2,1)S(1)} %collective-permute-done.10.refs_8_.refs_4_), channel_id=1, source_target_pairs={{0,6},{1,7},{2,4},{3,5},{4,2},{5,3},{6,0},{7,1},{8,14},{9,15},{10,... | collective-permute-start | bytes 786440 | tf_op jit(solution)/shard_map/ppermute | solution.py:279
  50.9 10.9 %collective-permute-start.12 = (bf16[512,256]{1,0:T(8,128)(2,1)S(1)}, bf16[512,256]{1,0:T(8,128)(2,1)S(1)}, u32[]{:S(2)}, u32[]{:S(2)}) collective-permute-start(bf16[512,256]{1,0:T(8,128)(2,1)S(1)} %collective-permute-done.10.refs_8_.refs_4_), channel_id=1, source_target_pairs={{0,2},{1,3},{2,0},{3,1},{4,6},{5,7},{6,4},{7,5},{8,10},{9,11},{10,... | collective-permute-start | bytes 786440 | tf_op jit(solution)/shard_map/ppermute | solution.py:279
  51.7 10.7 %collective-permute-start.11 = (bf16[512,256]{1,0:T(8,128)(2,1)S(1)}, bf16[512,256]{1,0:T(8,128)(2,1)S(1)}, u32[]{:S(2)}, u32[]{:S(2)}) collective-permute-start(bf16[512,256]{1,0:T(8,128)(2,1)S(1)} %collective-permute-done.10.refs_8_.refs_4_), channel_id=1, source_target_pairs={{0,4},{1,5},{2,6},{3,7},{4,0},{5,1},{6,2},{7,3},{8,12},{9,13},{10,... | collective-permute-start | bytes 786440 | tf_op jit(solution)/shard_map/ppermute | solution.py:279
  53.0 10.8 %collective-permute-start.18 = (f32[1,514]{1,0:T(1,128)S(1)}, f32[1,514]{1,0:T(1,128)S(1)}, u32[]{:S(2)}, u32[]{:S(2)}) collective-permute-start(f32[1,514]{1,0:T(1,128)S(1)} %pad_maximum_fusion.3), channel_id=1, source_target_pairs={{0,1},{1,0},{2,3},{3,2},{4,5},{5,4},{6,7},{7,6},{8,9},{9,8},{10,11... | collective-permute-start | bytes 6176 | tf_op jit(solution)/shard_map/ppermute | solution.py:279
  59.6 28.3 %collective-permute-start.15 = (bf16[448,256]{1,0:T(8,128)(2,1)S(1)}, bf16[448,256]{1,0:T(8,128)(2,1)S(1)}, u32[]{:S(2)}, u32[]{:S(2)}) collective-permute-start(bf16[448,256]{1,0:T(8,128)(2,1)S(1)} %get-tuple-element.41.own_ref), channel_id=1, source_target_pairs={{0,16},{8,24},{16,0},{24,8},{1,17},{9,25},{17,1},{25,9},{2,18},{10... | collective-permute-start | bytes 688136 | tf_op jit(solution)/shard_map/ppermute | solution.py:282
  63.6 24.3 %collective-permute-start.14 = (bf16[448,256]{1,0:T(8,128)(2,1)S(1)}, bf16[448,256]{1,0:T(8,128)(2,1)S(1)}, u32[]{:S(2)}, u32[]{:S(2)}) collective-permute-start(bf16[448,256]{1,0:T(8,128)(2,1)S(1)} %products.4.far_ref), channel_id=1, source_target_pairs={{0,16},{8,24},{16,0},{24,8},{1,17},{9,25},{17,1},{25,9},{2,18},{10... | collective-permute-start | bytes 688136 | tf_op jit(solution)/shard_map/ppermute | solution.py:282
  63.8 24.0 %collective-permute-start.16 = (f32[1,1024]{1,0:T(1,128)S(1)}, f32[1,1024]{1,0:T(1,128)S(1)}, u32[]{:S(2)}, u32[]{:S(2)}) collective-permute-start(f32[1,1024]{1,0:T(1,128)S(1)} %get-tuple-element.43.message_ref), channel_id=1, source_target_pairs={{0,16},{8,24},{16,0},{24,8},{1,17},{9,25},{17,1},{25,9},{2,18},{10... | collective-permute-start | bytes 12296 | tf_op jit(solution)/shard_map/ppermute | solution.py:282
  68.8 27.7 %collective-permute-start.17 = (bf16[448,256]{1,0:T(8,128)(2,1)S(1)}, bf16[448,256]{1,0:T(8,128)(2,1)S(1)}, u32[]{:S(2)}, u32[]{:S(2)}) collective-permute-start(bf16[448,256]{1,0:T(8,128)(2,1)S(1)} %get-tuple-element.46), channel_id=1, source_target_pairs={{0,16},{8,24},{16,0},{24,8},{1,17},{9,25},{17,1},{25,9},{2,18},{10... | collective-permute-start | bytes 688136 | tf_op jit(solution)/shard_map/ppermute | solution.py:282
  99.3 8.5 %collective-permute-start.24 = (bf16[512,128]{1,0:T(8,128)(2,1)S(1)}, bf16[512,128]{1,0:T(8,128)(2,1)S(1)}, u32[]{:S(2)}, u32[]{:S(2)}) collective-permute-start(bf16[512,128]{1,0:T(8,128)(2,1)S(1)} %get-tuple-element.54), channel_id=1, source_target_pairs={{0,2},{1,3},{2,0},{3,1},{4,6},{5,7},{6,4},{7,5},{8,10},{9,11},{10,... | collective-permute-start | bytes 393224 | tf_op jit(solution)/shard_map/ppermute | solution.py:279
  101.6 8.6 %collective-permute-start.25 = (bf16[512,128]{1,0:T(8,128)(2,1)S(1)}, bf16[512,128]{1,0:T(8,128)(2,1)S(1)}, u32[]{:S(2)}, u32[]{:S(2)}) collective-permute-start(bf16[512,128]{1,0:T(8,128)(2,1)S(1)} %get-tuple-element.55), channel_id=1, source_target_pairs={{0,6},{1,7},{2,4},{3,5},{4,2},{5,3},{6,0},{7,1},{8,14},{9,15},{10,... | collective-permute-start | bytes 393224 | tf_op jit(solution)/shard_map/ppermute | solution.py:279
  103.0 9.3 %collective-permute-start.27 = (bf16[512,128]{1,0:T(8,128)(2,1)S(1)}, bf16[512,128]{1,0:T(8,128)(2,1)S(1)}, u32[]{:S(2)}, u32[]{:S(2)}) collective-permute-start(bf16[512,128]{1,0:T(8,128)(2,1)S(1)} %get-tuple-element.57), channel_id=1, source_target_pairs={{0,4},{1,5},{2,6},{3,7},{4,0},{5,1},{6,2},{7,3},{8,12},{9,13},{10,... | collective-permute-start | bytes 393224 | tf_op jit(solution)/shard_map/ppermute | solution.py:279
  103.5 8.7 %collective-permute-start.28 = (bf16[512,128]{1,0:T(8,128)(2,1)S(1)}, bf16[512,128]{1,0:T(8,128)(2,1)S(1)}, u32[]{:S(2)}, u32[]{:S(2)}) collective-permute-start(bf16[512,128]{1,0:T(8,128)(2,1)S(1)} %get-tuple-element.58), channel_id=1, source_target_pairs={{0,2},{1,3},{2,0},{3,1},{4,6},{5,7},{6,4},{7,5},{8,10},{9,11},{10,... | collective-permute-start | bytes 393224 | tf_op jit(solution)/shard_map/ppermute | solution.py:279
  106.0 7.7 %collective-permute-start.29 = (bf16[512,128]{1,0:T(8,128)(2,1)S(1)}, bf16[512,128]{1,0:T(8,128)(2,1)S(1)}, u32[]{:S(2)}, u32[]{:S(2)}) collective-permute-start(bf16[512,128]{1,0:T(8,128)(2,1)S(1)} %get-tuple-element.59), channel_id=1, source_target_pairs={{0,6},{1,7},{2,4},{3,5},{4,2},{5,3},{6,0},{7,1},{8,14},{9,15},{10,... | collective-permute-start | bytes 393224 | tf_op jit(solution)/shard_map/ppermute | solution.py:279
  110.3 10.1 %collective-permute-start.26 = (bf16[512,128]{1,0:T(8,128)(2,1)S(1)}, bf16[512,128]{1,0:T(8,128)(2,1)S(1)}, u32[]{:S(2)}, u32[]{:S(2)}) collective-permute-start(bf16[512,128]{1,0:T(8,128)(2,1)S(1)} %add_convert_fusion.1), channel_id=1, source_target_pairs={{0,0},{1,16},{2,2},{3,18},{4,1},{5,17},{6,3},{7,19},{8,8},{9,24},{... | collective-permute-start | bytes 393224 | tf_op jit(solution)/shard_map/ppermute | solution.py:484
  113.8 10.1 %collective-permute-start.30 = (bf16[512,128]{1,0:T(8,128)(2,1)S(1)}, bf16[512,128]{1,0:T(8,128)(2,1)S(1)}, u32[]{:S(2)}, u32[]{:S(2)}) collective-permute-start(bf16[512,128]{1,0:T(8,128)(2,1)S(1)} %add_convert_fusion), channel_id=1, source_target_pairs={{0,0},{1,16},{2,2},{3,18},{4,1},{5,17},{6,3},{7,19},{8,8},{9,24},{... | collective-permute-start | bytes 393224 | tf_op jit(solution)/shard_map/ppermute | solution.py:484
  (10 other events, 192.6 us)
